TPU v7x, 32 devices: a whole 2x2x4 slice. The times are simulated.
32 devices in a mesh: group: 2 (over x), seq: 16 (over z, y, core).
Axes of the slice: x: 2, y: 2, z: 4, core: 2. Of those that a mesh axis runs over, the one named last changes fastest.
Arguments:
- tokens: bfloat16 [16384, 2048], P(('group', 'seq')), parts along dimension 0, may hold values from -6 to 6
- w_qkv: bfloat16 [2048, 3072], P('seq'), may hold values from -0.125 to 0.125
- w_out: bfloat16 [1024, 2048], P('seq'), may hold values from -0.1875 to 0.1875
- level_weight: float32 [14, 4, 16384], P(None, None, ('group', 'seq')), parts along dimension 2, may hold values from 0.1 to 1
Outputs:
- mixed: bfloat16 [16384, 2048], P(('group', 'seq')), parts along dimension 0
There are 2 independent parts, one for each index of `group`. A program takes and returns all parts, laid end to end along the dimension named above; an argument that names none is the same for every part. Nothing has to cross between parts.
All inputs are finite; a program needn't handle non-finite values.
Results may differ from a plain program's by a relative error of at most 0.0085.
Values may be sent and summed in bfloat16 or wider, within the bound.
No kernel may reach another device: no remote copies, remote signals or barrier semaphores. Data moves between devices by JAX's collectives and lax.ppermute only.
A program may use at most 128 MiB of HBM per device.

v0:
```python
import math

import jax
import jax.numpy as jnp
from jax import lax
from jax.sharding import PartitionSpec as P

HEADS = 4
HEAD = 256
SPAN = 256
CBITS = 8


def partner_2(value, axis, bit):
    mask = 2**bit
    pairs = [(source, source ^ mask) for source in range(lax.axis_size(axis))]
    return lax.ppermute(value, axis, pairs)


def bit_length_of(values):
    result = jnp.zeros(values.shape, jnp.int32)
    for bit_pos in range(24):
        result = result + (values >= 1 << bit_pos).astype(jnp.int32)
    return result


def intra_table(span, cbits, head):
    position = jnp.arange(span, dtype=jnp.int32)
    pair_level = bit_length_of(position[:, None] ^ position[None, :])
    causal = position[:, None] >= position[None, :]
    levels_all = jnp.arange(cbits + 1, dtype=jnp.int32)
    gains = jnp.asarray(
        [1.0 / math.sqrt(head * max(1, 2 ** (level_no - 1))) for level_no in range(cbits + 1)],
        jnp.float32,
    )
    onehot = ((pair_level[None] == levels_all[:, None, None]) & causal[None]).astype(jnp.float32)
    return onehot * gains[:, None, None]


def split_read(form, query_half, state):
    upper_part = state.astype(jnp.bfloat16)
    lower_part = (state - upper_part.astype(jnp.float32)).astype(jnp.bfloat16)
    first = jnp.einsum(form, query_half, upper_part, preferred_element_type=jnp.float32)
    second = jnp.einsum(form, query_half, lower_part, preferred_element_type=jnp.float32)
    return first + second


def on_device(tokens, w_qkv, w_out, level_weight):
    highest = lax.Precision.HIGHEST
    head_cols = HEADS * HEAD
    tok_rows = tokens.shape[0]
    count = tok_rows // SPAN
    columns = tokens
    qkv = jnp.dot(
        columns,
        lax.all_gather(w_qkv, "seq", axis=0, tiled=True),
        preferred_element_type=jnp.float32,
    ).astype(jnp.bfloat16)
    queries = qkv[:, :head_cols].reshape(count, SPAN, HEADS, HEAD)
    key_rows = qkv[:, head_cols : 2 * head_cols].reshape(count, SPAN, HEADS, HEAD)
    value_rows = qkv[:, 2 * head_cols :].reshape(count, SPAN, HEADS, HEAD)
    weights = level_weight.reshape(level_weight.shape[0], HEADS, count, SPAN)
    table = intra_table(SPAN, CBITS, HEAD)
    mixing = jnp.einsum("lij,lhci->chij", table, weights[: CBITS + 1], precision=highest)
    scores = jnp.einsum("cihe,cjhe->chij", queries, key_rows, preferred_element_type=jnp.float32)
    probs = (scores * mixing).astype(jnp.bfloat16)
    intra = jnp.einsum("chij,cjhe->cihe", probs, value_rows, preferred_element_type=jnp.float32)
    states = jnp.einsum("cjhe,cjhf->chef", key_rows, value_rows, preferred_element_type=jnp.float32)
    inter = jnp.zeros((count, SPAN, HEADS, HEAD), jnp.float32)
    local_bits = count.bit_length() - 1
    level_no = 1
    half_size = 2 ** (level_no - 1)
    blocks = count // (2 * half_size)
    left = states.reshape(blocks, 2, half_size, HEADS, HEAD, HEAD)[:, 0].sum(axis=1)
    right_q = queries.reshape(blocks, 2, half_size, SPAN, HEADS, HEAD)[:, 1]
    read = split_read("bmihe,bhef->bmihf", right_q, left)
    scale = weights[CBITS + level_no].reshape(HEADS, blocks, 2, half_size, SPAN)[:, :, 1]
    scale = jnp.transpose(scale, (1, 2, 3, 0)) * (1.0 / math.sqrt(SPAN * half_size * HEAD))
    shaped = inter.reshape(blocks, 2, half_size, SPAN, HEADS, HEAD)
    inter = shaped.at[:, 1].add(read * scale[..., None]).reshape(count, SPAN, HEADS, HEAD)
    block_total = states.sum(axis=0)
    seq_bits = lax.axis_size("seq").bit_length() - 1
    device = lax.axis_index("seq")
    for bit_pos in range(seq_bits):
        upper = (device >> bit_pos & 1).astype(jnp.float32)
        partner = partner_2(block_total, "seq", bit_pos)
        level_no = local_bits + bit_pos + 1
        gain = 1.0 / math.sqrt(SPAN * 2 ** (level_no - 1) * HEAD)
        level_scale = jnp.transpose(weights[CBITS + level_no], (1, 2, 0)) * (upper * gain)
        single = split_read("cihe,hef->cihf", queries, partner)
        inter = inter + single * level_scale[..., None]
        if bit_pos + 1 < seq_bits:
            block_total = block_total + partner
    attended = (intra + inter).reshape(tok_rows, head_cols).astype(jnp.bfloat16)
    columns = attended
    mixed = jnp.dot(
        columns,
        lax.all_gather(w_out, "seq", axis=0, tiled=True),
        preferred_element_type=jnp.float32,
    )
    return mixed.astype(jnp.bfloat16)


def solution(mesh):
    return jax.shard_map(
        on_device,
        mesh=mesh,
        in_specs=(
            P(("group", "seq"), None),
            P("seq", None),
            P("seq", None),
            P(None, None, ("group", "seq")),
        ),
        out_specs=P(("group", "seq"), None),
        check_vma=False,
    )
```

profile of v0, /device:TPU:0, one launch (start us, length us, event | category | flops | bytes accessed | tf_op | source)
XLA Modules:
  0.0 262.6 jit_solution(4871203415658004380)
XLA Ops:
  6.5 0.0 copy-start
  6.5 0.0 all-gather.3.cloned.1.call-start
  6.5 0.7 all-gather.3.cloned.1.call-update
  7.3 0.0 all-gather.5.cloned.1.call-start
  7.3 0.7 all-gather.5.cloned.1.call-update
  8.0 104.8 %all-gather.3.cloned.1.call-done = bf16[2048,3072]{1,0:T(8,128)(2,1)} async-done(((bf16[128,3072]{1,0:T(8,128)(2,1)}), bf16[2048,3072]{1,0:T(8,128)(2,1)}) %all-gather.3.cloned.1.call-update) | async-done | bytes 12582928 | tf_op jit(solution)/shard_map/all_gather | solution.py:56
  112.8 0.0 copy-done
  112.8 9.6 %convolution_convert_fusion = bf16[512,3072]{1,0:T(8,128)(2,1)S(1)} fusion(bf16[512,2048]{1,0:T(8,128)(2,1)S(1)} %copy-done, bf16[2048,3072]{1,0:T(8,128)(2,1)} %all-gather.3.cloned.1.call-done), kind=kOutput, calls=%fused_computation | convolution fusion | flops 6444023808 | bytes 17825792 | tf_op jit(solution)/shard_map/dot_general | solution.py:54
  122.4 1.3 fusion.89
  123.7 0.8 reshape.219
  124.5 0.7 copy.99
  125.2 0.8 reshape.217
  126.0 1.8 fusion.90
  127.8 1.4 copy.101
  129.2 0.3 collective-permute-start
  129.5 0.8 convert_add_fusion
  130.3 0.0 copy-done.9
  130.3 0.0 copy-start.10
  130.3 1.8 collective-permute-done
  132.1 2.8 %add.256 = f32[4,256,256]{1,2,0:T(8,128)} add(f32[4,256,256]{1,2,0:T(8,128)} %copy.101, f32[4,256,256]{1,2,0:T(8,128)S(1)} %collective-permute-done) | non-fusion elementwise | flops 262144 | bytes 3145728 | tf_op jit(solution)/shard_map/add | solution.py:93
  134.9 0.6 collective-permute-start.1
  135.5 0.0 slice-done
  135.5 0.1 slice.83
  135.6 1.3 copy.96
  136.9 0.0 copy-done.2
  136.9 0.0 copy-done.10
  136.9 8.4 %fusion = f32[256,256,4,2]{1,2,3,0:T(4,128)} fusion(f32[9,4,2,256]{0,1,2,3:T(4,128)} %copy.96, f32[9]{0:T(128)S(1)} %copy-done.10, s32[256,256]{1,0:T(8,128)} %convert_add_fusion, pred[256,256]{1,0:T(8,128)(4,1)S(1)} %iota_compare_fusion.1), kind=kOutput, calls=%fused_computation.1 | convolution fusion | flops 58392576 | bytes 2498596 | tf_op jit(solution)/shard_map/lij,lhci->chij/dot_general | solution.py:64
  145.3 1.9 reshape.218
  147.2 2.6 %reshape_reshape.3 = bf16[1,2,1,256,4,256]{5,4,3,1,2,0:T(4,128)(2,1)} reshape(bf16[512,1024]{1,0:T(8,128)(2,1)} %get-tuple-element.17) | data formatting | bytes 2097152 | tf_op jit(solution)/shard_map/reshape;reshape | solution.py:75
  149.8 1.2 slice.96
  151.0 0.0 copy-start.6
  151.0 0.8 copy-done.6
  151.9 2.5 fusion.42
  154.4 4.2 %fusion.15 = f32[2,4,256,256]{3,2,1,0:T(8,128)} fusion(f32[256,256,4,2]{1,2,3,0:T(4,128)} %fusion, bf16[2,256,4,256]{1,3,2,0:T(8,128)(2,1)S(1)} %copy.99, bf16[2,256,4,256]{3,2,1,0:T(4,128)(2,1)S(1)} %reshape.217, bf16[2,256,4,256]{3,2,1,0:T(4,128)(2,1)S(1)} %reshape.218), kind=kOutput, calls=%fused_computation.22 | convolution fusion | flops 537919488 | bytes 7340032 | tf_op jit(solution)/shard_map/chij,cjhe->cihe/dot_general | solution.py:67
  158.6 13.2 %collective-permute-done.1 = f32[4,256,256]{1,2,0:T(8,128)} collective-permute-done((f32[4,256,256]{1,2,0:T(8,128)}, f32[4,256,256]{1,2,0:T(8,128)}, u32[]{:S(2)}, u32[]{:S(2)}) %collective-permute-start.1) | collective-permute-done | bytes 1048608 | tf_op jit(solution)/shard_map/ppermute | solution.py:17
  171.8 1.7 add.260
  173.5 0.5 collective-permute-start.2
  174.0 0.0 copy-done.3
  174.0 0.5 fusion.25
  174.4 0.0 copy-start.5
  174.4 0.0 copy-start.7
  174.5 0.0 copy-start.8
  174.5 0.5 bitcast_multiply_fusion.3
  175.0 1.1 copy-done.5
  176.0 0.1 copy-done.7
  176.1 0.3 copy-done.8
  176.4 0.5 fusion.19
  177.0 21.0 %collective-permute-done.2 = f32[4,256,256]{1,2,0:T(8,128)S(1)} collective-permute-done((f32[4,256,256]{1,2,0:T(8,128)S(1)}, f32[4,256,256]{1,2,0:T(8,128)S(1)}, u32[]{:S(2)}, u32[]{:S(2)}) %collective-permute-start.2) | collective-permute-done | bytes 1048608 | tf_op jit(solution)/shard_map/ppermute | solution.py:17
  198.0 0.1 add.264
  198.2 1.5 collective-permute-start.3
  199.7 1.7 fusion.39
  201.4 2.1 fusion.28
  203.5 0.5 fusion.37
  203.9 0.5 fusion.31
  204.4 0.0 copy-start.4
  204.4 40.6 %collective-permute-done.3 = f32[4,256,256]{1,2,0:T(8,128)S(1)} collective-permute-done((f32[4,256,256]{1,2,0:T(8,128)S(1)}, f32[4,256,256]{1,2,0:T(8,128)S(1)}, u32[]{:S(2)}, u32[]{:S(2)}) %collective-permute-start.3) | collective-permute-done | bytes 1048608 | tf_op jit(solution)/shard_map/ppermute | solution.py:17
  245.1 0.5 fusion.34
  245.6 0.0 copy-done.4
  245.6 2.3 fusion.7
  247.8 1.7 copy.127
  249.5 0.2 copy.156
  249.7 0.0 all-gather.5.cloned.1.call-done
  249.8 0.0 copy-start.1
  249.8 6.0 %convolution_convert_fusion.1 = bf16[512,2048]{1,0:T(8,128)(2,1)} fusion(bf16[512,1024]{1,0:T(8,128)(2,1)S(1)} %bitcast.123, bf16[1024,2048]{1,0:T(8,128)(2,1)} %all-gather.5.cloned.1.call-done), kind=kOutput, calls=%fused_computation.6 | convolution fusion | flops 2148532224 | bytes 7340032 | tf_op jit(solution)/shard_map/dot_general | solution.py:96
  (8 shorter events, 0.0 us)
Async XLA Ops:
  6.5 106.3 %copy-start = (bf16[512,2048]{1,0:T(8,128)(2,1)S(1)}, bf16[512,2048]{1,0:T(8,128)(2,1)}, u32[]{:S(2)}) copy-start(bf16[512,2048]{1,0:T(8,128)(2,1)} %param.7) | copy-start | bytes 6291460
  6.5 106.3 %all-gather.3.cloned.1.call-start = ((), (), s32[]{:S(2)}) async-start(), calls=%async_computation | async-start | bytes 13369344 | tf_op jit(solution)/shard_map/all_gather | solution.py:56
  7.3 242.5 %all-gather.5.cloned.1.call-start = ((), (), s32[]{:S(2)}) async-start(), calls=%async_computation.1 | async-start | bytes 4456448 | tf_op jit(solution)/shard_map/all_gather | solution.py:98
  127.8 2.5 copy-start.9
  129.2 6.3 %slice-start = ((f32[14,4,512]{2,1,0:T(4,128)}), f32[9,4,512]{2,1,0:T(4,128)S(1)}, s32[]{:S(2)}) async-start(f32[14,4,512]{2,1,0:T(4,128)} %param.10), calls=%async_computation.2 | async-start | bytes 147456 | tf_op jit(solution)/shard_map/slice | solution.py:64
  129.2 2.9 %collective-permute-start = (f32[4,256,256]{1,2,0:T(8,128)}, f32[4,256,256]{1,2,0:T(8,128)S(1)}, u32[]{:S(2)}, u32[]{:S(2)}) collective-permute-start(f32[4,256,256]{1,2,0:T(8,128)} %copy.101), channel_id=1, source_target_pairs={{0,1},{1,0},{2,3},{3,2},{4,5},{5,4},{6,7},{7,6},{8,9},{9,8},{10,11... | collective-permute-start | bytes 3145736 | tf_op jit(solution)/shard_map/ppermute | solution.py:17
  130.3 6.6 %copy-start.10 = (f32[9]{0:T(128)S(1)}, f32[9]{0:T(128)}, u32[]{:S(2)}) copy-start(f32[9]{0:T(128)} %constant.101.clone) | copy-start | bytes 112
  132.1 4.8 %copy-start.2 = (f32[4,256,256]{1,2,0:T(8,128)}, f32[4,256,256]{1,2,0:T(8,128)S(1)}, u32[]{:S(2)}) copy-start(f32[4,256,256]{1,2,0:T(8,128)S(1)} %collective-permute-done) | copy-start | bytes 3145732
  134.9 36.9 %collective-permute-start.1 = (f32[4,256,256]{1,2,0:T(8,128)}, f32[4,256,256]{1,2,0:T(8,128)}, u32[]{:S(2)}, u32[]{:S(2)}) collective-permute-start(f32[4,256,256]{1,2,0:T(8,128)} %add.256), channel_id=1, source_target_pairs={{0,2},{1,3},{2,0},{3,1},{4,6},{5,7},{6,4},{7,5},{8,10},{9,11},{10,... | collective-permute-start | bytes 3145736 | tf_op jit(solution)/shard_map/ppermute | solution.py:17
  151.0 0.9 copy-start.6
  158.6 15.3 %copy-start.3 = (f32[4,256,256]{1,2,0:T(8,128)S(1)}, f32[4,256,256]{1,2,0:T(8,128)}, u32[]{:S(2)}) copy-start(f32[4,256,256]{1,2,0:T(8,128)} %copy-done.2) | copy-start | bytes 3145732
  173.5 24.6 %collective-permute-start.2 = (f32[4,256,256]{1,2,0:T(8,128)S(1)}, f32[4,256,256]{1,2,0:T(8,128)S(1)}, u32[]{:S(2)}, u32[]{:S(2)}) collective-permute-start(f32[4,256,256]{1,2,0:T(8,128)S(1)} %add.260), channel_id=1, source_target_pairs={{0,4},{1,5},{2,6},{3,7},{4,0},{5,1},{6,2},{7,3},{8,12},{9,13},{10,... | collective-permute-start | bytes 3145736 | tf_op jit(solution)/shard_map/ppermute | solution.py:17
  174.4 1.6 copy-start.5
  174.4 1.7 copy-start.7
  174.5 2.0 copy-start.8
  198.2 46.9 %collective-permute-start.3 = (f32[4,256,256]{1,2,0:T(8,128)S(1)}, f32[4,256,256]{1,2,0:T(8,128)S(1)}, u32[]{:S(2)}, u32[]{:S(2)}) collective-permute-start(f32[4,256,256]{1,2,0:T(8,128)S(1)} %add.264), channel_id=1, source_target_pairs={{0,8},{1,9},{2,10},{3,11},{4,12},{5,13},{6,14},{7,15},{8,0},{9,1},... | collective-permute-start | bytes 3145736 | tf_op jit(solution)/shard_map/ppermute | solution.py:17
  204.4 41.1 %copy-start.4 = (f32[2,4,256,256]{3,2,1,0:T(8,128)S(1)}, f32[2,4,256,256]{3,2,1,0:T(8,128)}, u32[]{:S(2)}) copy-start(f32[2,4,256,256]{3,2,1,0:T(8,128)} %fusion.15) | copy-start | bytes 6291460
  249.8 6.0 %copy-start.1 = (bf16[512,2048]{1,0:T(8,128)(2,1)S(1)}, bf16[512,2048]{1,0:T(8,128)(2,1)}, u32[]{:S(2)}) copy-start(bf16[512,2048]{1,0:T(8,128)(2,1)} %param.7) | copy-start | bytes 6291460
Sparse Core Ops, SparseCore 0:
  9.6 103.1 all-gather.2
  115.0 60.1 all-gather.4
where the time goes:
time: 263 us
  waiting for transfers between devices  183 us (70%)
  matrix products  41.5 us (16%)
  local copies, waits for them, and re-layouts  16.3 us (6%)
  between operations  13.6 us (5%)
  other arithmetic  5.45 us (2%)
  starting transfers between devices  2.87 us (1%)
    all_gather x1, waiting for transfers between devices, on_device(): lax.all_gather(w_qkv, 'seq', axis=0, tiled=True)  105 us
    ppermute x4, waiting for transfers between devices, partner_2(): return lax.ppermute(value, axis, pairs)  76.6 us
    dot_general x1, matrix products, on_device(): jnp.dot(columns, lax.all_gather(w_qkv, 'seq', axis=0, tiled=True), prefer...  9.63 us
    dot_general x1, matrix products, on_device(): jnp.einsum('lij,lhci->chij', table, weights[:CBITS + 1], precision=highest)  8.37 us
    dot_general x5, matrix products, split_read(): jnp.einsum(form, query_half, upper_part, preferred_element_type=jnp.float32)  7.49 us
    dot_general x1, matrix products, on_device(): jnp.dot(columns, lax.all_gather(w_out, 'seq', axis=0, tiled=True), prefer...  5.99 us
  transfers between devices with their start and end apart: 6, of which 5 were waited for; matrix products, arithmetic and copies ran while one was open for 21% of the time, Pallas kernels for 0%

commit v1 on v0

v1 whole, which is shorter than its diff:
```python
import functools
import math

import jax
import jax.numpy as jnp
from jax import lax
from jax.experimental import pallas as pl
from jax.experimental.pallas import tpu as pltpu
from jax.sharding import PartitionSpec as P


HEADS = 4
HEAD = 256
SPAN = 256
CBITS = 8
CORES = 2
F32 = jnp.float32
BF16 = jnp.bfloat16


def swap(value, bit):
    mask = 1 << bit
    return lax.ppermute(value, "seq", [(i, i ^ mask) for i in range(lax.axis_size("seq"))])


def swap_crossed(value, bit):
    size = lax.axis_size("seq")
    pairs = [
        (g * size + i, g * size + (i ^ (1 << bit) ^ (g % 2)))
        for g in range(lax.axis_size("group"))
        for i in range(size)
    ]
    return lax.ppermute(value, ("group", "seq"), pairs)


def swap_x(value):
    return lax.ppermute(value, "group", [(i, i ^ 1) for i in range(lax.axis_size("group"))])


OWN, OTHER, MINE, FAR = range(4)


def gather_rows(first, mine, arrived, zbits, turn):
    pieces = [(mine, 0, MINE), (arrived, 0, FAR)]
    across = swap_crossed(first, 1)
    pieces.append((across, 1, OWN))
    pieces.append((swap_x(across), 1, OTHER))
    held = []
    for bit in reversed(zbits):
        flip = 1 << (bit - 1)
        got = [(swap_crossed(first, bit), flip)]
        for piece, before in held:
            got.append((swap(piece, bit), before ^ flip))
        held += got
    for at, (piece, flip) in enumerate(held):
        side = swap_x(piece)
        across = swap(piece, 1)
        if (at + turn) % 2:
            corner = swap_x(across)
        else:
            corner = swap(side, 1)
        pieces += [(piece, flip, OWN), (side, flip, OTHER), (across, flip ^ 1, OWN), (corner, flip ^ 1, OTHER)]
    return pieces


def first_rows(pieces, rows, device, sent_core):
    core, chip = device % CORES, device // CORES
    flips = jnp.asarray([piece[1] for piece in pieces], jnp.int32)
    halves = jnp.asarray([piece[2] for piece in pieces], jnp.int32)
    return ((chip ^ flips) * CORES + (jnp.where(halves < MINE, sent_core, core) ^ (halves & 1))) * rows


def split_kernel(parts, width, *refs):
    sources, outs = refs[:-3], refs[-3:]
    core = lax.axis_index("seq") % CORES
    sent_core = core ^ (lax.axis_index("group") % 2)
    for out, half in zip(outs, (sent_core, core, 1 - core)):
        row = 0
        for source, offset, stride in parts:
            ref = sources[source]
            start = pl.multiple_of(offset + half * stride, width)
            out[row : row + ref.shape[0], :] = ref[:, pl.ds(start, width)]
            row += ref.shape[0]


def row_copies(dst, refs, offset, cols, starts, rows, sem, first, base=0):
    copies = []
    for at, ref in enumerate(refs):
        start = pl.multiple_of(starts[base + at], rows)
        copies.append(
            pltpu.make_async_copy(
                ref.at[pl.ds(offset, rows), :], dst.at[pl.ds(start, rows), cols], sem.at[first + at]
            )
        )
    return copies


def dot(a, b):
    return lax.dot_general(a, b, (((1,), (0,)), ((), ())), preferred_element_type=F32)


def dot_tt(a, b):
    return lax.dot_general(a, b, (((1,), (1,)), ((), ())), preferred_element_type=F32)


def dot_outer(a, b):
    return lax.dot_general(a, b, (((0,), (0,)), ((), ())), preferred_element_type=F32)


def keys_values_kernel(n, rows, heads, starts, xa, xb, scale, *refs):
    del scale
    pieces = refs[:n]
    ka, kb, va, vb, da, db, sent, wk, wv, x, sem, xsem = refs[n:]
    everything = slice(None)
    vcopies = row_copies(wv, pieces, 0, everything, starts, rows, sem, 0)
    kcopies = row_copies(wk, pieces, rows, everything, starts, rows, sem, n)
    xcopies = [pltpu.make_async_copy(src, x.at[i], xsem.at[i]) for i, src in enumerate((xa, xb))]
    xcopies[0].start()
    for copy in kcopies + vcopies:
        copy.start()
    xcopies[1].start()
    xcopies[0].wait()
    for copy in kcopies:
        copy.wait()
    sums = [None] * heads
    for i, (k_out, v_out) in enumerate(((ka, va), (kb, vb))):
        if i:
            xcopies[i].wait()
        k = dot(x[i], wk[...]).astype(BF16)
        k_out[...] = k
        if i == 0:
            for copy in vcopies:
                copy.wait()
        v = dot(x[i], wv[...]).astype(BF16)
        v_out[...] = v
        for h in range(heads):
            cols = slice(h * HEAD, (h + 1) * HEAD)
            state = dot_outer(k[:, cols], v[:, cols])
            (da, db)[i][h] = state.astype(BF16)
            sums[h] = state if i == 0 else sums[h] + state
    for h in range(heads):
        sent[h] = sums[h].astype(BF16)


def attend_kernel(which, n, nb, rows, out_rows, heads, levels, local_bits, starts, x_hbm, k, v, other, scale, *refs):
    buckets, pieces, refs = refs[:nb], refs[nb : nb + n], refs[nb + n :]
    if which:
        out, w_out, wq, x, sem, xsem, w, wsem = refs
    else:
        out, wq, x, sem, xsem = refs
    xcopy = pltpu.make_async_copy(x_hbm, x, xsem.at[0])
    xcopy.start()
    copies = row_copies(wq, pieces, 0, slice(None), starts, rows, sem, 0)
    for copy in copies:
        copy.start()
    moves = []
    if which:
        width = pieces[0].shape[1]
        for part in range(w.shape[1] // width):
            cols_of = pl.ds(part * width, width)
            moves += row_copies(w, pieces, rows + part * out_rows, cols_of, starts, out_rows, wsem, len(moves), n)
        for move in moves:
            move.start()
    row = lax.broadcasted_iota(jnp.int32, (SPAN, SPAN), 0)
    col = lax.broadcasted_iota(jnp.int32, (SPAN, SPAN), 1)
    apart = row ^ col
    causal = row >= col
    xcopy.wait()
    for copy in copies:
        copy.wait()
    q = dot(x[...], wq[...]).astype(BF16)
    store = None
    if which:
        for move in moves:
            move.wait()
        store = pltpu.make_async_copy(w, w_out, xsem.at[1])
        store.start()
    first = CBITS + local_bits + 1
    for h in range(heads):
        cols = slice(h * HEAD, (h + 1) * HEAD)
        states = []
        for c in range(q.shape[0] // SPAN):
            span = slice(c * SPAN, (c + 1) * SPAN)

            def weight(level):
                at = h * levels + level
                return scale[which, span, at : at + 1]

            mixing = jnp.broadcast_to(weight(0), (SPAN, SPAN))
            for level in range(1, CBITS + 1):
                mixing = jnp.where(apart >= 1 << (level - 1), weight(level), mixing)
            qh, kh, vh = q[span, cols], k[span, cols], v[span, cols]
            probs = jnp.where(causal, dot_tt(qh, kh) * mixing, 0.0).astype(BF16)
            value = dot(probs, vh)
            states.append(dot_outer(kh, vh) if c + 1 < q.shape[0] // SPAN else None)
            for b in range(1, local_bits + 1):
                half = 1 << (b - 1)
                if c & half:
                    base = (c >> b) << b
                    bucket = sum(states[base + 1 : base + half], states[base])
                    value = value + dot(qh, bucket.astype(BF16)) * weight(CBITS + b)
            for at, bucket in enumerate((other, *buckets)):
                value = value + dot(qh, bucket[h]) * weight(first + at)
            out[span, cols] = value.astype(BF16)
    if which:
        store.wait()


def output_kernel(width, core_ref, mine, theirs, w_mine, w_theirs, out, w, block, wsem, osem):
    depth = mine.shape[1]
    core = core_ref[0]
    parts = w_mine.shape[1] // width
    loads, stores = [], []
    for side, src in enumerate((w_mine, w_theirs)):
        for part in range(parts):
            at = side * parts + part
            loads.append(pltpu.make_async_copy(src.at[:, pl.ds(part * width, width)], w.at[at], wsem.at[at]))
            loads[-1].start()
    low = pl.multiple_of(core * depth, depth)
    high = pl.multiple_of((1 - core) * depth, depth)
    for at, load in enumerate(loads):
        load.wait()
        value = dot(mine[...], w[at, pl.ds(low, depth), :]) + dot(theirs[...], w[at, pl.ds(high, depth), :])
        block[at] = value.astype(BF16)
        half = core if at < parts else 1 - core
        start = pl.multiple_of((half * parts + at % parts) * width, width)
        stores.append(pltpu.make_async_copy(block.at[at], out.at[:, pl.ds(start, width)], osem.at[at]))
        stores[-1].start()
    for store in stores:
        store.wait()


ANY = pl.BlockSpec(memory_space=pl.ANY)


def whole(shape):
    return pl.BlockSpec(shape, lambda *ids: (0,) * len(shape))


def call(kernel, in_specs, out_specs, out_shape, scratch, flops, grid=(1,)):
    return pl.pallas_call(
        kernel,
        grid_spec=pltpu.PrefetchScalarGridSpec(
            num_scalar_prefetch=1, grid=grid, in_specs=in_specs, out_specs=out_specs, scratch_shapes=scratch
        ),
        out_shape=out_shape,
        compiler_params=pltpu.CompilerParams(dimension_semantics=("arbitrary",), vmem_limit_bytes=60 << 20),
        cost_estimate=pl.CostEstimate(flops=flops, bytes_accessed=8 << 20, transcendentals=0),
    )


def on_device(tokens, w_qkv, w_out, level_weight):
    seq_bits = lax.axis_size("seq").bit_length() - 1
    device = lax.axis_index("seq")
    core = device % CORES
    odd_group = lax.axis_index("group") % 2
    sent_core = core ^ odd_group
    zbits = list(range(2, seq_bits))
    toks, width = tokens.shape
    levels = level_weight.shape[0]
    heads = HEADS // CORES
    cols = heads * HEAD
    head_cols = HEADS * HEAD
    local_bits = (toks // SPAN).bit_length() - 1
    rows = w_qkv.shape[0]
    out_rows, out_width = w_out.shape
    out_cols = out_width // CORES
    sd = jax.ShapeDtypeStruct

    def split(sources, parts):
        shape = (sum(sources[part[0]].shape[0] for part in parts), cols)
        first, mine, far = pl.pallas_call(
            functools.partial(split_kernel, parts, cols),
            out_shape=[sd(shape, BF16)] * 3,
            cost_estimate=pl.CostEstimate(flops=1 << 20, bytes_accessed=2 << 20, transcendentals=0),
        )(*sources)
        return first, mine, swap(far, 0)

    kv_split = split((w_qkv,), ((0, 2 * head_cols, cols), (0, head_cols, cols)))
    out_parts = out_cols // cols
    qo_split = split((w_qkv, w_out), ((0, 0, cols),) + tuple((1, n * cols, out_cols) for n in range(out_parts)))
    far_tokens = swap(tokens, 0)

    own_w = lax.dynamic_slice(level_weight, (0, core * heads, 0), (levels, heads, toks))
    far_w = swap(lax.dynamic_slice(level_weight, (0, (1 - core) * heads, 0), (levels, heads, toks)), 0)
    gains = [1.0 / math.sqrt(HEAD * max(1, 2 ** (n - 1))) for n in range(CBITS + 1)]
    gains += [1.0 / math.sqrt(SPAN * 2 ** (b - 1) * HEAD) for b in range(1, levels - CBITS)]
    first_bit = CBITS + 1 + local_bits
    shifts = jnp.asarray([max(0, n - first_bit) for n in range(levels)], jnp.int32)
    always = jnp.asarray([n < first_bit for n in range(levels)])
    block_device = jnp.stack([device, device ^ 1])
    on = jnp.where(always[None], 1, (block_device[:, None] >> shifts[None]) & 1).astype(F32)
    on = on * jnp.asarray(gains, F32)[None]
    scale = jnp.stack([own_w, far_w]) * on[:, :, None, None]
    scale = jnp.transpose(scale, (0, 3, 2, 1)).reshape(2, toks, heads * levels)

    kvp = gather_rows(*kv_split, zbits, 0)
    qop = gather_rows(*qo_split, zbits, 1)

    act = sd((toks, cols), BF16)
    act_spec = whole((toks, cols))
    state_spec = whole((heads, HEAD, HEAD))
    state = sd((heads, HEAD, HEAD), BF16)
    ka, kb, va, vb, da, db, total = call(
        functools.partial(keys_values_kernel, len(kvp), rows, heads),
        [ANY] * (3 + len(kvp)),
        [act_spec] * 4 + [state_spec] * 3,
        [act] * 4 + [state] * 3,
        [
            pltpu.VMEM((width, cols), BF16),
            pltpu.VMEM((width, cols), BF16),
            pltpu.VMEM((2, toks, width), BF16),
            pltpu.SemaphoreType.DMA((2 * len(kvp),)),
            pltpu.SemaphoreType.DMA((2,)),
        ],
        2 * 2 * toks * width * 2 * cols,
    )(first_rows(kvp, rows, device, sent_core), tokens, far_tokens, scale, *(piece[0] for piece in kvp))

    buckets = []
    for bit in range(1, seq_bits):
        arrived = swap(total, bit)
        buckets.append(arrived)
        total = (total.astype(F32) + arrived.astype(F32)).astype(BF16)

    def attend(which, x, k, v, other):
        specs, shapes = [act_spec], [act]
        scratch = [
            pltpu.VMEM((width, cols), BF16),
            pltpu.VMEM((toks, width), BF16),
            pltpu.SemaphoreType.DMA((len(qop),)),
            pltpu.SemaphoreType.DMA((2,)),
        ]
        if which:
            specs.append(ANY)
            shapes.append(sd((head_cols, out_cols), BF16))
            scratch += [pltpu.VMEM((head_cols, out_cols), BF16), pltpu.SemaphoreType.DMA((out_parts * len(qop),))]
        return call(
            functools.partial(
                attend_kernel, which, len(qop), len(buckets), rows, out_rows, heads, levels, local_bits
            ),
            [ANY] + [act_spec] * 2 + [state_spec] + [whole(scale.shape)] + [state_spec] * len(buckets)
            + [ANY] * len(qop),
            specs,
            shapes,
            scratch,
            2 * toks * width * cols,
        )(
            jnp.concatenate(
                [first_rows(qop, rows, device, sent_core), first_rows(qop, out_rows, device, sent_core)]
            ),
            x, k, v, other, scale, *buckets, *(piece[0] for piece in qop),
        )

    far_part, w_mine = attend(1, far_tokens, kb, vb, da)
    theirs = swap(far_part, 0)
    w_theirs = swap(w_mine, 0)
    (mine,) = attend(0, tokens, ka, va, db)
    n_blocks = CORES * out_parts
    return call(
        functools.partial(output_kernel, cols),
        [act_spec, act_spec, ANY, ANY],
        ANY,
        sd((toks, out_width), BF16),
        [
            pltpu.VMEM((n_blocks, head_cols, cols), BF16),
            pltpu.VMEM((n_blocks, toks, cols), BF16),
            pltpu.SemaphoreType.DMA((n_blocks,)),
            pltpu.SemaphoreType.DMA((n_blocks,)),
        ],
        2 * toks * head_cols * out_width,
    )(core.reshape(1).astype(jnp.int32), mine, theirs, w_mine, w_theirs)


def solution(mesh):
    return jax.shard_map(
        on_device,
        mesh=mesh,
        in_specs=(
            P(("group", "seq"), None),
            P("seq", None),
            P("seq", None),
            P(None, None, ("group", "seq")),
        ),
        out_specs=P(("group", "seq"), None),
        check_vma=False,
    )
```

time: 263 us -> 136 us (0.52)
  waiting for transfers between devices: 183 us -> 49.4 us
  matrix products: 41.5 us -> 0 us
  Pallas kernels: 0 us -> 38.7 us
  starting transfers between devices: 2.87 us -> 37.1 us
  between operations: 13.6 us -> 0.3 us
  local copies, waits for them, and re-layouts: 16.3 us -> 5.66 us
    all_gather x2 -> x0, waiting for transfers between devices: 105 us -> none  [the longest x1 105 us: on_device(): lax.all_gather(w_qkv, 'seq', axis=0, tiled=True)]
    dot_general x15 -> x0, matrix products: 41.5 us -> none  [the longest x1 9.63 us: on_device(): jnp.dot(columns, lax.all_gather(w_qkv, 'seq', axis=0, tiled=True), prefer...]
    pallas_call x0 -> x6, Pallas kernels: none -> 38.7 us  [the longest x2 18.1 us: attend(): call(functools.partial(attend_kernel, which, len(qop), len(buckets), rows...]
    ppermute x4 -> x37, starting transfers between devices: 2.83 us -> 37.1 us  [the longest x20 15.8 us: swap(): lax.ppermute(value, 'seq', [(i, i ^ mask) for i in range(lax.axis_size('s...]
    ppermute x4 -> x37, waiting for transfers between devices: 76.6 us -> 49.4 us  [the longest x20 29.2 us: swap(): lax.ppermute(value, 'seq', [(i, i ^ mask) for i in range(lax.axis_size('s...]
    add x4 -> x0, other arithmetic: 5.41 us -> none  [the longest x3 4.61 us: on_device(): block_total = block_total + partner]
    slice x6 -> x0, local copies, waits for them, and re-layouts: 3.92 us -> none  [the longest x4 1.41 us: on_device(): weights[:CBITS + 1]]
    reshape x4 -> x1, local copies, waits for them, and re-layouts: 4.11 us -> 1.03 us  [on_device(): scale = jnp.transpose(scale, (0, 3, 2, 1)).reshape(2, toks, heads * levels)]
  transfers between devices with their start and end apart: 6 -> 37, of which waited for: 5 -> 17; matrix products, arithmetic and copies ran while one was open for 21% -> 4% of each run, Pallas kernels for 0% -> 17%
where the time goes in v1:
time: 136 us; the launch traced here: 135 us
  waiting for transfers between devices  49.4 us (36%)
  Pallas kernels  38.7 us (28%)
  starting transfers between devices  37.1 us (27%)
  local copies, waits for them, and re-layouts  5.66 us (4%)
  other arithmetic  3.89 us (3%)
    ppermute x20, waiting for transfers between devices, swap(): lax.ppermute(value, 'seq', [(i, i ^ mask) for i in range(lax.axis_size('s...  29.2 us
    pallas_call x2, Pallas kernels, attend(): call(functools.partial(attend_kernel, which, len(qop), len(buckets), rows...  18.1 us
    ppermute x20, starting transfers between devices, swap(): lax.ppermute(value, 'seq', [(i, i ^ mask) for i in range(lax.axis_size('s...  15.8 us
    ppermute x11, waiting for transfers between devices, swap_x(): lax.ppermute(value, 'group', [(i, i ^ 1) for i in range(lax.axis_size('gr...  11.9 us
    ppermute x11, starting transfers between devices, swap_x(): lax.ppermute(value, 'group', [(i, i ^ 1) for i in range(lax.axis_size('gr...  11.3 us
    pallas_call x1, Pallas kernels, on_device(): call(functools.partial(keys_values_kernel, len(kvp), rows, heads), [ANY]...  10.3 us
    ppermute x6, starting transfers between devices, swap_crossed(): return lax.ppermute(value, ('group', 'seq'), pairs)  9.9 us
    ppermute x6, waiting for transfers between devices, swap_crossed(): return lax.ppermute(value, ('group', 'seq'), pairs)  8.31 us
  transfers between devices with their start and end apart: 37, of which 17 were waited for; matrix products, arithmetic and copies ran while one was open for 4% of the time, Pallas kernels for 17%

profile of v1, /device:TPU:0, one launch (start us, length us, event | category | flops | bytes accessed | tf_op | source)
XLA Modules:
  0.0 135.0 jit_solution(10227504166967796709)
XLA Ops:
  0.0 0.5 collective-permute-start
  0.5 2.1 %shard_map.163 = (bf16[256,512]{1,0:T(8,128)(2,1)}, bf16[256,512]{1,0:T(8,128)(2,1)}, bf16[256,512]{1,0:T(8,128)(2,1)}) custom-call(bf16[128,3072]{1,0:T(8,128)(2,1)} %refs_0_.3), custom_call_target="tpu_custom_call" | custom-call | flops 1048576 | bytes 2097152 | tf_op jit(solution)/shard_map/pallas_call | solution.py:272
  2.5 2.5 %collective-permute-start.3 = (bf16[256,512]{1,0:T(8,128)(2,1)}, bf16[256,512]{1,0:T(8,128)(2,1)S(1)}, u32[]{:S(2)}, u32[]{:S(2)}) collective-permute-start(bf16[256,512]{1,0:T(8,128)(2,1)} %get-tuple-element.22), channel_id=1, source_target_pairs={{0,2},{1,3},{2,0},{3,1},{4,6},{5,7},{6,4},{7,5},{8,10},{9,11},{10,... | collective-permute-start | bytes 786440 | tf_op jit(solution)/shard_map/ppermute | solution.py:33
  5.1 2.6 %collective-permute-start.5 = (bf16[256,512]{1,0:T(8,128)(2,1)}, bf16[256,512]{1,0:T(8,128)(2,1)S(1)}, u32[]{:S(2)}, u32[]{:S(2)}) collective-permute-start(bf16[256,512]{1,0:T(8,128)(2,1)} %get-tuple-element.22), channel_id=1, source_target_pairs={{0,8},{1,9},{2,10},{3,11},{4,12},{5,13},{6,14},{7,15},{8,0},{9,1},... | collective-permute-start | bytes 786440 | tf_op jit(solution)/shard_map/ppermute | solution.py:33
  7.6 1.0 dynamic-slice_bitcast_fusion
  8.7 0.6 collective-permute-start.1
  9.3 0.9 collective-permute-done.1
  10.1 1.6 %collective-permute-start.9 = (bf16[256,512]{1,0:T(8,128)(2,1)}, bf16[256,512]{1,0:T(8,128)(2,1)S(1)}, u32[]{:S(2)}, u32[]{:S(2)}) collective-permute-start(bf16[256,512]{1,0:T(8,128)(2,1)} %get-tuple-element.22), channel_id=1, source_target_pairs={{0,4},{1,5},{2,6},{3,7},{4,0},{5,1},{6,2},{7,3},{8,12},{9,13},{10,... | collective-permute-start | bytes 786440 | tf_op jit(solution)/shard_map/ppermute | solution.py:33
  11.7 0.5 collective-permute-done.3.refs_2_
  12.2 0.9 collective-permute-start.4
  13.2 7.2 %collective-permute-done.5.refs_4_ = bf16[256,512]{1,0:T(8,128)(2,1)S(1)} collective-permute-done((bf16[256,512]{1,0:T(8,128)(2,1)}, bf16[256,512]{1,0:T(8,128)(2,1)S(1)}, u32[]{:S(2)}, u32[]{:S(2)}) %collective-permute-start.5) | collective-permute-done | bytes 262176 | tf_op jit(solution)/shard_map/ppermute | solution.py:33
  20.3 1.5 %collective-permute-start.6 = (bf16[256,512]{1,0:T(8,128)(2,1)S(1)}, bf16[256,512]{1,0:T(8,128)(2,1)}, u32[]{:S(2)}, u32[]{:S(2)}) collective-permute-start(bf16[256,512]{1,0:T(8,128)(2,1)S(1)} %collective-permute-done.5.refs_4_), channel_id=1, source_target_pairs={{0,16},{16,0},{1,17},{17,1},{2,18},{18,2},{3,19},{19,3},{4,20},{20... | collective-permute-start | bytes 786440 | tf_op jit(solution)/shard_map/ppermute | solution.py:37
  21.8 1.0 collective-permute-start.13
  22.8 0.6 collective-permute-done.9.refs_8_
  23.4 0.5 collective-permute-start.7
  23.9 1.3 collective-permute-start.10
  25.2 4.4 %collective-permute-done.6.refs_5_ = bf16[256,512]{1,0:T(8,128)(2,1)} collective-permute-done((bf16[256,512]{1,0:T(8,128)(2,1)S(1)}, bf16[256,512]{1,0:T(8,128)(2,1)}, u32[]{:S(2)}, u32[]{:S(2)}) %collective-permute-start.6) | collective-permute-done | bytes 262176 | tf_op jit(solution)/shard_map/ppermute | solution.py:37
  29.6 0.5 collective-permute-start.11
  30.1 1.5 %collective-permute-start.14 = (bf16[256,512]{1,0:T(8,128)(2,1)}, bf16[256,512]{1,0:T(8,128)(2,1)}, u32[]{:S(2)}, u32[]{:S(2)}) collective-permute-start(bf16[256,512]{1,0:T(8,128)(2,1)} %collective-permute-done.13.refs_12_), channel_id=1, source_target_pairs={{0,16},{16,0},{1,17},{17,1},{2,18},{18,2},{3,19},{19,3},{4,20},{20... | collective-permute-start | bytes 786440 | tf_op jit(solution)/shard_map/ppermute | solution.py:37
  31.7 0.8 convert_multiply_fusion
  32.5 1.5 %collective-permute-start.15 = (bf16[256,512]{1,0:T(8,128)(2,1)}, bf16[256,512]{1,0:T(8,128)(2,1)}, u32[]{:S(2)}, u32[]{:S(2)}) collective-permute-start(bf16[256,512]{1,0:T(8,128)(2,1)} %collective-permute-done.13.refs_12_), channel_id=1, source_target_pairs={{0,2},{1,3},{2,0},{3,1},{4,6},{5,7},{6,4},{7,5},{8,10},{9,11},{10,... | collective-permute-start | bytes 786440 | tf_op jit(solution)/shard_map/ppermute | solution.py:23
  34.0 1.3 collective-permute-done.10.refs_9_
  35.2 0.5 collective-permute-start.8
  35.7 3.2 %collective-permute-done.11.refs_10_ = bf16[256,512]{1,0:T(8,128)(2,1)} collective-permute-done((bf16[256,512]{1,0:T(8,128)(2,1)S(1)}, bf16[256,512]{1,0:T(8,128)(2,1)}, u32[]{:S(2)}, u32[]{:S(2)}) %collective-permute-start.11) | collective-permute-done | bytes 262176 | tf_op jit(solution)/shard_map/ppermute | solution.py:23
  38.9 1.5 %collective-permute-start.12 = (bf16[256,512]{1,0:T(8,128)(2,1)}, bf16[256,512]{1,0:T(8,128)(2,1)}, u32[]{:S(2)}, u32[]{:S(2)}) collective-permute-start(bf16[256,512]{1,0:T(8,128)(2,1)} %collective-permute-done.11.refs_10_), channel_id=1, source_target_pairs={{0,16},{16,0},{1,17},{17,1},{2,18},{18,2},{3,19},{19,3},{4,20},{20... | collective-permute-start | bytes 786440 | tf_op jit(solution)/shard_map/ppermute | solution.py:37
  40.4 0.5 collective-permute-start.16
  40.9 1.2 broadcast_multiply_fusion.1
  42.1 2.1 %shard_map.165 = (bf16[256,512]{1,0:T(8,128)(2,1)}, bf16[256,512]{1,0:T(8,128)(2,1)}, bf16[256,512]{1,0:T(8,128)(2,1)}) custom-call(bf16[128,3072]{1,0:T(8,128)(2,1)} %refs_0_.3, bf16[64,2048]{1,0:T(8,128)(2,1)} %refs_1_.1), custom_call_target="tpu_custom_call" | custom-call | flops 1048576 | bytes 2097152 | tf_op jit(solution)/shard_map/pallas_call | solution.py:272
  44.4 1.0 copy.20.scale
  45.4 4.7 %collective-permute-done.8.refs_7_ = bf16[256,512]{1,0:T(8,128)(2,1)} collective-permute-done((bf16[256,512]{1,0:T(8,128)(2,1)}, bf16[256,512]{1,0:T(8,128)(2,1)}, u32[]{:S(2)}, u32[]{:S(2)}) %collective-permute-start.8) | collective-permute-done | bytes 262176 | tf_op jit(solution)/shard_map/ppermute | solution.py:23
  50.1 0.5 collective-permute-start.21
  50.6 2.2 %collective-permute-start.23 = (bf16[256,512]{1,0:T(8,128)(2,1)}, bf16[256,512]{1,0:T(8,128)(2,1)S(1)}, u32[]{:S(2)}, u32[]{:S(2)}) collective-permute-start(bf16[256,512]{1,0:T(8,128)(2,1)} %get-tuple-element.29), channel_id=1, source_target_pairs={{0,8},{1,9},{2,10},{3,11},{4,12},{5,13},{6,14},{7,15},{8,0},{9,1},... | collective-permute-start | bytes 786440 | tf_op jit(solution)/shard_map/ppermute | solution.py:33
  52.8 3.0 %collective-permute-done.16.refs_15_ = bf16[256,512]{1,0:T(8,128)(2,1)} collective-permute-done((bf16[256,512]{1,0:T(8,128)(2,1)}, bf16[256,512]{1,0:T(8,128)(2,1)}, u32[]{:S(2)}, u32[]{:S(2)}) %collective-permute-start.16) | collective-permute-done | bytes 262176 | tf_op jit(solution)/shard_map/ppermute | solution.py:23
  55.8 1.3 copy-done.2
  57.1 10.3 %shard_map.164 = (bf16[512,512]{1,0:T(8,128)(2,1)}, bf16[512,512]{1,0:T(8,128)(2,1)}, bf16[512,512]{1,0:T(8,128)(2,1)}, bf16[512,512]{1,0:T(8,128)(2,1)}, bf16[2...) custom-call(s32[16]{0:T(128)} %get-tuple-element.35.starts, ...), custom_call_target="tpu_custom_call" | custom-call | flops 4294967296 | bytes 8388608 | tf_op jit(solution)/shard_map/pallas_call | solution.py:304
  67.4 0.5 collective-permute-start.17
  67.9 0.6 collective-permute-start.27
  68.5 1.0 collective-permute-start.22
  69.5 1.9 %collective-permute-start.31 = (bf16[256,512]{1,0:T(8,128)(2,1)S(1)}, bf16[256,512]{1,0:T(8,128)(2,1)S(1)}, u32[]{:S(2)}, u32[]{:S(2)}) collective-permute-start(bf16[256,512]{1,0:T(8,128)(2,1)S(1)} %collective-permute-done.23.refs_7_), channel_id=1, source_target_pairs={{0,4},{1,5},{2,6},{3,7},{4,0},{5,1},{6,2},{7,3},{8,12},{9,13},{10,... | collective-permute-start | bytes 786440 | tf_op jit(solution)/shard_map/ppermute | solution.py:23
  71.4 2.7 %collective-permute-done.17.refs_0_ = bf16[2,256,256]{2,1,0:T(8,128)(2,1)S(1)} collective-permute-done((bf16[2,256,256]{2,1,0:T(8,128)(2,1)}, bf16[2,256,256]{2,1,0:T(8,128)(2,1)S(1)}, u32[]{:S(2)}, u32[]{:S(2)}) %collective-permute-start.17) | collective-permute-done | bytes 262176 | tf_op jit(solution)/shard_map/ppermute | solution.py:23
  74.0 1.1 add_convert_fusion.1
  75.1 0.8 collective-permute-start.18
  75.9 1.4 %collective-permute-start.24 = (bf16[256,512]{1,0:T(8,128)(2,1)S(1)}, bf16[256,512]{1,0:T(8,128)(2,1)S(1)}, u32[]{:S(2)}, u32[]{:S(2)}) collective-permute-start(bf16[256,512]{1,0:T(8,128)(2,1)S(1)} %collective-permute-done.23.refs_7_), channel_id=1, source_target_pairs={{0,16},{16,0},{1,17},{17,1},{2,18},{18,2},{3,19},{19,3},{4,20},{20... | collective-permute-start | bytes 786440 | tf_op jit(solution)/shard_map/ppermute | solution.py:37
  77.4 1.2 collective-permute-start.25
  78.7 3.9 %collective-permute-done.31.refs_15_ = bf16[256,512]{1,0:T(8,128)(2,1)S(1)} collective-permute-done((bf16[256,512]{1,0:T(8,128)(2,1)S(1)}, bf16[256,512]{1,0:T(8,128)(2,1)S(1)}, u32[]{:S(2)}, u32[]{:S(2)}) %collective-permute-start.31) | collective-permute-done | bytes 262176 | tf_op jit(solution)/shard_map/ppermute | solution.py:23
  82.6 1.6 %collective-permute-start.33 = (bf16[256,512]{1,0:T(8,128)(2,1)S(1)}, bf16[256,512]{1,0:T(8,128)(2,1)S(1)}, u32[]{:S(2)}, u32[]{:S(2)}) collective-permute-start(bf16[256,512]{1,0:T(8,128)(2,1)S(1)} %collective-permute-done.31.refs_15_), channel_id=1, source_target_pairs={{0,2},{1,3},{2,0},{3,1},{4,6},{5,7},{6,4},{7,5},{8,10},{9,11},{10,... | collective-permute-start | bytes 786440 | tf_op jit(solution)/shard_map/ppermute | solution.py:23
  84.2 1.6 %collective-permute-done.18.refs_1_ = bf16[2,256,256]{2,1,0:T(8,128)(2,1)S(1)} collective-permute-done((bf16[2,256,256]{2,1,0:T(8,128)(2,1)S(1)}, bf16[2,256,256]{2,1,0:T(8,128)(2,1)S(1)}, u32[]{:S(2)}, u32[]{:S(2)}) %collective-permute-start.18) | collective-permute-done | bytes 262176 | tf_op jit(solution)/shard_map/ppermute | solution.py:23
  85.7 1.6 %collective-permute-start.29 = (bf16[256,512]{1,0:T(8,128)(2,1)S(1)}, bf16[256,512]{1,0:T(8,128)(2,1)S(1)}, u32[]{:S(2)}, u32[]{:S(2)}) collective-permute-start(bf16[256,512]{1,0:T(8,128)(2,1)S(1)} %collective-permute-done.27.refs_11_), channel_id=1, source_target_pairs={{0,2},{1,3},{2,0},{3,1},{4,6},{5,7},{6,4},{7,5},{8,10},{9,11},{10,... | collective-permute-start | bytes 786440 | tf_op jit(solution)/shard_map/ppermute | solution.py:23
  87.6 1.9 %collective-permute-start.26 = (bf16[256,512]{1,0:T(8,128)(2,1)S(1)}, bf16[256,512]{1,0:T(8,128)(2,1)S(1)}, u32[]{:S(2)}, u32[]{:S(2)}) collective-permute-start(bf16[256,512]{1,0:T(8,128)(2,1)S(1)} %collective-permute-done.25.refs_9_), channel_id=1, source_target_pairs={{0,16},{16,0},{1,17},{17,1},{2,18},{18,2},{3,19},{19,3},{4,20},{20... | collective-permute-start | bytes 786440 | tf_op jit(solution)/shard_map/ppermute | solution.py:37
  89.5 0.7 collective-permute-start.30
  90.1 2.0 %collective-permute-done.33.refs_17_ = bf16[256,512]{1,0:T(8,128)(2,1)S(1)} collective-permute-done((bf16[256,512]{1,0:T(8,128)(2,1)S(1)}, bf16[256,512]{1,0:T(8,128)(2,1)S(1)}, u32[]{:S(2)}, u32[]{:S(2)}) %collective-permute-start.33) | collective-permute-done | bytes 262176 | tf_op jit(solution)/shard_map/ppermute | solution.py:23
  92.2 5.6 %collective-permute-done.29.refs_13_ = bf16[256,512]{1,0:T(8,128)(2,1)S(1)} collective-permute-done((bf16[256,512]{1,0:T(8,128)(2,1)S(1)}, bf16[256,512]{1,0:T(8,128)(2,1)S(1)}, u32[]{:S(2)}, u32[]{:S(2)}) %collective-permute-start.29) | collective-permute-done | bytes 262176 | tf_op jit(solution)/shard_map/ppermute | solution.py:23
  97.8 1.6 %collective-permute-start.19 = (bf16[2,256,256]{2,1,0:T(8,128)(2,1)S(1)}, bf16[2,256,256]{2,1,0:T(8,128)(2,1)S(1)}, u32[]{:S(2)}, u32[]{:S(2)}) collective-permute-start(bf16[2,256,256]{2,1,0:T(8,128)(2,1)S(1)} %add_convert_fusion), channel_id=1, source_target_pairs={{0,8},{1,9},{2,10},{3,11},{4,12},{5,13},{6,14},{7,15},{8,0},{9,1},... | collective-permute-start | bytes 786440 | tf_op jit(solution)/shard_map/ppermute | solution.py:23
  99.4 0.6 pad_add_fusion.starts
  99.9 2.3 %collective-permute-done.26.refs_10_ = bf16[256,512]{1,0:T(8,128)(2,1)S(1)} collective-permute-done((bf16[256,512]{1,0:T(8,128)(2,1)S(1)}, bf16[256,512]{1,0:T(8,128)(2,1)S(1)}, u32[]{:S(2)}, u32[]{:S(2)}) %collective-permute-start.26) | collective-permute-done | bytes 262176 | tf_op jit(solution)/shard_map/ppermute | solution.py:37
  102.3 3.9 %collective-permute-done.34.refs_18_ = bf16[256,512]{1,0:T(8,128)(2,1)S(1)} collective-permute-done((bf16[256,512]{1,0:T(8,128)(2,1)S(1)}, bf16[256,512]{1,0:T(8,128)(2,1)S(1)}, u32[]{:S(2)}, u32[]{:S(2)}) %collective-permute-start.34) | collective-permute-done | bytes 262176 | tf_op jit(solution)/shard_map/ppermute | solution.py:37
  106.2 1.7 %collective-permute-done.19.refs_2_ = bf16[2,256,256]{2,1,0:T(8,128)(2,1)S(1)} collective-permute-done((bf16[2,256,256]{2,1,0:T(8,128)(2,1)S(1)}, bf16[2,256,256]{2,1,0:T(8,128)(2,1)S(1)}, u32[]{:S(2)}, u32[]{:S(2)}) %collective-permute-start.19) | collective-permute-done | bytes 262176 | tf_op jit(solution)/shard_map/ppermute | solution.py:23
  107.9 0.7 copy-done.18
  108.7 10.1 %shard_map.167 = (bf16[512,512]{1,0:T(8,128)(2,1)}, bf16[1024,1024]{1,0:T(8,128)(2,1)}) custom-call(s32[32]{0:T(128)} %pad_add_fusion.starts, bf16[512,2048]{1,0:T(8,128)(2,1)} %copy-done.2, bf16[512,512]{1,0:T(8,128)(2,1)} %get-tuple-element.30.k, bf16[512,512]{1,0:T(8,128)(2,1)} %get-tuple-element.31.v, bf16[2,256,256]{2,1,0:T(8,128)(2,1)} %get-tuple-element.32.other, ...), custom_call_target="tpu_custom_call" | custom-call | flops 1073741824 | bytes 8388608 | tf_op jit(solution)/shard_map/pallas_call | solution.py:337
  118.9 0.5 collective-permute-start.35
  119.4 8.0 %shard_map.166.mine = bf16[512,512]{1,0:T(8,128)(2,1)} custom-call(s32[32]{0:T(128)} %pad_add_fusion.starts, bf16[512,2048]{1,0:T(8,128)(2,1)} %x_hbm.1, bf16[512,512]{1,0:T(8,128)(2,1)} %get-tuple-element.23.k, bf16[512,512]{1,0:T(8,128)(2,1)} %get-tuple-element.24.v, bf16[2,256,256]{2,1,0:T(8,128)(2,1)} %get-tuple-element.25.other, ...), custom_call_target="tpu_custom_call" | custom-call | flops 1073741824 | bytes 8388608 | tf_op jit(solution)/shard_map/pallas_call | solution.py:337
  127.4 0.8 copy-done.21
  128.2 0.7 copy-done.20
  128.9 6.1 %shard_map.168 = bf16[512,2048]{1,0:T(8,128)(2,1)} custom-call(s32[1]{0:T(128)} %bitcast.core_ref, bf16[512,512]{1,0:T(8,128)(2,1)} %shard_map.166.mine, bf16[512,512]{1,0:T(8,128)(2,1)} %copy-done.21, bf16[1024,1024]{1,0:T(8,128)(2,1)} %get-tuple-element.34.w_mine, bf16[1024,1024]{1,0:T(8,128)(2,1)} %copy-done.20), custom_call_target="tpu_custom_call" | custom-call | flops 2147483648 | bytes 8388608 | tf_op jit(solution)/shard_map/pallas_call | solution.py:359
  (81 shorter events, 0.9 us)
Async XLA Ops:
  0.0 55.8 %collective-permute-start = (bf16[512,2048]{1,0:T(8,128)(2,1)}, bf16[512,2048]{1,0:T(8,128)(2,1)S(1)}, u32[]{:S(2)}, u32[]{:S(2)}) collective-permute-start(bf16[512,2048]{1,0:T(8,128)(2,1)} %x_hbm.1), channel_id=1, source_target_pairs={{0,1},{1,0},{2,3},{3,2},{4,5},{5,4},{6,7},{7,6},{8,9},{9,8},{10,11... | collective-permute-start | bytes 6291464 | tf_op jit(solution)/shard_map/ppermute | solution.py:23
  2.5 9.7 %collective-permute-start.3 = (bf16[256,512]{1,0:T(8,128)(2,1)}, bf16[256,512]{1,0:T(8,128)(2,1)S(1)}, u32[]{:S(2)}, u32[]{:S(2)}) collective-permute-start(bf16[256,512]{1,0:T(8,128)(2,1)} %get-tuple-element.22), channel_id=1, source_target_pairs={{0,2},{1,3},{2,0},{3,1},{4,6},{5,7},{6,4},{7,5},{8,10},{9,11},{10,... | collective-permute-start | bytes 786440 | tf_op jit(solution)/shard_map/ppermute | solution.py:33
  5.1 15.3 %collective-permute-start.5 = (bf16[256,512]{1,0:T(8,128)(2,1)}, bf16[256,512]{1,0:T(8,128)(2,1)S(1)}, u32[]{:S(2)}, u32[]{:S(2)}) collective-permute-start(bf16[256,512]{1,0:T(8,128)(2,1)} %get-tuple-element.22), channel_id=1, source_target_pairs={{0,8},{1,9},{2,10},{3,11},{4,12},{5,13},{6,14},{7,15},{8,0},{9,1},... | collective-permute-start | bytes 786440 | tf_op jit(solution)/shard_map/ppermute | solution.py:33
  7.6 14.2 %collective-permute-start.2 = (bf16[256,512]{1,0:T(8,128)(2,1)}, bf16[256,512]{1,0:T(8,128)(2,1)S(1)}, u32[]{:S(2)}, u32[]{:S(2)}) collective-permute-start(bf16[256,512]{1,0:T(8,128)(2,1)} %get-tuple-element.21), channel_id=1, source_target_pairs={{0,1},{1,0},{2,3},{3,2},{4,5},{5,4},{6,7},{7,6},{8,9},{9,8},{10,11... | collective-permute-start | bytes 786440 | tf_op jit(solution)/shard_map/ppermute | solution.py:23
  8.7 1.5 %collective-permute-start.1 = (f32[14,2,512]{2,1,0:T(2,128)S(1)}, f32[14,2,512]{2,1,0:T(2,128)S(1)}, u32[]{:S(2)}, u32[]{:S(2)}) collective-permute-start(f32[14,2,512]{2,1,0:T(2,128)S(1)} %get-tuple-element.38), channel_id=1, source_target_pairs={{0,1},{1,0},{2,3},{3,2},{4,5},{5,4},{6,7},{7,6},{8,9},{9,8},{10,11... | collective-permute-start | bytes 172040 | tf_op jit(solution)/shard_map/ppermute | solution.py:23
  10.1 13.3 %collective-permute-start.9 = (bf16[256,512]{1,0:T(8,128)(2,1)}, bf16[256,512]{1,0:T(8,128)(2,1)S(1)}, u32[]{:S(2)}, u32[]{:S(2)}) collective-permute-start(bf16[256,512]{1,0:T(8,128)(2,1)} %get-tuple-element.22), channel_id=1, source_target_pairs={{0,4},{1,5},{2,6},{3,7},{4,0},{5,1},{6,2},{7,3},{8,12},{9,13},{10,... | collective-permute-start | bytes 786440 | tf_op jit(solution)/shard_map/ppermute | solution.py:33
  12.2 43.5 %copy-start.22 = (bf16[256,512]{1,0:T(8,128)(2,1)}, bf16[256,512]{1,0:T(8,128)(2,1)S(1)}, u32[]{:S(2)}) copy-start(bf16[256,512]{1,0:T(8,128)(2,1)S(1)} %collective-permute-done.3.refs_2_) | copy-start | bytes 786436
  12.2 11.7 %collective-permute-start.4 = (bf16[256,512]{1,0:T(8,128)(2,1)S(1)}, bf16[256,512]{1,0:T(8,128)(2,1)S(1)}, u32[]{:S(2)}, u32[]{:S(2)}) collective-permute-start(bf16[256,512]{1,0:T(8,128)(2,1)S(1)} %collective-permute-done.3.refs_2_), channel_id=1, source_target_pairs={{0,16},{16,0},{1,17},{17,1},{2,18},{18,2},{3,19},{19,3},{4,20},{20... | collective-permute-start | bytes 786440 | tf_op jit(solution)/shard_map/ppermute | solution.py:37
  20.3 35.4 %copy-start.23 = (bf16[256,512]{1,0:T(8,128)(2,1)}, bf16[256,512]{1,0:T(8,128)(2,1)S(1)}, u32[]{:S(2)}) copy-start(bf16[256,512]{1,0:T(8,128)(2,1)S(1)} %collective-permute-done.5.refs_4_) | copy-start | bytes 786436
  20.3 9.3 %collective-permute-start.6 = (bf16[256,512]{1,0:T(8,128)(2,1)S(1)}, bf16[256,512]{1,0:T(8,128)(2,1)}, u32[]{:S(2)}, u32[]{:S(2)}) collective-permute-start(bf16[256,512]{1,0:T(8,128)(2,1)S(1)} %collective-permute-done.5.refs_4_), channel_id=1, source_target_pairs={{0,16},{16,0},{1,17},{17,1},{2,18},{18,2},{3,19},{19,3},{4,20},{20... | collective-permute-start | bytes 786440 | tf_op jit(solution)/shard_map/ppermute | solution.py:37
  21.8 34.0 %copy-start.24 = (bf16[256,512]{1,0:T(8,128)(2,1)}, bf16[256,512]{1,0:T(8,128)(2,1)S(1)}, u32[]{:S(2)}) copy-start(bf16[256,512]{1,0:T(8,128)(2,1)S(1)} %collective-permute-done.2.refs_1_) | copy-start | bytes 786436
  21.8 8.3 %collective-permute-start.13 = (bf16[256,512]{1,0:T(8,128)(2,1)S(1)}, bf16[256,512]{1,0:T(8,128)(2,1)}, u32[]{:S(2)}, u32[]{:S(2)}) collective-permute-start(bf16[256,512]{1,0:T(8,128)(2,1)S(1)} %collective-permute-done.5.refs_4_), channel_id=1, source_target_pairs={{0,4},{1,5},{2,6},{3,7},{4,0},{5,1},{6,2},{7,3},{8,12},{9,13},{10,... | collective-permute-start | bytes 786440 | tf_op jit(solution)/shard_map/ppermute | solution.py:23
  23.4 32.4 %copy-start.25 = (bf16[256,512]{1,0:T(8,128)(2,1)}, bf16[256,512]{1,0:T(8,128)(2,1)S(1)}, u32[]{:S(2)}) copy-start(bf16[256,512]{1,0:T(8,128)(2,1)S(1)} %collective-permute-done.9.refs_8_) | copy-start | bytes 786436
  23.4 9.0 %collective-permute-start.7 = (bf16[256,512]{1,0:T(8,128)(2,1)S(1)}, bf16[256,512]{1,0:T(8,128)(2,1)}, u32[]{:S(2)}, u32[]{:S(2)}) collective-permute-start(bf16[256,512]{1,0:T(8,128)(2,1)S(1)} %collective-permute-done.5.refs_4_), channel_id=1, source_target_pairs={{0,2},{1,3},{2,0},{3,1},{4,6},{5,7},{6,4},{7,5},{8,10},{9,11},{10,... | collective-permute-start | bytes 786440 | tf_op jit(solution)/shard_map/ppermute | solution.py:23
  23.9 31.9 %copy-start.26 = (bf16[256,512]{1,0:T(8,128)(2,1)}, bf16[256,512]{1,0:T(8,128)(2,1)S(1)}, u32[]{:S(2)}) copy-start(bf16[256,512]{1,0:T(8,128)(2,1)S(1)} %collective-permute-done.4.refs_3_) | copy-start | bytes 786436
  23.9 11.3 %collective-permute-start.10 = (bf16[256,512]{1,0:T(8,128)(2,1)S(1)}, bf16[256,512]{1,0:T(8,128)(2,1)}, u32[]{:S(2)}, u32[]{:S(2)}) collective-permute-start(bf16[256,512]{1,0:T(8,128)(2,1)S(1)} %collective-permute-done.9.refs_8_), channel_id=1, source_target_pairs={{0,16},{16,0},{1,17},{17,1},{2,18},{18,2},{3,19},{19,3},{4,20},{20... | collective-permute-start | bytes 786440 | tf_op jit(solution)/shard_map/ppermute | solution.py:37
  29.6 9.3 %collective-permute-start.11 = (bf16[256,512]{1,0:T(8,128)(2,1)S(1)}, bf16[256,512]{1,0:T(8,128)(2,1)}, u32[]{:S(2)}, u32[]{:S(2)}) collective-permute-start(bf16[256,512]{1,0:T(8,128)(2,1)S(1)} %collective-permute-done.9.refs_8_), channel_id=1, source_target_pairs={{0,2},{1,3},{2,0},{3,1},{4,6},{5,7},{6,4},{7,5},{8,10},{9,11},{10,... | collective-permute-start | bytes 786440 | tf_op jit(solution)/shard_map/ppermute | solution.py:23
  30.1 10.3 %collective-permute-start.14 = (bf16[256,512]{1,0:T(8,128)(2,1)}, bf16[256,512]{1,0:T(8,128)(2,1)}, u32[]{:S(2)}, u32[]{:S(2)}) collective-permute-start(bf16[256,512]{1,0:T(8,128)(2,1)} %collective-permute-done.13.refs_12_), channel_id=1, source_target_pairs={{0,16},{16,0},{1,17},{17,1},{2,18},{18,2},{3,19},{19,3},{4,20},{20... | collective-permute-start | bytes 786440 | tf_op jit(solution)/shard_map/ppermute | solution.py:37
  32.5 20.3 %collective-permute-start.15 = (bf16[256,512]{1,0:T(8,128)(2,1)}, bf16[256,512]{1,0:T(8,128)(2,1)}, u32[]{:S(2)}, u32[]{:S(2)}) collective-permute-start(bf16[256,512]{1,0:T(8,128)(2,1)} %collective-permute-done.13.refs_12_), channel_id=1, source_target_pairs={{0,2},{1,3},{2,0},{3,1},{4,6},{5,7},{6,4},{7,5},{8,10},{9,11},{10,... | collective-permute-start | bytes 786440 | tf_op jit(solution)/shard_map/ppermute | solution.py:23
  35.2 14.9 %collective-permute-start.8 = (bf16[256,512]{1,0:T(8,128)(2,1)}, bf16[256,512]{1,0:T(8,128)(2,1)}, u32[]{:S(2)}, u32[]{:S(2)}) collective-permute-start(bf16[256,512]{1,0:T(8,128)(2,1)} %collective-permute-done.6.refs_5_), channel_id=1, source_target_pairs={{0,2},{1,3},{2,0},{3,1},{4,6},{5,7},{6,4},{7,5},{8,10},{9,11},{10,... | collective-permute-start | bytes 786440 | tf_op jit(solution)/shard_map/ppermute | solution.py:23
  38.9 11.7 %collective-permute-start.12 = (bf16[256,512]{1,0:T(8,128)(2,1)}, bf16[256,512]{1,0:T(8,128)(2,1)}, u32[]{:S(2)}, u32[]{:S(2)}) collective-permute-start(bf16[256,512]{1,0:T(8,128)(2,1)} %collective-permute-done.11.refs_10_), channel_id=1, source_target_pairs={{0,16},{16,0},{1,17},{17,1},{2,18},{18,2},{3,19},{19,3},{4,20},{20... | collective-permute-start | bytes 786440 | tf_op jit(solution)/shard_map/ppermute | solution.py:37
  40.4 15.4 %collective-permute-start.16 = (bf16[256,512]{1,0:T(8,128)(2,1)}, bf16[256,512]{1,0:T(8,128)(2,1)}, u32[]{:S(2)}, u32[]{:S(2)}) collective-permute-start(bf16[256,512]{1,0:T(8,128)(2,1)} %collective-permute-done.14.refs_13_), channel_id=1, source_target_pairs={{0,2},{1,3},{2,0},{3,1},{4,6},{5,7},{6,4},{7,5},{8,10},{9,11},{10,... | collective-permute-start | bytes 786440 | tf_op jit(solution)/shard_map/ppermute | solution.py:23
  50.1 18.4 %collective-permute-start.21 = (bf16[256,512]{1,0:T(8,128)(2,1)}, bf16[256,512]{1,0:T(8,128)(2,1)S(1)}, u32[]{:S(2)}, u32[]{:S(2)}) collective-permute-start(bf16[256,512]{1,0:T(8,128)(2,1)} %get-tuple-element.29), channel_id=1, source_target_pairs={{0,2},{1,3},{2,0},{3,1},{4,6},{5,7},{6,4},{7,5},{8,10},{9,11},{10,... | collective-permute-start | bytes 786440 | tf_op jit(solution)/shard_map/ppermute | solution.py:33
  50.6 18.9 %collective-permute-start.23 = (bf16[256,512]{1,0:T(8,128)(2,1)}, bf16[256,512]{1,0:T(8,128)(2,1)S(1)}, u32[]{:S(2)}, u32[]{:S(2)}) collective-permute-start(bf16[256,512]{1,0:T(8,128)(2,1)} %get-tuple-element.29), channel_id=1, source_target_pairs={{0,8},{1,9},{2,10},{3,11},{4,12},{5,13},{6,14},{7,15},{8,0},{9,1},... | collective-permute-start | bytes 786440 | tf_op jit(solution)/shard_map/ppermute | solution.py:33
  55.8 1.3 copy-start.2
  57.1 42.3 %copy-start.19 = (s32[16]{0:T(128)S(1)}, s32[16]{0:T(128)}, u32[]{:S(2)}) copy-start(s32[16]{0:T(128)} %get-tuple-element.35.starts) | copy-start | bytes 196
  67.4 6.6 %collective-permute-start.17 = (bf16[2,256,256]{2,1,0:T(8,128)(2,1)}, bf16[2,256,256]{2,1,0:T(8,128)(2,1)S(1)}, u32[]{:S(2)}, u32[]{:S(2)}) collective-permute-start(bf16[2,256,256]{2,1,0:T(8,128)(2,1)} %get-tuple-element.26), channel_id=1, source_target_pairs={{0,2},{1,3},{2,0},{3,1},{4,6},{5,7},{6,4},{7,5},{8,10},{9,11},{10,... | collective-permute-start | bytes 786440 | tf_op jit(solution)/shard_map/ppermute | solution.py:23
  67.9 9.4 %collective-permute-start.27 = (bf16[256,512]{1,0:T(8,128)(2,1)}, bf16[256,512]{1,0:T(8,128)(2,1)S(1)}, u32[]{:S(2)}, u32[]{:S(2)}) collective-permute-start(bf16[256,512]{1,0:T(8,128)(2,1)} %get-tuple-element.29), channel_id=1, source_target_pairs={{0,4},{1,5},{2,6},{3,7},{4,0},{5,1},{6,2},{7,3},{8,12},{9,13},{10,... | collective-permute-start | bytes 786440 | tf_op jit(solution)/shard_map/ppermute | solution.py:33
  68.5 7.4 %collective-permute-start.20 = (bf16[256,512]{1,0:T(8,128)(2,1)}, bf16[256,512]{1,0:T(8,128)(2,1)S(1)}, u32[]{:S(2)}, u32[]{:S(2)}) collective-permute-start(bf16[256,512]{1,0:T(8,128)(2,1)} %get-tuple-element.28), channel_id=1, source_target_pairs={{0,1},{1,0},{2,3},{3,2},{4,5},{5,4},{6,7},{7,6},{8,9},{9,8},{10,11... | collective-permute-start | bytes 786440 | tf_op jit(solution)/shard_map/ppermute | solution.py:23
  68.5 40.1 %copy-start.3 = (bf16[256,512]{1,0:T(8,128)(2,1)}, bf16[256,512]{1,0:T(8,128)(2,1)S(1)}, u32[]{:S(2)}) copy-start(bf16[256,512]{1,0:T(8,128)(2,1)S(1)} %collective-permute-done.21.refs_5_) | copy-start | bytes 786436
  68.5 10.0 %collective-permute-start.22 = (bf16[256,512]{1,0:T(8,128)(2,1)S(1)}, bf16[256,512]{1,0:T(8,128)(2,1)S(1)}, u32[]{:S(2)}, u32[]{:S(2)}) collective-permute-start(bf16[256,512]{1,0:T(8,128)(2,1)S(1)} %collective-permute-done.21.refs_5_), channel_id=1, source_target_pairs={{0,16},{16,0},{1,17},{17,1},{2,18},{18,2},{3,19},{19,3},{4,20},{20... | collective-permute-start | bytes 786440 | tf_op jit(solution)/shard_map/ppermute | solution.py:37
  69.5 39.0 %copy-start.4 = (bf16[256,512]{1,0:T(8,128)(2,1)}, bf16[256,512]{1,0:T(8,128)(2,1)S(1)}, u32[]{:S(2)}) copy-start(bf16[256,512]{1,0:T(8,128)(2,1)S(1)} %collective-permute-done.23.refs_7_) | copy-start | bytes 786436
  69.5 13.0 %collective-permute-start.31 = (bf16[256,512]{1,0:T(8,128)(2,1)S(1)}, bf16[256,512]{1,0:T(8,128)(2,1)S(1)}, u32[]{:S(2)}, u32[]{:S(2)}) collective-permute-start(bf16[256,512]{1,0:T(8,128)(2,1)S(1)} %collective-permute-done.23.refs_7_), channel_id=1, source_target_pairs={{0,4},{1,5},{2,6},{3,7},{4,0},{5,1},{6,2},{7,3},{8,12},{9,13},{10,... | collective-permute-start | bytes 786440 | tf_op jit(solution)/shard_map/ppermute | solution.py:23
  74.0 34.5 %copy-start = (bf16[2,256,256]{2,1,0:T(8,128)(2,1)}, bf16[2,256,256]{2,1,0:T(8,128)(2,1)S(1)}, u32[]{:S(2)}) copy-start(bf16[2,256,256]{2,1,0:T(8,128)(2,1)S(1)} %collective-permute-done.17.refs_0_) | copy-start | bytes 786436
  75.1 10.6 %collective-permute-start.18 = (bf16[2,256,256]{2,1,0:T(8,128)(2,1)S(1)}, bf16[2,256,256]{2,1,0:T(8,128)(2,1)S(1)}, u32[]{:S(2)}, u32[]{:S(2)}) collective-permute-start(bf16[2,256,256]{2,1,0:T(8,128)(2,1)S(1)} %add_convert_fusion.1), channel_id=1, source_target_pairs={{0,4},{1,5},{2,6},{3,7},{4,0},{5,1},{6,2},{7,3},{8,12},{9,13},{10,... | collective-permute-start | bytes 786440 | tf_op jit(solution)/shard_map/ppermute | solution.py:23
  75.9 32.7 %copy-start.6 = (bf16[256,512]{1,0:T(8,128)(2,1)}, bf16[256,512]{1,0:T(8,128)(2,1)S(1)}, u32[]{:S(2)}) copy-start(bf16[256,512]{1,0:T(8,128)(2,1)S(1)} %collective-permute-done.20.refs_4_) | copy-start | bytes 786436
  75.9 11.5 %collective-permute-start.24 = (bf16[256,512]{1,0:T(8,128)(2,1)S(1)}, bf16[256,512]{1,0:T(8,128)(2,1)S(1)}, u32[]{:S(2)}, u32[]{:S(2)}) collective-permute-start(bf16[256,512]{1,0:T(8,128)(2,1)S(1)} %collective-permute-done.23.refs_7_), channel_id=1, source_target_pairs={{0,16},{16,0},{1,17},{17,1},{2,18},{18,2},{3,19},{19,3},{4,20},{20... | collective-permute-start | bytes 786440 | tf_op jit(solution)/shard_map/ppermute | solution.py:37
  77.3 31.2 %copy-start.5 = (bf16[256,512]{1,0:T(8,128)(2,1)}, bf16[256,512]{1,0:T(8,128)(2,1)S(1)}, u32[]{:S(2)}) copy-start(bf16[256,512]{1,0:T(8,128)(2,1)S(1)} %collective-permute-done.27.refs_11_) | copy-start | bytes 786436
  77.4 10.3 %collective-permute-start.25 = (bf16[256,512]{1,0:T(8,128)(2,1)S(1)}, bf16[256,512]{1,0:T(8,128)(2,1)S(1)}, u32[]{:S(2)}, u32[]{:S(2)}) collective-permute-start(bf16[256,512]{1,0:T(8,128)(2,1)S(1)} %collective-permute-done.23.refs_7_), channel_id=1, source_target_pairs={{0,2},{1,3},{2,0},{3,1},{4,6},{5,7},{6,4},{7,5},{8,10},{9,11},{10,... | collective-permute-start | bytes 786440 | tf_op jit(solution)/shard_map/ppermute | solution.py:23
  78.5 30.0 %copy-start.7 = (bf16[256,512]{1,0:T(8,128)(2,1)}, bf16[256,512]{1,0:T(8,128)(2,1)S(1)}, u32[]{:S(2)}) copy-start(bf16[256,512]{1,0:T(8,128)(2,1)S(1)} %collective-permute-done.22.refs_6_) | copy-start | bytes 786436
  78.5 10.9 %collective-permute-start.28 = (bf16[256,512]{1,0:T(8,128)(2,1)S(1)}, bf16[256,512]{1,0:T(8,128)(2,1)S(1)}, u32[]{:S(2)}, u32[]{:S(2)}) collective-permute-start(bf16[256,512]{1,0:T(8,128)(2,1)S(1)} %collective-permute-done.27.refs_11_), channel_id=1, source_target_pairs={{0,16},{16,0},{1,17},{17,1},{2,18},{18,2},{3,19},{19,3},{4,20},{20... | collective-permute-start | bytes 786440 | tf_op jit(solution)/shard_map/ppermute | solution.py:37
  82.6 26.0 %copy-start.8 = (bf16[256,512]{1,0:T(8,128)(2,1)}, bf16[256,512]{1,0:T(8,128)(2,1)S(1)}, u32[]{:S(2)}) copy-start(bf16[256,512]{1,0:T(8,128)(2,1)S(1)} %collective-permute-done.31.refs_15_) | copy-start | bytes 786436
  82.6 9.6 %collective-permute-start.33 = (bf16[256,512]{1,0:T(8,128)(2,1)S(1)}, bf16[256,512]{1,0:T(8,128)(2,1)S(1)}, u32[]{:S(2)}, u32[]{:S(2)}) collective-permute-start(bf16[256,512]{1,0:T(8,128)(2,1)S(1)} %collective-permute-done.31.refs_15_), channel_id=1, source_target_pairs={{0,2},{1,3},{2,0},{3,1},{4,6},{5,7},{6,4},{7,5},{8,10},{9,11},{10,... | collective-permute-start | bytes 786440 | tf_op jit(solution)/shard_map/ppermute | solution.py:23
  85.7 22.9 %copy-start.1 = (bf16[2,256,256]{2,1,0:T(8,128)(2,1)}, bf16[2,256,256]{2,1,0:T(8,128)(2,1)S(1)}, u32[]{:S(2)}) copy-start(bf16[2,256,256]{2,1,0:T(8,128)(2,1)S(1)} %collective-permute-done.18.refs_1_) | copy-start | bytes 786436
  85.7 12.0 %collective-permute-start.29 = (bf16[256,512]{1,0:T(8,128)(2,1)S(1)}, bf16[256,512]{1,0:T(8,128)(2,1)S(1)}, u32[]{:S(2)}, u32[]{:S(2)}) collective-permute-start(bf16[256,512]{1,0:T(8,128)(2,1)S(1)} %collective-permute-done.27.refs_11_), channel_id=1, source_target_pairs={{0,2},{1,3},{2,0},{3,1},{4,6},{5,7},{6,4},{7,5},{8,10},{9,11},{10,... | collective-permute-start | bytes 786440 | tf_op jit(solution)/shard_map/ppermute | solution.py:23
  87.4 21.2 %copy-start.9 = (bf16[256,512]{1,0:T(8,128)(2,1)}, bf16[256,512]{1,0:T(8,128)(2,1)S(1)}, u32[]{:S(2)}) copy-start(bf16[256,512]{1,0:T(8,128)(2,1)S(1)} %collective-permute-done.24.refs_8_) | copy-start | bytes 786436
  87.4 14.9 %collective-permute-start.32 = (bf16[256,512]{1,0:T(8,128)(2,1)S(1)}, bf16[256,512]{1,0:T(8,128)(2,1)S(1)}, u32[]{:S(2)}, u32[]{:S(2)}) collective-permute-start(bf16[256,512]{1,0:T(8,128)(2,1)S(1)} %collective-permute-done.31.refs_15_), channel_id=1, source_target_pairs={{0,16},{16,0},{1,17},{17,1},{2,18},{18,2},{3,19},{19,3},{4,20},{20... | collective-permute-start | bytes 786440 | tf_op jit(solution)/shard_map/ppermute | solution.py:37
  87.6 21.0 %copy-start.10 = (bf16[256,512]{1,0:T(8,128)(2,1)}, bf16[256,512]{1,0:T(8,128)(2,1)S(1)}, u32[]{:S(2)}) copy-start(bf16[256,512]{1,0:T(8,128)(2,1)S(1)} %collective-permute-done.25.refs_9_) | copy-start | bytes 786436
  87.6 14.6 %collective-permute-start.26 = (bf16[256,512]{1,0:T(8,128)(2,1)S(1)}, bf16[256,512]{1,0:T(8,128)(2,1)S(1)}, u32[]{:S(2)}, u32[]{:S(2)}) collective-permute-start(bf16[256,512]{1,0:T(8,128)(2,1)S(1)} %collective-permute-done.25.refs_9_), channel_id=1, source_target_pairs={{0,16},{16,0},{1,17},{17,1},{2,18},{18,2},{3,19},{19,3},{4,20},{20... | collective-permute-start | bytes 786440 | tf_op jit(solution)/shard_map/ppermute | solution.py:37
  89.5 19.1 %copy-start.11 = (bf16[256,512]{1,0:T(8,128)(2,1)}, bf16[256,512]{1,0:T(8,128)(2,1)S(1)}, u32[]{:S(2)}) copy-start(bf16[256,512]{1,0:T(8,128)(2,1)S(1)} %collective-permute-done.28.refs_12_) | copy-start | bytes 786436
  89.5 12.8 %collective-permute-start.30 = (bf16[256,512]{1,0:T(8,128)(2,1)S(1)}, bf16[256,512]{1,0:T(8,128)(2,1)S(1)}, u32[]{:S(2)}, u32[]{:S(2)}) collective-permute-start(bf16[256,512]{1,0:T(8,128)(2,1)S(1)} %collective-permute-done.28.refs_12_), channel_id=1, source_target_pairs={{0,2},{1,3},{2,0},{3,1},{4,6},{5,7},{6,4},{7,5},{8,10},{9,11},{10,... | collective-permute-start | bytes 786440 | tf_op jit(solution)/shard_map/ppermute | solution.py:23
  92.1 16.5 %copy-start.12 = (bf16[256,512]{1,0:T(8,128)(2,1)}, bf16[256,512]{1,0:T(8,128)(2,1)S(1)}, u32[]{:S(2)}) copy-start(bf16[256,512]{1,0:T(8,128)(2,1)S(1)} %collective-permute-done.33.refs_17_) | copy-start | bytes 786436
  92.1 14.0 %collective-permute-start.34 = (bf16[256,512]{1,0:T(8,128)(2,1)S(1)}, bf16[256,512]{1,0:T(8,128)(2,1)S(1)}, u32[]{:S(2)}, u32[]{:S(2)}) collective-permute-start(bf16[256,512]{1,0:T(8,128)(2,1)S(1)} %collective-permute-done.33.refs_17_), channel_id=1, source_target_pairs={{0,16},{16,0},{1,17},{17,1},{2,18},{18,2},{3,19},{19,3},{4,20},{20... | collective-permute-start | bytes 786440 | tf_op jit(solution)/shard_map/ppermute | solution.py:37
  97.8 10.9 %copy-start.13 = (bf16[256,512]{1,0:T(8,128)(2,1)}, bf16[256,512]{1,0:T(8,128)(2,1)S(1)}, u32[]{:S(2)}) copy-start(bf16[256,512]{1,0:T(8,128)(2,1)S(1)} %collective-permute-done.29.refs_13_) | copy-start | bytes 786436
  97.8 10.1 %collective-permute-start.19 = (bf16[2,256,256]{2,1,0:T(8,128)(2,1)S(1)}, bf16[2,256,256]{2,1,0:T(8,128)(2,1)S(1)}, u32[]{:S(2)}, u32[]{:S(2)}) collective-permute-start(bf16[2,256,256]{2,1,0:T(8,128)(2,1)S(1)} %add_convert_fusion), channel_id=1, source_target_pairs={{0,8},{1,9},{2,10},{3,11},{4,12},{5,13},{6,14},{7,15},{8,0},{9,1},... | collective-permute-start | bytes 786440 | tf_op jit(solution)/shard_map/ppermute | solution.py:23
  102.2 6.4 %copy-start.15 = (bf16[256,512]{1,0:T(8,128)(2,1)}, bf16[256,512]{1,0:T(8,128)(2,1)S(1)}, u32[]{:S(2)}) copy-start(bf16[256,512]{1,0:T(8,128)(2,1)S(1)} %collective-permute-done.26.refs_10_) | copy-start | bytes 786436
  102.2 3.9 %copy-start.16 = (bf16[256,512]{1,0:T(8,128)(2,1)}, bf16[256,512]{1,0:T(8,128)(2,1)S(1)}, u32[]{:S(2)}) copy-start(bf16[256,512]{1,0:T(8,128)(2,1)S(1)} %collective-permute-done.30.refs_14_) | copy-start | bytes 786436
  102.2 6.4 %copy-start.14 = (bf16[256,512]{1,0:T(8,128)(2,1)}, bf16[256,512]{1,0:T(8,128)(2,1)S(1)}, u32[]{:S(2)}) copy-start(bf16[256,512]{1,0:T(8,128)(2,1)S(1)} %collective-permute-done.32.refs_16_) | copy-start | bytes 786436
  106.2 1.7 %copy-start.17 = (bf16[256,512]{1,0:T(8,128)(2,1)}, bf16[256,512]{1,0:T(8,128)(2,1)S(1)}, u32[]{:S(2)}) copy-start(bf16[256,512]{1,0:T(8,128)(2,1)S(1)} %collective-permute-done.34.refs_18_) | copy-start | bytes 786436
  107.8 0.7 copy-start.18
  118.8 8.6 %collective-permute-start.36 = (bf16[1024,1024]{1,0:T(8,128)(2,1)}, bf16[1024,1024]{1,0:T(8,128)(2,1)S(1)}, u32[]{:S(2)}, u32[]{:S(2)}) collective-permute-start(bf16[1024,1024]{1,0:T(8,128)(2,1)} %get-tuple-element.34.w_mine), channel_id=1, source_target_pairs={{0,1},{1,0},{2,3},{3,2},{4,5},{5,4},{6,7},{7,6},{8,9},{9,8},{10,11... | collective-permute-start | bytes 6291464 | tf_op jit(solution)/shard_map/ppermute | solution.py:23
  118.9 8.5 %collective-permute-start.35 = (bf16[512,512]{1,0:T(8,128)(2,1)}, bf16[512,512]{1,0:T(8,128)(2,1)S(1)}, u32[]{:S(2)}, u32[]{:S(2)}) collective-permute-start(bf16[512,512]{1,0:T(8,128)(2,1)} %get-tuple-element.33), channel_id=1, source_target_pairs={{0,1},{1,0},{2,3},{3,2},{4,5},{5,4},{6,7},{7,6},{8,9},{9,8},{10,11... | collective-permute-start | bytes 1572872 | tf_op jit(solution)/shard_map/ppermute | solution.py:23
  127.4 0.8 copy-start.21
  127.4 1.5 %copy-start.20 = (bf16[1024,1024]{1,0:T(8,128)(2,1)}, bf16[1024,1024]{1,0:T(8,128)(2,1)S(1)}, u32[]{:S(2)}) copy-start(bf16[1024,1024]{1,0:T(8,128)(2,1)S(1)} %collective-permute-done.36.w_theirs) | copy-start | bytes 6291460

commit v2 on v1

--- a/solution.py
+++ b/solution.py
@@ -83,16 +83,10 @@
             row += ref.shape[0]
 
 
-def row_copies(dst, refs, offset, cols, starts, rows, sem, first, base=0):
-    copies = []
-    for at, ref in enumerate(refs):
+def place_rows(dst, pieces, offset, cols, starts, base, rows):
+    for at, piece in enumerate(pieces):
         start = pl.multiple_of(starts[base + at], rows)
-        copies.append(
-            pltpu.make_async_copy(
-                ref.at[pl.ds(offset, rows), :], dst.at[pl.ds(start, rows), cols], sem.at[first + at]
-            )
-        )
-    return copies
+        dst[pl.ds(start, rows), cols] = piece[offset : offset + rows, :]
 
 
 def dot(a, b):
@@ -110,71 +104,40 @@
 def keys_values_kernel(n, rows, heads, starts, xa, xb, scale, *refs):
     del scale
     pieces = refs[:n]
-    ka, kb, va, vb, da, db, sent, wk, wv, x, sem, xsem = refs[n:]
+    ka, kb, va, vb, da, db, sent, wk, wv = refs[n:]
     everything = slice(None)
-    vcopies = row_copies(wv, pieces, 0, everything, starts, rows, sem, 0)
-    kcopies = row_copies(wk, pieces, rows, everything, starts, rows, sem, n)
-    xcopies = [pltpu.make_async_copy(src, x.at[i], xsem.at[i]) for i, src in enumerate((xa, xb))]
-    xcopies[0].start()
-    for copy in kcopies + vcopies:
-        copy.start()
-    xcopies[1].start()
-    xcopies[0].wait()
-    for copy in kcopies:
-        copy.wait()
+    place_rows(wk, pieces, rows, everything, starts, 0, rows)
+    place_rows(wv, pieces, 0, everything, starts, 0, rows)
     sums = [None] * heads
-    for i, (k_out, v_out) in enumerate(((ka, va), (kb, vb))):
-        if i:
-            xcopies[i].wait()
-        k = dot(x[i], wk[...]).astype(BF16)
+    for i, (x, k_out, v_out, device_sum) in enumerate(((xa, ka, va, da), (xb, kb, vb, db))):
+        k = dot(x[...], wk[...]).astype(BF16)
         k_out[...] = k
-        if i == 0:
-            for copy in vcopies:
-                copy.wait()
-        v = dot(x[i], wv[...]).astype(BF16)
+        v = dot(x[...], wv[...]).astype(BF16)
         v_out[...] = v
         for h in range(heads):
             cols = slice(h * HEAD, (h + 1) * HEAD)
             state = dot_outer(k[:, cols], v[:, cols])
-            (da, db)[i][h] = state.astype(BF16)
+            device_sum[h] = state.astype(BF16)
             sums[h] = state if i == 0 else sums[h] + state
     for h in range(heads):
         sent[h] = sums[h].astype(BF16)
 
 
-def attend_kernel(which, n, nb, rows, out_rows, heads, levels, local_bits, starts, x_hbm, k, v, other, scale, *refs):
+def attend_kernel(which, n, nb, rows, out_rows, heads, levels, local_bits, starts, x, k, v, other, scale, *refs):
     buckets, pieces, refs = refs[:nb], refs[nb : nb + n], refs[nb + n :]
+    out, wq = refs[0], refs[-1]
+    place_rows(wq, pieces, 0, slice(None), starts, 0, rows)
     if which:
-        out, w_out, wq, x, sem, xsem, w, wsem = refs
-    else:
-        out, wq, x, sem, xsem = refs
-    xcopy = pltpu.make_async_copy(x_hbm, x, xsem.at[0])
-    xcopy.start()
-    copies = row_copies(wq, pieces, 0, slice(None), starts, rows, sem, 0)
-    for copy in copies:
-        copy.start()
-    moves = []
-    if which:
+        w = refs[1]
         width = pieces[0].shape[1]
         for part in range(w.shape[1] // width):
-            cols_of = pl.ds(part * width, width)
-            moves += row_copies(w, pieces, rows + part * out_rows, cols_of, starts, out_rows, wsem, len(moves), n)
-        for move in moves:
-            move.start()
+            cols = slice(part * width, (part + 1) * width)
+            place_rows(w, pieces, rows + part * out_rows, cols, starts, n, out_rows)
     row = lax.broadcasted_iota(jnp.int32, (SPAN, SPAN), 0)
     col = lax.broadcasted_iota(jnp.int32, (SPAN, SPAN), 1)
     apart = row ^ col
     causal = row >= col
-    xcopy.wait()
-    for copy in copies:
-        copy.wait()
     q = dot(x[...], wq[...]).astype(BF16)
-    store = None
-    if which:
-        for move in moves:
-            move.wait()
-        store = pltpu.make_async_copy(w, w_out, xsem.at[1])
-        store.start()
     first = CBITS + local_bits + 1
     for h in range(heads):
         cols = slice(h * HEAD, (h + 1) * HEAD)
@@ -202,51 +165,44 @@
             for at, bucket in enumerate((other, *buckets)):
                 value = value + dot(qh, bucket[h]) * weight(first + at)
             out[span, cols] = value.astype(BF16)
-    if which:
-        store.wait()
-
-
-def output_kernel(width, core_ref, mine, theirs, w_mine, w_theirs, out, w, block, wsem, osem):
+
+
+def output_kernel(width, core_ref, mine, theirs, w_mine, w_theirs, out, block, sem):
     depth = mine.shape[1]
     core = core_ref[0]
     parts = w_mine.shape[1] // width
-    loads, stores = [], []
-    for side, src in enumerate((w_mine, w_theirs)):
+    low = pl.multiple_of(core * depth, depth)
+    high = pl.multiple_of((1 - core) * depth, depth)
+    stores = []
+    for side, w in enumerate((w_mine, w_theirs)):
         for part in range(parts):
             at = side * parts + part
-            loads.append(pltpu.make_async_copy(src.at[:, pl.ds(part * width, width)], w.at[at], wsem.at[at]))
-            loads[-1].start()
-    low = pl.multiple_of(core * depth, depth)
-    high = pl.multiple_of((1 - core) * depth, depth)
-    for at, load in enumerate(loads):
-        load.wait()
-        value = dot(mine[...], w[at, pl.ds(low, depth), :]) + dot(theirs[...], w[at, pl.ds(high, depth), :])
-        block[at] = value.astype(BF16)
-        half = core if at < parts else 1 - core
-        start = pl.multiple_of((half * parts + at % parts) * width, width)
-        stores.append(pltpu.make_async_copy(block.at[at], out.at[:, pl.ds(start, width)], osem.at[at]))
-        stores[-1].start()
+            cols = slice(part * width, (part + 1) * width)
+            value = dot(mine[...], w[pl.ds(low, depth), cols]) + dot(theirs[...], w[pl.ds(high, depth), cols])
+            block[at] = value.astype(BF16)
+            half = core if side == 0 else 1 - core
+            start = pl.multiple_of((half * parts + part) * width, width)
+            stores.append(pltpu.make_async_copy(block.at[at], out.at[:, pl.ds(start, width)], sem.at[at]))
+            stores[-1].start()
     for store in stores:
         store.wait()
 
 
 ANY = pl.BlockSpec(memory_space=pl.ANY)
-
-
-def whole(shape):
-    return pl.BlockSpec(shape, lambda *ids: (0,) * len(shape))
-
-
-def call(kernel, in_specs, out_specs, out_shape, scratch, flops, grid=(1,)):
+SMALL = pl.BlockSpec(memory_space=pltpu.SMEM)
+FAST = pl.BlockSpec(memory_space=pltpu.VMEM)
+
+
+def call(kernel, operands, out_specs, out_shape, scratch, flops, room=24):
     return pl.pallas_call(
         kernel,
-        grid_spec=pltpu.PrefetchScalarGridSpec(
-            num_scalar_prefetch=1, grid=grid, in_specs=in_specs, out_specs=out_specs, scratch_shapes=scratch
-        ),
+        in_specs=[SMALL] + [FAST] * (len(operands) - 1),
+        out_specs=out_specs,
         out_shape=out_shape,
-        compiler_params=pltpu.CompilerParams(dimension_semantics=("arbitrary",), vmem_limit_bytes=60 << 20),
+        scratch_shapes=scratch,
+        compiler_params=pltpu.CompilerParams(vmem_limit_bytes=room << 20),
         cost_estimate=pl.CostEstimate(flops=flops, bytes_accessed=8 << 20, transcendentals=0),
-    )
+    )(*operands)
 
 
 def on_device(tokens, w_qkv, w_out, level_weight):
@@ -298,23 +254,15 @@
     qop = gather_rows(*qo_split, zbits, 1)
 
     act = sd((toks, cols), BF16)
-    act_spec = whole((toks, cols))
-    state_spec = whole((heads, HEAD, HEAD))
     state = sd((heads, HEAD, HEAD), BF16)
     ka, kb, va, vb, da, db, total = call(
         functools.partial(keys_values_kernel, len(kvp), rows, heads),
-        [ANY] * (3 + len(kvp)),
-        [act_spec] * 4 + [state_spec] * 3,
+        [first_rows(kvp, rows, device, sent_core), tokens, far_tokens, scale, *(piece[0] for piece in kvp)],
+        [FAST] * 7,
         [act] * 4 + [state] * 3,
-        [
-            pltpu.VMEM((width, cols), BF16),
-            pltpu.VMEM((width, cols), BF16),
-            pltpu.VMEM((2, toks, width), BF16),
-            pltpu.SemaphoreType.DMA((2 * len(kvp),)),
-            pltpu.SemaphoreType.DMA((2,)),
-        ],
+        [pltpu.VMEM((width, cols), BF16), pltpu.VMEM((width, cols), BF16)],
         2 * 2 * toks * width * 2 * cols,
-    )(first_rows(kvp, rows, device, sent_core), tokens, far_tokens, scale, *(piece[0] for piece in kvp))
+    )
 
     buckets = []
     for bit in range(1, seq_bits):
@@ -322,33 +270,21 @@
         buckets.append(arrived)
         total = (total.astype(F32) + arrived.astype(F32)).astype(BF16)
 
+    starts = jnp.concatenate(
+        [first_rows(qop, rows, device, sent_core), first_rows(qop, out_rows, device, sent_core)]
+    )
+
     def attend(which, x, k, v, other):
-        specs, shapes = [act_spec], [act]
-        scratch = [
-            pltpu.VMEM((width, cols), BF16),
-            pltpu.VMEM((toks, width), BF16),
-            pltpu.SemaphoreType.DMA((len(qop),)),
-            pltpu.SemaphoreType.DMA((2,)),
-        ]
-        if which:
-            specs.append(ANY)
-            shapes.append(sd((head_cols, out_cols), BF16))
-            scratch += [pltpu.VMEM((head_cols, out_cols), BF16), pltpu.SemaphoreType.DMA((out_parts * len(qop),))]
+        shapes = [act] + [sd((head_cols, out_cols), BF16)] * which
         return call(
             functools.partial(
                 attend_kernel, which, len(qop), len(buckets), rows, out_rows, heads, levels, local_bits
             ),
-            [ANY] + [act_spec] * 2 + [state_spec] + [whole(scale.shape)] + [state_spec] * len(buckets)
-            + [ANY] * len(qop),
-            specs,
+            [starts, x, k, v, other, scale, *buckets, *(piece[0] for piece in qop)],
+            [FAST] * len(shapes),
             shapes,
-            scratch,
+            [pltpu.VMEM((width, cols), BF16)],
             2 * toks * width * cols,
-        )(
-            jnp.concatenate(
-                [first_rows(qop, rows, device, sent_core), first_rows(qop, out_rows, device, sent_core)]
-            ),
-            x, k, v, other, scale, *buckets, *(piece[0] for piece in qop),
         )
 
     far_part, w_mine = attend(1, far_tokens, kb, vb, da)
@@ -358,17 +294,12 @@
     n_blocks = CORES * out_parts
     return call(
         functools.partial(output_kernel, cols),
-        [act_spec, act_spec, ANY, ANY],
+        [core.reshape(1).astype(jnp.int32), mine, theirs, w_mine, w_theirs],
         ANY,
         sd((toks, out_width), BF16),
-        [
-            pltpu.VMEM((n_blocks, head_cols, cols), BF16),
-            pltpu.VMEM((n_blocks, toks, cols), BF16),
-            pltpu.SemaphoreType.DMA((n_blocks,)),
-            pltpu.SemaphoreType.DMA((n_blocks,)),
-        ],
+        [pltpu.VMEM((n_blocks, toks, cols), BF16), pltpu.SemaphoreType.DMA((n_blocks,))],
         2 * toks * head_cols * out_width,
-    )(core.reshape(1).astype(jnp.int32), mine, theirs, w_mine, w_theirs)
+    )
 
 
 def solution(mesh):

time: 136 us -> 120 us (0.88); the launches traced: 135 us -> 117 us
  Pallas kernels: 38.7 us -> 22.8 us
  local copies, waits for them, and re-layouts: 5.66 us -> 3.23 us
  other arithmetic: 3.89 us -> 1.85 us
  starting transfers between devices: 37.1 us -> 38.8 us
    pallas_call x4, Pallas kernels: 34.5 us -> 18.5 us  [call(): pl.pallas_call(kernel, in_specs=[SMALL] + [FAST] * (len(operands) - 1), o...]
    ppermute x11, waiting for transfers between devices: 11.9 us -> 15.4 us  [swap_x(): lax.ppermute(value, 'group', [(i, i ^ 1) for i in range(lax.axis_size('gr...]
    ppermute x20, waiting for transfers between devices: 29.2 us -> 27.1 us  [swap(): lax.ppermute(value, 'seq', [(i, i ^ mask) for i in range(lax.axis_size('s...]
    ppermute x11, starting transfers between devices: 11.3 us -> 13 us  [swap_x(): lax.ppermute(value, 'group', [(i, i ^ 1) for i in range(lax.axis_size('gr...]
    unnamed x54 -> x18, local copies, waits for them, and re-layouts: 3.54 us -> 1.92 us
  transfers between devices with their start and end apart: 37 -> 37, of which waited for: 17 -> 19; matrix products, arithmetic and copies ran while one was open for 4% -> 3% of each run, Pallas kernels for 17% -> 13%
where the time goes in v2:
time: 120 us; the launch traced here: 117 us
  waiting for transfers between devices  50.6 us (42%)
  starting transfers between devices  38.8 us (32%)
  Pallas kernels  22.8 us (19%)
  local copies, waits for them, and re-layouts  3.23 us (3%)
  other arithmetic  1.85 us (2%)
    ppermute x20, waiting for transfers between devices, swap(): lax.ppermute(value, 'seq', [(i, i ^ mask) for i in range(lax.axis_size('s...  27.1 us
    pallas_call x4, Pallas kernels, call(): pl.pallas_call(kernel, in_specs=[SMALL] + [FAST] * (len(operands) - 1), o...  18.5 us
    ppermute x11, waiting for transfers between devices, swap_x(): lax.ppermute(value, 'group', [(i, i ^ 1) for i in range(lax.axis_size('gr...  15.4 us
    ppermute x20, starting transfers between devices, swap(): lax.ppermute(value, 'seq', [(i, i ^ mask) for i in range(lax.axis_size('s...  15.4 us
    ppermute x11, starting transfers between devices, swap_x(): lax.ppermute(value, 'group', [(i, i ^ 1) for i in range(lax.axis_size('gr...  13 us
    ppermute x6, starting transfers between devices, swap_crossed(): return lax.ppermute(value, ('group', 'seq'), pairs)  10.3 us
    ppermute x6, waiting for transfers between devices, swap_crossed(): return lax.ppermute(value, ('group', 'seq'), pairs)  8.02 us
    pallas_call x2, Pallas kernels, split(): pl.pallas_call(functools.partial(split_kernel, parts, cols), out_shape=[s...  4.33 us
  transfers between devices with their start and end apart: 37, of which 19 were waited for; matrix products, arithmetic and copies ran while one was open for 3% of the time, Pallas kernels for 13%

profile of v2, /device:TPU:0, one launch (start us, length us, event | category | flops | bytes accessed | tf_op | source)
XLA Modules:
  0.0 117.4 jit_solution(12426851201716931280)
XLA Ops:
  0.0 0.5 collective-permute-start
  0.5 2.2 %shard_map.127 = (bf16[256,512]{1,0:T(8,128)(2,1)}, bf16[256,512]{1,0:T(8,128)(2,1)}, bf16[256,512]{1,0:T(8,128)(2,1)}) custom-call(bf16[128,3072]{1,0:T(8,128)(2,1)} %refs_0_.3), custom_call_target="tpu_custom_call" | custom-call | flops 1048576 | bytes 2097152 | tf_op jit(solution)/shard_map/pallas_call | solution.py:228
  2.7 2.5 %collective-permute-start.3 = (bf16[256,512]{1,0:T(8,128)(2,1)}, bf16[256,512]{1,0:T(8,128)(2,1)S(1)}, u32[]{:S(2)}, u32[]{:S(2)}) collective-permute-start(bf16[256,512]{1,0:T(8,128)(2,1)} %get-tuple-element.22), channel_id=1, source_target_pairs={{0,2},{1,3},{2,0},{3,1},{4,6},{5,7},{6,4},{7,5},{8,10},{9,11},{10,... | collective-permute-start | bytes 786440 | tf_op jit(solution)/shard_map/ppermute | solution.py:33
  5.2 2.6 %collective-permute-start.5 = (bf16[256,512]{1,0:T(8,128)(2,1)}, bf16[256,512]{1,0:T(8,128)(2,1)S(1)}, u32[]{:S(2)}, u32[]{:S(2)}) collective-permute-start(bf16[256,512]{1,0:T(8,128)(2,1)} %get-tuple-element.22), channel_id=1, source_target_pairs={{0,8},{1,9},{2,10},{3,11},{4,12},{5,13},{6,14},{7,15},{8,0},{9,1},... | collective-permute-start | bytes 786440 | tf_op jit(solution)/shard_map/ppermute | solution.py:33
  7.8 1.0 dynamic-slice_bitcast_fusion
  8.8 0.6 collective-permute-start.1
  9.4 0.9 collective-permute-done.1
  10.3 1.6 %collective-permute-start.9 = (bf16[256,512]{1,0:T(8,128)(2,1)}, bf16[256,512]{1,0:T(8,128)(2,1)S(1)}, u32[]{:S(2)}, u32[]{:S(2)}) collective-permute-start(bf16[256,512]{1,0:T(8,128)(2,1)} %get-tuple-element.22), channel_id=1, source_target_pairs={{0,4},{1,5},{2,6},{3,7},{4,0},{5,1},{6,2},{7,3},{8,12},{9,13},{10,... | collective-permute-start | bytes 786440 | tf_op jit(solution)/shard_map/ppermute | solution.py:33
  11.9 0.4 collective-permute-done.3.refs_2_
  12.2 1.2 %collective-permute-start.4 = (bf16[256,512]{1,0:T(8,128)(2,1)S(1)}, bf16[256,512]{1,0:T(8,128)(2,1)}, u32[]{:S(2)}, u32[]{:S(2)}) collective-permute-start(bf16[256,512]{1,0:T(8,128)(2,1)S(1)} %collective-permute-done.3.refs_2_), channel_id=1, source_target_pairs={{0,16},{16,0},{1,17},{17,1},{2,18},{18,2},{3,19},{19,3},{4,20},{20... | collective-permute-start | bytes 786440 | tf_op jit(solution)/shard_map/ppermute | solution.py:37
  13.4 6.9 %collective-permute-done.5.refs_4_ = bf16[256,512]{1,0:T(8,128)(2,1)S(1)} collective-permute-done((bf16[256,512]{1,0:T(8,128)(2,1)}, bf16[256,512]{1,0:T(8,128)(2,1)S(1)}, u32[]{:S(2)}, u32[]{:S(2)}) %collective-permute-start.5) | collective-permute-done | bytes 262176 | tf_op jit(solution)/shard_map/ppermute | solution.py:33
  20.3 1.4 %collective-permute-start.6 = (bf16[256,512]{1,0:T(8,128)(2,1)S(1)}, bf16[256,512]{1,0:T(8,128)(2,1)}, u32[]{:S(2)}, u32[]{:S(2)}) collective-permute-start(bf16[256,512]{1,0:T(8,128)(2,1)S(1)} %collective-permute-done.5.refs_4_), channel_id=1, source_target_pairs={{0,16},{16,0},{1,17},{17,1},{2,18},{18,2},{3,19},{19,3},{4,20},{20... | collective-permute-start | bytes 786440 | tf_op jit(solution)/shard_map/ppermute | solution.py:37
  21.8 1.1 collective-permute-start.13
  22.8 0.8 collective-permute-done.9.refs_8_
  23.6 0.5 collective-permute-start.7
  24.0 1.2 collective-permute-start.10
  25.2 4.4 %collective-permute-done.6.refs_5_ = bf16[256,512]{1,0:T(8,128)(2,1)} collective-permute-done((bf16[256,512]{1,0:T(8,128)(2,1)S(1)}, bf16[256,512]{1,0:T(8,128)(2,1)}, u32[]{:S(2)}, u32[]{:S(2)}) %collective-permute-start.6) | collective-permute-done | bytes 262176 | tf_op jit(solution)/shard_map/ppermute | solution.py:37
  29.7 0.3 collective-permute-done.13.refs_12_
  30.0 1.5 %collective-permute-start.14 = (bf16[256,512]{1,0:T(8,128)(2,1)}, bf16[256,512]{1,0:T(8,128)(2,1)}, u32[]{:S(2)}, u32[]{:S(2)}) collective-permute-start(bf16[256,512]{1,0:T(8,128)(2,1)} %collective-permute-done.13.refs_12_), channel_id=1, source_target_pairs={{0,16},{16,0},{1,17},{17,1},{2,18},{18,2},{3,19},{19,3},{4,20},{20... | collective-permute-start | bytes 786440 | tf_op jit(solution)/shard_map/ppermute | solution.py:37
  31.5 0.8 convert_multiply_fusion
  32.3 0.3 collective-permute-done.7.refs_6_
  32.6 1.3 %collective-permute-start.15 = (bf16[256,512]{1,0:T(8,128)(2,1)}, bf16[256,512]{1,0:T(8,128)(2,1)}, u32[]{:S(2)}, u32[]{:S(2)}) collective-permute-start(bf16[256,512]{1,0:T(8,128)(2,1)} %collective-permute-done.13.refs_12_), channel_id=1, source_target_pairs={{0,2},{1,3},{2,0},{3,1},{4,6},{5,7},{6,4},{7,5},{8,10},{9,11},{10,... | collective-permute-start | bytes 786440 | tf_op jit(solution)/shard_map/ppermute | solution.py:23
  33.9 1.3 %collective-permute-done.10.refs_9_ = bf16[256,512]{1,0:T(8,128)(2,1)} collective-permute-done((bf16[256,512]{1,0:T(8,128)(2,1)S(1)}, bf16[256,512]{1,0:T(8,128)(2,1)}, u32[]{:S(2)}, u32[]{:S(2)}) %collective-permute-start.10) | collective-permute-done | bytes 262176 | tf_op jit(solution)/shard_map/ppermute | solution.py:37
  35.3 3.6 %collective-permute-done.11.refs_10_ = bf16[256,512]{1,0:T(8,128)(2,1)} collective-permute-done((bf16[256,512]{1,0:T(8,128)(2,1)S(1)}, bf16[256,512]{1,0:T(8,128)(2,1)}, u32[]{:S(2)}, u32[]{:S(2)}) %collective-permute-start.11) | collective-permute-done | bytes 262176 | tf_op jit(solution)/shard_map/ppermute | solution.py:23
  38.9 1.4 %collective-permute-start.12 = (bf16[256,512]{1,0:T(8,128)(2,1)}, bf16[256,512]{1,0:T(8,128)(2,1)}, u32[]{:S(2)}, u32[]{:S(2)}) collective-permute-start(bf16[256,512]{1,0:T(8,128)(2,1)} %collective-permute-done.11.refs_10_), channel_id=1, source_target_pairs={{0,16},{16,0},{1,17},{17,1},{2,18},{18,2},{3,19},{19,3},{4,20},{20... | collective-permute-start | bytes 786440 | tf_op jit(solution)/shard_map/ppermute | solution.py:37
  40.3 0.4 collective-permute-start.16
  40.7 0.7 broadcast_multiply_fusion.1
  41.4 2.1 %shard_map.129 = (bf16[256,512]{1,0:T(8,128)(2,1)}, bf16[256,512]{1,0:T(8,128)(2,1)}, bf16[256,512]{1,0:T(8,128)(2,1)}) custom-call(bf16[128,3072]{1,0:T(8,128)(2,1)} %refs_0_.3, bf16[64,2048]{1,0:T(8,128)(2,1)} %refs_1_.1), custom_call_target="tpu_custom_call" | custom-call | flops 1048576 | bytes 2097152 | tf_op jit(solution)/shard_map/pallas_call | solution.py:228
  43.6 0.1 fusion
  43.8 0.2 copy.16.scale
  44.0 6.2 %collective-permute-done.8.refs_7_ = bf16[256,512]{1,0:T(8,128)(2,1)} collective-permute-done((bf16[256,512]{1,0:T(8,128)(2,1)}, bf16[256,512]{1,0:T(8,128)(2,1)}, u32[]{:S(2)}, u32[]{:S(2)}) %collective-permute-start.8) | collective-permute-done | bytes 262176 | tf_op jit(solution)/shard_map/ppermute | solution.py:23
  50.2 2.6 %collective-permute-start.23 = (bf16[256,512]{1,0:T(8,128)(2,1)}, bf16[256,512]{1,0:T(8,128)(2,1)S(1)}, u32[]{:S(2)}, u32[]{:S(2)}) collective-permute-start(bf16[256,512]{1,0:T(8,128)(2,1)} %get-tuple-element.29), channel_id=1, source_target_pairs={{0,8},{1,9},{2,10},{3,11},{4,12},{5,13},{6,14},{7,15},{8,0},{9,1},... | collective-permute-start | bytes 786440 | tf_op jit(solution)/shard_map/ppermute | solution.py:33
  52.8 3.0 %collective-permute-done.16.refs_15_ = bf16[256,512]{1,0:T(8,128)(2,1)} collective-permute-done((bf16[256,512]{1,0:T(8,128)(2,1)}, bf16[256,512]{1,0:T(8,128)(2,1)}, u32[]{:S(2)}, u32[]{:S(2)}) %collective-permute-start.16) | collective-permute-done | bytes 262176 | tf_op jit(solution)/shard_map/ppermute | solution.py:23
  55.8 0.9 copy-done.4
  56.7 0.9 copy-done.6
  57.7 7.6 %shard_map.128 = (bf16[512,512]{1,0:T(8,128)(2,1)S(1)}, bf16[512,512]{1,0:T(8,128)(2,1)S(1)}, bf16[512,512]{1,0:T(8,128)(2,1)S(1)}, bf16[512,512]{1,0:T(8,128)(2...) custom-call(s32[16]{0:T(128)S(1)} %get-tuple-element.35.starts, ...), custom_call_target="tpu_custom_call" | custom-call | flops 4294967296 | bytes 8388608 | tf_op jit(solution)/shard_map/pallas_call | solution.py:197
  65.3 0.1 collective-permute-start.17
  65.4 1.0 collective-permute-start.27
  66.4 0.9 collective-permute-start.22
  67.4 1.9 %collective-permute-start.31 = (bf16[256,512]{1,0:T(8,128)(2,1)S(1)}, bf16[256,512]{1,0:T(8,128)(2,1)S(1)}, u32[]{:S(2)}, u32[]{:S(2)}) collective-permute-start(bf16[256,512]{1,0:T(8,128)(2,1)S(1)} %collective-permute-done.23.refs_7_), channel_id=1, source_target_pairs={{0,4},{1,5},{2,6},{3,7},{4,0},{5,1},{6,2},{7,3},{8,12},{9,13},{10,... | collective-permute-start | bytes 786440 | tf_op jit(solution)/shard_map/ppermute | solution.py:23
  69.3 2.4 %collective-permute-done.17.refs_0_ = bf16[2,256,256]{2,1,0:T(8,128)(2,1)S(1)} collective-permute-done((bf16[2,256,256]{2,1,0:T(8,128)(2,1)S(1)}, bf16[2,256,256]{2,1,0:T(8,128)(2,1)S(1)}, u32[]{:S(2)}, u32[]{:S(2)}) %collective-permute-start.17) | collective-permute-done | bytes 262176 | tf_op jit(solution)/shard_map/ppermute | solution.py:23
  71.8 0.8 collective-permute-start.18
  72.5 1.4 %collective-permute-start.24 = (bf16[256,512]{1,0:T(8,128)(2,1)S(1)}, bf16[256,512]{1,0:T(8,128)(2,1)S(1)}, u32[]{:S(2)}, u32[]{:S(2)}) collective-permute-start(bf16[256,512]{1,0:T(8,128)(2,1)S(1)} %collective-permute-done.23.refs_7_), channel_id=1, source_target_pairs={{0,16},{16,0},{1,17},{17,1},{2,18},{18,2},{3,19},{19,3},{4,20},{20... | collective-permute-start | bytes 786440 | tf_op jit(solution)/shard_map/ppermute | solution.py:37
  74.0 1.8 %collective-permute-start.25 = (bf16[256,512]{1,0:T(8,128)(2,1)S(1)}, bf16[256,512]{1,0:T(8,128)(2,1)S(1)}, u32[]{:S(2)}, u32[]{:S(2)}) collective-permute-start(bf16[256,512]{1,0:T(8,128)(2,1)S(1)} %collective-permute-done.23.refs_7_), channel_id=1, source_target_pairs={{0,2},{1,3},{2,0},{3,1},{4,6},{5,7},{6,4},{7,5},{8,10},{9,11},{10,... | collective-permute-start | bytes 786440 | tf_op jit(solution)/shard_map/ppermute | solution.py:23
  75.8 1.6 %collective-permute-start.28 = (bf16[256,512]{1,0:T(8,128)(2,1)S(1)}, bf16[256,512]{1,0:T(8,128)(2,1)S(1)}, u32[]{:S(2)}, u32[]{:S(2)}) collective-permute-start(bf16[256,512]{1,0:T(8,128)(2,1)S(1)} %collective-permute-done.27.refs_11_), channel_id=1, source_target_pairs={{0,16},{16,0},{1,17},{17,1},{2,18},{18,2},{3,19},{19,3},{4,20},{20... | collective-permute-start | bytes 786440 | tf_op jit(solution)/shard_map/ppermute | solution.py:37
  77.4 1.8 %collective-permute-done.31.refs_15_ = bf16[256,512]{1,0:T(8,128)(2,1)S(1)} collective-permute-done((bf16[256,512]{1,0:T(8,128)(2,1)S(1)}, bf16[256,512]{1,0:T(8,128)(2,1)S(1)}, u32[]{:S(2)}, u32[]{:S(2)}) %collective-permute-start.31) | collective-permute-done | bytes 262176 | tf_op jit(solution)/shard_map/ppermute | solution.py:23
  79.2 2.2 %collective-permute-start.33 = (bf16[256,512]{1,0:T(8,128)(2,1)S(1)}, bf16[256,512]{1,0:T(8,128)(2,1)S(1)}, u32[]{:S(2)}, u32[]{:S(2)}) collective-permute-start(bf16[256,512]{1,0:T(8,128)(2,1)S(1)} %collective-permute-done.31.refs_15_), channel_id=1, source_target_pairs={{0,2},{1,3},{2,0},{3,1},{4,6},{5,7},{6,4},{7,5},{8,10},{9,11},{10,... | collective-permute-start | bytes 786440 | tf_op jit(solution)/shard_map/ppermute | solution.py:23
  81.4 1.6 %collective-permute-done.18.refs_1_ = bf16[2,256,256]{2,1,0:T(8,128)(2,1)S(1)} collective-permute-done((bf16[2,256,256]{2,1,0:T(8,128)(2,1)S(1)}, bf16[2,256,256]{2,1,0:T(8,128)(2,1)S(1)}, u32[]{:S(2)}, u32[]{:S(2)}) %collective-permute-start.18) | collective-permute-done | bytes 262176 | tf_op jit(solution)/shard_map/ppermute | solution.py:23
  83.0 1.9 %collective-permute-start.29 = (bf16[256,512]{1,0:T(8,128)(2,1)S(1)}, bf16[256,512]{1,0:T(8,128)(2,1)S(1)}, u32[]{:S(2)}, u32[]{:S(2)}) collective-permute-start(bf16[256,512]{1,0:T(8,128)(2,1)S(1)} %collective-permute-done.27.refs_11_), channel_id=1, source_target_pairs={{0,2},{1,3},{2,0},{3,1},{4,6},{5,7},{6,4},{7,5},{8,10},{9,11},{10,... | collective-permute-start | bytes 786440 | tf_op jit(solution)/shard_map/ppermute | solution.py:23
  85.1 0.5 collective-permute-start.32
  85.6 1.6 %collective-permute-start.26 = (bf16[256,512]{1,0:T(8,128)(2,1)S(1)}, bf16[256,512]{1,0:T(8,128)(2,1)S(1)}, u32[]{:S(2)}, u32[]{:S(2)}) collective-permute-start(bf16[256,512]{1,0:T(8,128)(2,1)S(1)} %collective-permute-done.25.refs_9_), channel_id=1, source_target_pairs={{0,16},{16,0},{1,17},{17,1},{2,18},{18,2},{3,19},{19,3},{4,20},{20... | collective-permute-start | bytes 786440 | tf_op jit(solution)/shard_map/ppermute | solution.py:37
  87.2 0.9 collective-permute-start.30
  88.0 0.6 collective-permute-done.33.refs_17_
  88.6 0.2 collective-permute-start.34
  88.8 5.4 %collective-permute-done.29.refs_13_ = bf16[256,512]{1,0:T(8,128)(2,1)S(1)} collective-permute-done((bf16[256,512]{1,0:T(8,128)(2,1)S(1)}, bf16[256,512]{1,0:T(8,128)(2,1)S(1)}, u32[]{:S(2)}, u32[]{:S(2)}) %collective-permute-start.29) | collective-permute-done | bytes 262176 | tf_op jit(solution)/shard_map/ppermute | solution.py:23
  94.2 0.8 collective-permute-start.19
  95.0 0.1 pad_add_fusion.starts
  95.0 4.9 %collective-permute-done.26.refs_10_ = bf16[256,512]{1,0:T(8,128)(2,1)S(1)} collective-permute-done((bf16[256,512]{1,0:T(8,128)(2,1)S(1)}, bf16[256,512]{1,0:T(8,128)(2,1)S(1)}, u32[]{:S(2)}, u32[]{:S(2)}) %collective-permute-start.26) | collective-permute-done | bytes 262176 | tf_op jit(solution)/shard_map/ppermute | solution.py:37
  99.9 4.8 %collective-permute-done.34.refs_18_ = bf16[256,512]{1,0:T(8,128)(2,1)S(1)} collective-permute-done((bf16[256,512]{1,0:T(8,128)(2,1)S(1)}, bf16[256,512]{1,0:T(8,128)(2,1)S(1)}, u32[]{:S(2)}, u32[]{:S(2)}) %collective-permute-start.34) | collective-permute-done | bytes 262176 | tf_op jit(solution)/shard_map/ppermute | solution.py:37
  104.7 4.5 %shard_map.131 = (bf16[512,512]{1,0:T(8,128)(2,1)S(1)}, bf16[1024,1024]{1,0:T(8,128)(2,1)S(1)}) custom-call(s32[32]{0:T(128)S(1)} %pad_add_fusion.starts, bf16[512,2048]{1,0:T(8,128)(2,1)} %collective-permute-done.xb.x, bf16[512,512]{1,0:T(8,128)(2,1)S(1)} %get-tuple-element.30.k, bf16[512,512]{1,0:T(8,128)(2,1)S(1)} %get-tuple-element.31.v, ...), custom_call_target="tpu_custom_call" | custom-call | flops 1073741824 | bytes 8388608 | tf_op jit(solution)/shard_map/pallas_call | solution.py:197
  109.3 0.5 collective-permute-start.35
  109.8 3.3 %shard_map.130.mine = bf16[512,512]{1,0:T(8,128)(2,1)S(1)} custom-call(s32[32]{0:T(128)S(1)} %pad_add_fusion.starts, bf16[512,2048]{1,0:T(8,128)(2,1)S(1)} %copy-done, bf16[512,512]{1,0:T(8,128)(2,1)S(1)} %get-tuple-element.23.k, bf16[512,512]{1,0:T(8,128)(2,1)S(1)} %get-tuple-element.24.v, bf16[2,256,256]{2,1,0:T(8,128)(2,1)S(1)} %get-tuple-element.25.other, ...), custom_call_target="tpu_custom_call" | custom-call | flops 1073741824 | bytes 8388608 | tf_op jit(solution)/shard_map/pallas_call | solution.py:197
  113.0 1.1 collective-permute-done.35.theirs
  114.2 3.2 %shard_map.132 = bf16[512,2048]{1,0:T(8,128)(2,1)} custom-call(s32[1]{0:T(128)} %bitcast.core_ref, bf16[512,512]{1,0:T(8,128)(2,1)S(1)} %shard_map.130.mine, bf16[512,512]{1,0:T(8,128)(2,1)S(1)} %collective-permute-done.35.theirs, bf16[1024,1024]{1,0:T(8,128)(2,1)S(1)} %get-tuple-element.34.w_mine, bf16[1024,1024]{1,0:T(8,128)(2,1)S(1)} %collective-permute-done.36.w_theirs), custom_call_target="tpu_custom_call" | custom-call | flops 2147483648 | bytes 8388608 | tf_op jit(solution)/shard_map/pallas_call | solution.py:197
  (45 shorter events, 0.6 us)
Async XLA Ops:
  0.0 55.8 %copy-start = (bf16[512,2048]{1,0:T(8,128)(2,1)S(1)}, bf16[512,2048]{1,0:T(8,128)(2,1)}, u32[]{:S(2)}) copy-start(bf16[512,2048]{1,0:T(8,128)(2,1)} %x.1) | copy-start | bytes 6291460
  0.0 55.8 %collective-permute-start = (bf16[512,2048]{1,0:T(8,128)(2,1)}, bf16[512,2048]{1,0:T(8,128)(2,1)}, u32[]{:S(2)}, u32[]{:S(2)}) collective-permute-start(bf16[512,2048]{1,0:T(8,128)(2,1)} %x.1), channel_id=1, source_target_pairs={{0,1},{1,0},{2,3},{3,2},{4,5},{5,4},{6,7},{7,6},{8,9},{9,8},{10,11... | collective-permute-start | bytes 6291464 | tf_op jit(solution)/shard_map/ppermute | solution.py:23
  2.7 53.1 %copy-start.2 = (bf16[256,512]{1,0:T(8,128)(2,1)S(1)}, bf16[256,512]{1,0:T(8,128)(2,1)}, u32[]{:S(2)}) copy-start(bf16[256,512]{1,0:T(8,128)(2,1)} %get-tuple-element.20.refs_0_) | copy-start | bytes 786436
  2.7 9.6 %collective-permute-start.3 = (bf16[256,512]{1,0:T(8,128)(2,1)}, bf16[256,512]{1,0:T(8,128)(2,1)S(1)}, u32[]{:S(2)}, u32[]{:S(2)}) collective-permute-start(bf16[256,512]{1,0:T(8,128)(2,1)} %get-tuple-element.22), channel_id=1, source_target_pairs={{0,2},{1,3},{2,0},{3,1},{4,6},{5,7},{6,4},{7,5},{8,10},{9,11},{10,... | collective-permute-start | bytes 786440 | tf_op jit(solution)/shard_map/ppermute | solution.py:33
  5.2 15.1 %collective-permute-start.5 = (bf16[256,512]{1,0:T(8,128)(2,1)}, bf16[256,512]{1,0:T(8,128)(2,1)S(1)}, u32[]{:S(2)}, u32[]{:S(2)}) collective-permute-start(bf16[256,512]{1,0:T(8,128)(2,1)} %get-tuple-element.22), channel_id=1, source_target_pairs={{0,8},{1,9},{2,10},{3,11},{4,12},{5,13},{6,14},{7,15},{8,0},{9,1},... | collective-permute-start | bytes 786440 | tf_op jit(solution)/shard_map/ppermute | solution.py:33
  7.8 14.0 %collective-permute-start.2 = (bf16[256,512]{1,0:T(8,128)(2,1)}, bf16[256,512]{1,0:T(8,128)(2,1)S(1)}, u32[]{:S(2)}, u32[]{:S(2)}) collective-permute-start(bf16[256,512]{1,0:T(8,128)(2,1)} %get-tuple-element.21), channel_id=1, source_target_pairs={{0,1},{1,0},{2,3},{3,2},{4,5},{5,4},{6,7},{7,6},{8,9},{9,8},{10,11... | collective-permute-start | bytes 786440 | tf_op jit(solution)/shard_map/ppermute | solution.py:23
  8.8 1.5 %collective-permute-start.1 = (f32[14,2,512]{2,1,0:T(2,128)S(1)}, f32[14,2,512]{2,1,0:T(2,128)S(1)}, u32[]{:S(2)}, u32[]{:S(2)}) collective-permute-start(f32[14,2,512]{2,1,0:T(2,128)S(1)} %get-tuple-element.38), channel_id=1, source_target_pairs={{0,1},{1,0},{2,3},{3,2},{4,5},{5,4},{6,7},{7,6},{8,9},{9,8},{10,11... | collective-permute-start | bytes 172040 | tf_op jit(solution)/shard_map/ppermute | solution.py:23
  10.3 13.3 %collective-permute-start.9 = (bf16[256,512]{1,0:T(8,128)(2,1)}, bf16[256,512]{1,0:T(8,128)(2,1)S(1)}, u32[]{:S(2)}, u32[]{:S(2)}) collective-permute-start(bf16[256,512]{1,0:T(8,128)(2,1)} %get-tuple-element.22), channel_id=1, source_target_pairs={{0,4},{1,5},{2,6},{3,7},{4,0},{5,1},{6,2},{7,3},{8,12},{9,13},{10,... | collective-permute-start | bytes 786440 | tf_op jit(solution)/shard_map/ppermute | solution.py:33
  12.2 11.8 %collective-permute-start.4 = (bf16[256,512]{1,0:T(8,128)(2,1)S(1)}, bf16[256,512]{1,0:T(8,128)(2,1)}, u32[]{:S(2)}, u32[]{:S(2)}) collective-permute-start(bf16[256,512]{1,0:T(8,128)(2,1)S(1)} %collective-permute-done.3.refs_2_), channel_id=1, source_target_pairs={{0,16},{16,0},{1,17},{17,1},{2,18},{18,2},{3,19},{19,3},{4,20},{20... | collective-permute-start | bytes 786440 | tf_op jit(solution)/shard_map/ppermute | solution.py:37
  20.3 9.3 %collective-permute-start.6 = (bf16[256,512]{1,0:T(8,128)(2,1)S(1)}, bf16[256,512]{1,0:T(8,128)(2,1)}, u32[]{:S(2)}, u32[]{:S(2)}) collective-permute-start(bf16[256,512]{1,0:T(8,128)(2,1)S(1)} %collective-permute-done.5.refs_4_), channel_id=1, source_target_pairs={{0,16},{16,0},{1,17},{17,1},{2,18},{18,2},{3,19},{19,3},{4,20},{20... | collective-permute-start | bytes 786440 | tf_op jit(solution)/shard_map/ppermute | solution.py:37
  21.8 22.0 %copy-start.3 = (bf16[256,512]{1,0:T(8,128)(2,1)}, bf16[256,512]{1,0:T(8,128)(2,1)S(1)}, u32[]{:S(2)}) copy-start(bf16[256,512]{1,0:T(8,128)(2,1)S(1)} %collective-permute-done.2.refs_1_) | copy-start | bytes 786436
  21.8 8.2 %collective-permute-start.13 = (bf16[256,512]{1,0:T(8,128)(2,1)S(1)}, bf16[256,512]{1,0:T(8,128)(2,1)}, u32[]{:S(2)}, u32[]{:S(2)}) collective-permute-start(bf16[256,512]{1,0:T(8,128)(2,1)S(1)} %collective-permute-done.5.refs_4_), channel_id=1, source_target_pairs={{0,4},{1,5},{2,6},{3,7},{4,0},{5,1},{6,2},{7,3},{8,12},{9,13},{10,... | collective-permute-start | bytes 786440 | tf_op jit(solution)/shard_map/ppermute | solution.py:23
  23.6 20.2 %copy-start.5 = (bf16[256,512]{1,0:T(8,128)(2,1)}, bf16[256,512]{1,0:T(8,128)(2,1)S(1)}, u32[]{:S(2)}) copy-start(bf16[256,512]{1,0:T(8,128)(2,1)S(1)} %collective-permute-done.9.refs_8_) | copy-start | bytes 786436
  23.6 9.0 %collective-permute-start.7 = (bf16[256,512]{1,0:T(8,128)(2,1)S(1)}, bf16[256,512]{1,0:T(8,128)(2,1)}, u32[]{:S(2)}, u32[]{:S(2)}) collective-permute-start(bf16[256,512]{1,0:T(8,128)(2,1)S(1)} %collective-permute-done.5.refs_4_), channel_id=1, source_target_pairs={{0,2},{1,3},{2,0},{3,1},{4,6},{5,7},{6,4},{7,5},{8,10},{9,11},{10,... | collective-permute-start | bytes 786440 | tf_op jit(solution)/shard_map/ppermute | solution.py:23
  24.0 11.2 %collective-permute-start.10 = (bf16[256,512]{1,0:T(8,128)(2,1)S(1)}, bf16[256,512]{1,0:T(8,128)(2,1)}, u32[]{:S(2)}, u32[]{:S(2)}) collective-permute-start(bf16[256,512]{1,0:T(8,128)(2,1)S(1)} %collective-permute-done.9.refs_8_), channel_id=1, source_target_pairs={{0,16},{16,0},{1,17},{17,1},{2,18},{18,2},{3,19},{19,3},{4,20},{20... | collective-permute-start | bytes 786440 | tf_op jit(solution)/shard_map/ppermute | solution.py:37
  29.6 9.3 %collective-permute-start.11 = (bf16[256,512]{1,0:T(8,128)(2,1)S(1)}, bf16[256,512]{1,0:T(8,128)(2,1)}, u32[]{:S(2)}, u32[]{:S(2)}) collective-permute-start(bf16[256,512]{1,0:T(8,128)(2,1)S(1)} %collective-permute-done.9.refs_8_), channel_id=1, source_target_pairs={{0,2},{1,3},{2,0},{3,1},{4,6},{5,7},{6,4},{7,5},{8,10},{9,11},{10,... | collective-permute-start | bytes 786440 | tf_op jit(solution)/shard_map/ppermute | solution.py:23
  30.0 10.4 %collective-permute-start.14 = (bf16[256,512]{1,0:T(8,128)(2,1)}, bf16[256,512]{1,0:T(8,128)(2,1)}, u32[]{:S(2)}, u32[]{:S(2)}) collective-permute-start(bf16[256,512]{1,0:T(8,128)(2,1)} %collective-permute-done.13.refs_12_), channel_id=1, source_target_pairs={{0,16},{16,0},{1,17},{17,1},{2,18},{18,2},{3,19},{19,3},{4,20},{20... | collective-permute-start | bytes 786440 | tf_op jit(solution)/shard_map/ppermute | solution.py:37
  32.6 20.2 %collective-permute-start.15 = (bf16[256,512]{1,0:T(8,128)(2,1)}, bf16[256,512]{1,0:T(8,128)(2,1)}, u32[]{:S(2)}, u32[]{:S(2)}) collective-permute-start(bf16[256,512]{1,0:T(8,128)(2,1)} %collective-permute-done.13.refs_12_), channel_id=1, source_target_pairs={{0,2},{1,3},{2,0},{3,1},{4,6},{5,7},{6,4},{7,5},{8,10},{9,11},{10,... | collective-permute-start | bytes 786440 | tf_op jit(solution)/shard_map/ppermute | solution.py:23
  35.2 14.9 %collective-permute-start.8 = (bf16[256,512]{1,0:T(8,128)(2,1)}, bf16[256,512]{1,0:T(8,128)(2,1)}, u32[]{:S(2)}, u32[]{:S(2)}) collective-permute-start(bf16[256,512]{1,0:T(8,128)(2,1)} %collective-permute-done.6.refs_5_), channel_id=1, source_target_pairs={{0,2},{1,3},{2,0},{3,1},{4,6},{5,7},{6,4},{7,5},{8,10},{9,11},{10,... | collective-permute-start | bytes 786440 | tf_op jit(solution)/shard_map/ppermute | solution.py:23
  38.9 11.3 %collective-permute-start.12 = (bf16[256,512]{1,0:T(8,128)(2,1)}, bf16[256,512]{1,0:T(8,128)(2,1)}, u32[]{:S(2)}, u32[]{:S(2)}) collective-permute-start(bf16[256,512]{1,0:T(8,128)(2,1)} %collective-permute-done.11.refs_10_), channel_id=1, source_target_pairs={{0,16},{16,0},{1,17},{17,1},{2,18},{18,2},{3,19},{19,3},{4,20},{20... | collective-permute-start | bytes 786440 | tf_op jit(solution)/shard_map/ppermute | solution.py:37
  40.3 15.4 %collective-permute-start.16 = (bf16[256,512]{1,0:T(8,128)(2,1)}, bf16[256,512]{1,0:T(8,128)(2,1)}, u32[]{:S(2)}, u32[]{:S(2)}) collective-permute-start(bf16[256,512]{1,0:T(8,128)(2,1)} %collective-permute-done.14.refs_13_), channel_id=1, source_target_pairs={{0,2},{1,3},{2,0},{3,1},{4,6},{5,7},{6,4},{7,5},{8,10},{9,11},{10,... | collective-permute-start | bytes 786440 | tf_op jit(solution)/shard_map/ppermute | solution.py:23
  50.1 16.3 %collective-permute-start.21 = (bf16[256,512]{1,0:T(8,128)(2,1)}, bf16[256,512]{1,0:T(8,128)(2,1)S(1)}, u32[]{:S(2)}, u32[]{:S(2)}) collective-permute-start(bf16[256,512]{1,0:T(8,128)(2,1)} %get-tuple-element.29), channel_id=1, source_target_pairs={{0,2},{1,3},{2,0},{3,1},{4,6},{5,7},{6,4},{7,5},{8,10},{9,11},{10,... | collective-permute-start | bytes 786440 | tf_op jit(solution)/shard_map/ppermute | solution.py:33
  50.2 17.2 %collective-permute-start.23 = (bf16[256,512]{1,0:T(8,128)(2,1)}, bf16[256,512]{1,0:T(8,128)(2,1)S(1)}, u32[]{:S(2)}, u32[]{:S(2)}) collective-permute-start(bf16[256,512]{1,0:T(8,128)(2,1)} %get-tuple-element.29), channel_id=1, source_target_pairs={{0,8},{1,9},{2,10},{3,11},{4,12},{5,13},{6,14},{7,15},{8,0},{9,1},... | collective-permute-start | bytes 786440 | tf_op jit(solution)/shard_map/ppermute | solution.py:33
  55.8 1.0 copy-start.4
  56.7 0.9 copy-start.6
  57.7 7.7 %copy-start.7 = (bf16[256,512]{1,0:T(8,128)(2,1)S(1)}, bf16[256,512]{1,0:T(8,128)(2,1)}, u32[]{:S(2)}) copy-start(bf16[256,512]{1,0:T(8,128)(2,1)} %get-tuple-element.29) | copy-start | bytes 786436
  57.7 8.7 %copy-start.8 = (bf16[256,512]{1,0:T(8,128)(2,1)S(1)}, bf16[256,512]{1,0:T(8,128)(2,1)}, u32[]{:S(2)}) copy-start(bf16[256,512]{1,0:T(8,128)(2,1)} %get-tuple-element.28) | copy-start | bytes 786436
  57.7 47.0 %copy-start.1 = (bf16[256,512]{1,0:T(8,128)(2,1)S(1)}, bf16[256,512]{1,0:T(8,128)(2,1)}, u32[]{:S(2)}) copy-start(bf16[256,512]{1,0:T(8,128)(2,1)} %get-tuple-element.27.refs_3_) | copy-start | bytes 786436
  65.3 6.4 %collective-permute-start.17 = (bf16[2,256,256]{2,1,0:T(8,128)(2,1)S(1)}, bf16[2,256,256]{2,1,0:T(8,128)(2,1)S(1)}, u32[]{:S(2)}, u32[]{:S(2)}) collective-permute-start(bf16[2,256,256]{2,1,0:T(8,128)(2,1)S(1)} %get-tuple-element.26), channel_id=1, source_target_pairs={{0,2},{1,3},{2,0},{3,1},{4,6},{5,7},{6,4},{7,5},{8,10},{9,11},{10,... | collective-permute-start | bytes 786440 | tf_op jit(solution)/shard_map/ppermute | solution.py:23
  65.4 8.6 %collective-permute-start.27 = (bf16[256,512]{1,0:T(8,128)(2,1)S(1)}, bf16[256,512]{1,0:T(8,128)(2,1)S(1)}, u32[]{:S(2)}, u32[]{:S(2)}) collective-permute-start(bf16[256,512]{1,0:T(8,128)(2,1)S(1)} %copy-done.7), channel_id=1, source_target_pairs={{0,4},{1,5},{2,6},{3,7},{4,0},{5,1},{6,2},{7,3},{8,12},{9,13},{10,... | collective-permute-start | bytes 786440 | tf_op jit(solution)/shard_map/ppermute | solution.py:33
  66.4 6.1 %collective-permute-start.20 = (bf16[256,512]{1,0:T(8,128)(2,1)S(1)}, bf16[256,512]{1,0:T(8,128)(2,1)S(1)}, u32[]{:S(2)}, u32[]{:S(2)}) collective-permute-start(bf16[256,512]{1,0:T(8,128)(2,1)S(1)} %copy-done.8), channel_id=1, source_target_pairs={{0,1},{1,0},{2,3},{3,2},{4,5},{5,4},{6,7},{7,6},{8,9},{9,8},{10,11... | collective-permute-start | bytes 786440 | tf_op jit(solution)/shard_map/ppermute | solution.py:23
  66.4 9.4 %collective-permute-start.22 = (bf16[256,512]{1,0:T(8,128)(2,1)S(1)}, bf16[256,512]{1,0:T(8,128)(2,1)S(1)}, u32[]{:S(2)}, u32[]{:S(2)}) collective-permute-start(bf16[256,512]{1,0:T(8,128)(2,1)S(1)} %collective-permute-done.21.refs_5_), channel_id=1, source_target_pairs={{0,16},{16,0},{1,17},{17,1},{2,18},{18,2},{3,19},{19,3},{4,20},{20... | collective-permute-start | bytes 786440 | tf_op jit(solution)/shard_map/ppermute | solution.py:37
  67.4 11.8 %collective-permute-start.31 = (bf16[256,512]{1,0:T(8,128)(2,1)S(1)}, bf16[256,512]{1,0:T(8,128)(2,1)S(1)}, u32[]{:S(2)}, u32[]{:S(2)}) collective-permute-start(bf16[256,512]{1,0:T(8,128)(2,1)S(1)} %collective-permute-done.23.refs_7_), channel_id=1, source_target_pairs={{0,4},{1,5},{2,6},{3,7},{4,0},{5,1},{6,2},{7,3},{8,12},{9,13},{10,... | collective-permute-start | bytes 786440 | tf_op jit(solution)/shard_map/ppermute | solution.py:23
  71.8 11.3 %collective-permute-start.18 = (bf16[2,256,256]{2,1,0:T(8,128)(2,1)S(1)}, bf16[2,256,256]{2,1,0:T(8,128)(2,1)S(1)}, u32[]{:S(2)}, u32[]{:S(2)}) collective-permute-start(bf16[2,256,256]{2,1,0:T(8,128)(2,1)S(1)} %add_convert_fusion.1), channel_id=1, source_target_pairs={{0,4},{1,5},{2,6},{3,7},{4,0},{5,1},{6,2},{7,3},{8,12},{9,13},{10,... | collective-permute-start | bytes 786440 | tf_op jit(solution)/shard_map/ppermute | solution.py:23
  72.5 12.5 %collective-permute-start.24 = (bf16[256,512]{1,0:T(8,128)(2,1)S(1)}, bf16[256,512]{1,0:T(8,128)(2,1)S(1)}, u32[]{:S(2)}, u32[]{:S(2)}) collective-permute-start(bf16[256,512]{1,0:T(8,128)(2,1)S(1)} %collective-permute-done.23.refs_7_), channel_id=1, source_target_pairs={{0,16},{16,0},{1,17},{17,1},{2,18},{18,2},{3,19},{19,3},{4,20},{20... | collective-permute-start | bytes 786440 | tf_op jit(solution)/shard_map/ppermute | solution.py:37
  74.0 11.6 %collective-permute-start.25 = (bf16[256,512]{1,0:T(8,128)(2,1)S(1)}, bf16[256,512]{1,0:T(8,128)(2,1)S(1)}, u32[]{:S(2)}, u32[]{:S(2)}) collective-permute-start(bf16[256,512]{1,0:T(8,128)(2,1)S(1)} %collective-permute-done.23.refs_7_), channel_id=1, source_target_pairs={{0,2},{1,3},{2,0},{3,1},{4,6},{5,7},{6,4},{7,5},{8,10},{9,11},{10,... | collective-permute-start | bytes 786440 | tf_op jit(solution)/shard_map/ppermute | solution.py:23
  75.8 11.4 %collective-permute-start.28 = (bf16[256,512]{1,0:T(8,128)(2,1)S(1)}, bf16[256,512]{1,0:T(8,128)(2,1)S(1)}, u32[]{:S(2)}, u32[]{:S(2)}) collective-permute-start(bf16[256,512]{1,0:T(8,128)(2,1)S(1)} %collective-permute-done.27.refs_11_), channel_id=1, source_target_pairs={{0,16},{16,0},{1,17},{17,1},{2,18},{18,2},{3,19},{19,3},{4,20},{20... | collective-permute-start | bytes 786440 | tf_op jit(solution)/shard_map/ppermute | solution.py:37
  79.2 9.4 %collective-permute-start.33 = (bf16[256,512]{1,0:T(8,128)(2,1)S(1)}, bf16[256,512]{1,0:T(8,128)(2,1)S(1)}, u32[]{:S(2)}, u32[]{:S(2)}) collective-permute-start(bf16[256,512]{1,0:T(8,128)(2,1)S(1)} %collective-permute-done.31.refs_15_), channel_id=1, source_target_pairs={{0,2},{1,3},{2,0},{3,1},{4,6},{5,7},{6,4},{7,5},{8,10},{9,11},{10,... | collective-permute-start | bytes 786440 | tf_op jit(solution)/shard_map/ppermute | solution.py:23
  83.0 11.2 %collective-permute-start.29 = (bf16[256,512]{1,0:T(8,128)(2,1)S(1)}, bf16[256,512]{1,0:T(8,128)(2,1)S(1)}, u32[]{:S(2)}, u32[]{:S(2)}) collective-permute-start(bf16[256,512]{1,0:T(8,128)(2,1)S(1)} %collective-permute-done.27.refs_11_), channel_id=1, source_target_pairs={{0,2},{1,3},{2,0},{3,1},{4,6},{5,7},{6,4},{7,5},{8,10},{9,11},{10,... | collective-permute-start | bytes 786440 | tf_op jit(solution)/shard_map/ppermute | solution.py:23
  85.1 14.9 %collective-permute-start.32 = (bf16[256,512]{1,0:T(8,128)(2,1)S(1)}, bf16[256,512]{1,0:T(8,128)(2,1)S(1)}, u32[]{:S(2)}, u32[]{:S(2)}) collective-permute-start(bf16[256,512]{1,0:T(8,128)(2,1)S(1)} %collective-permute-done.31.refs_15_), channel_id=1, source_target_pairs={{0,16},{16,0},{1,17},{17,1},{2,18},{18,2},{3,19},{19,3},{4,20},{20... | collective-permute-start | bytes 786440 | tf_op jit(solution)/shard_map/ppermute | solution.py:37
  85.6 14.4 %collective-permute-start.26 = (bf16[256,512]{1,0:T(8,128)(2,1)S(1)}, bf16[256,512]{1,0:T(8,128)(2,1)S(1)}, u32[]{:S(2)}, u32[]{:S(2)}) collective-permute-start(bf16[256,512]{1,0:T(8,128)(2,1)S(1)} %collective-permute-done.25.refs_9_), channel_id=1, source_target_pairs={{0,16},{16,0},{1,17},{17,1},{2,18},{18,2},{3,19},{19,3},{4,20},{20... | collective-permute-start | bytes 786440 | tf_op jit(solution)/shard_map/ppermute | solution.py:37
  87.2 12.8 %collective-permute-start.30 = (bf16[256,512]{1,0:T(8,128)(2,1)S(1)}, bf16[256,512]{1,0:T(8,128)(2,1)S(1)}, u32[]{:S(2)}, u32[]{:S(2)}) collective-permute-start(bf16[256,512]{1,0:T(8,128)(2,1)S(1)} %collective-permute-done.28.refs_12_), channel_id=1, source_target_pairs={{0,2},{1,3},{2,0},{3,1},{4,6},{5,7},{6,4},{7,5},{8,10},{9,11},{10,... | collective-permute-start | bytes 786440 | tf_op jit(solution)/shard_map/ppermute | solution.py:23
  88.6 16.1 %collective-permute-start.34 = (bf16[256,512]{1,0:T(8,128)(2,1)S(1)}, bf16[256,512]{1,0:T(8,128)(2,1)S(1)}, u32[]{:S(2)}, u32[]{:S(2)}) collective-permute-start(bf16[256,512]{1,0:T(8,128)(2,1)S(1)} %collective-permute-done.33.refs_17_), channel_id=1, source_target_pairs={{0,16},{16,0},{1,17},{17,1},{2,18},{18,2},{3,19},{19,3},{4,20},{20... | collective-permute-start | bytes 786440 | tf_op jit(solution)/shard_map/ppermute | solution.py:37
  94.2 10.5 %collective-permute-start.19 = (bf16[2,256,256]{2,1,0:T(8,128)(2,1)S(1)}, bf16[2,256,256]{2,1,0:T(8,128)(2,1)S(1)}, u32[]{:S(2)}, u32[]{:S(2)}) collective-permute-start(bf16[2,256,256]{2,1,0:T(8,128)(2,1)S(1)} %add_convert_fusion), channel_id=1, source_target_pairs={{0,8},{1,9},{2,10},{3,11},{4,12},{5,13},{6,14},{7,15},{8,0},{9,1},... | collective-permute-start | bytes 786440 | tf_op jit(solution)/shard_map/ppermute | solution.py:23
  109.2 5.0 %collective-permute-start.36 = (bf16[1024,1024]{1,0:T(8,128)(2,1)S(1)}, bf16[1024,1024]{1,0:T(8,128)(2,1)S(1)}, u32[]{:S(2)}, u32[]{:S(2)}) collective-permute-start(bf16[1024,1024]{1,0:T(8,128)(2,1)S(1)} %get-tuple-element.34.w_mine), channel_id=1, source_target_pairs={{0,1},{1,0},{2,3},{3,2},{4,5},{5,4},{6,7},{7,6},{8,9},{9,8},{10,11... | collective-permute-start | bytes 6291464 | tf_op jit(solution)/shard_map/ppermute | solution.py:23
  109.3 4.9 %collective-permute-start.35 = (bf16[512,512]{1,0:T(8,128)(2,1)S(1)}, bf16[512,512]{1,0:T(8,128)(2,1)S(1)}, u32[]{:S(2)}, u32[]{:S(2)}) collective-permute-start(bf16[512,512]{1,0:T(8,128)(2,1)S(1)} %get-tuple-element.33), channel_id=1, source_target_pairs={{0,1},{1,0},{2,3},{3,2},{4,5},{5,4},{6,7},{7,6},{8,9},{9,8},{10,11... | collective-permute-start | bytes 1572872 | tf_op jit(solution)/shard_map/ppermute | solution.py:23

commit v3 on v2

--- a/solution.py
+++ b/solution.py
@@ -23,10 +23,10 @@
     return lax.ppermute(value, "seq", [(i, i ^ mask) for i in range(lax.axis_size("seq"))])
 
 
-def swap_crossed(value, bit):
+def swap_crossed(value, bit, even=0):
     size = lax.axis_size("seq")
     pairs = [
-        (g * size + i, g * size + (i ^ (1 << bit) ^ (g % 2)))
+        (g * size + i, g * size + (i ^ (1 << bit) ^ ((g + even) % 2)))
         for g in range(lax.axis_size("group"))
         for i in range(size)
     ]
@@ -40,11 +40,11 @@
 OWN, OTHER, MINE, FAR = range(4)
 
 
-def gather_rows(first, mine, arrived, zbits, turn):
+def gather_rows(first, second, mine, arrived, zbits, turn):
     pieces = [(mine, 0, MINE), (arrived, 0, FAR)]
-    across = swap_crossed(first, 1)
-    pieces.append((across, 1, OWN))
-    pieces.append((swap_x(across), 1, OTHER))
+    beside = swap_crossed(first, 1)
+    pieces.append((beside, 1, OWN))
+    pieces.append((swap_x(beside), 1, OTHER))
     held = []
     for bit in reversed(zbits):
         flip = 1 << (bit - 1)
@@ -53,9 +53,13 @@
             got.append((swap(piece, bit), before ^ flip))
         held += got
     for at, (piece, flip) in enumerate(held):
-        side = swap_x(piece)
-        across = swap(piece, 1)
-        if (at + turn) % 2:
+        if flip == 1 << (zbits[0] - 1):
+            side = swap_crossed(second, zbits[0], 1)
+            across = swap(beside, zbits[0])
+        else:
+            side = swap_x(piece)
+            across = swap(piece, 1)
+        if at in turn:
             corner = swap_x(across)
         else:
             corner = swap(side, 1)
@@ -71,10 +75,10 @@
 
 
 def split_kernel(parts, width, *refs):
-    sources, outs = refs[:-3], refs[-3:]
+    sources, outs = refs[:-4], refs[-4:]
     core = lax.axis_index("seq") % CORES
     sent_core = core ^ (lax.axis_index("group") % 2)
-    for out, half in zip(outs, (sent_core, core, 1 - core)):
+    for out, half in zip(outs, (sent_core, 1 - sent_core, core, 1 - core)):
         row = 0
         for source, offset, stride in parts:
             ref = sources[source]
@@ -125,10 +129,10 @@
 
 def attend_kernel(which, n, nb, rows, out_rows, heads, levels, local_bits, starts, x, k, v, other, scale, *refs):
     buckets, pieces, refs = refs[:nb], refs[nb : nb + n], refs[nb + n :]
-    out, wq = refs[0], refs[-1]
+    out, q_out, wq = refs[0], refs[1], refs[-1]
     place_rows(wq, pieces, 0, slice(None), starts, 0, rows)
     if which:
-        w = refs[1]
+        w = refs[2]
         width = pieces[0].shape[1]
         for part in range(w.shape[1] // width):
             cols = slice(part * width, (part + 1) * width)
@@ -138,6 +142,7 @@
     apart = row ^ col
     causal = row >= col
     q = dot(x[...], wq[...]).astype(BF16)
+    q_out[...] = q
     first = CBITS + local_bits + 1
     for h in range(heads):
         cols = slice(h * HEAD, (h + 1) * HEAD)
@@ -164,7 +169,15 @@
                     value = value + dot(qh, bucket.astype(BF16)) * weight(CBITS + b)
             for at, bucket in enumerate((other, *buckets)):
                 value = value + dot(qh, bucket[h]) * weight(first + at)
-            out[span, cols] = value.astype(BF16)
+            out[span, cols] = value
+
+
+def reads_kernel(which, heads, levels, level, scale, part, q, bucket, out):
+    for h in range(heads):
+        cols = slice(h * HEAD, (h + 1) * HEAD)
+        at = h * levels + level
+        weight = scale[which, :, at : at + 1]
+        out[:, cols] = (part[:, cols] + dot(q[:, cols], bucket[h]) * weight).astype(BF16)
 
 
 def output_kernel(width, core_ref, mine, theirs, w_mine, w_theirs, out, block, sem):
@@ -193,7 +206,7 @@
 FAST = pl.BlockSpec(memory_space=pltpu.VMEM)
 
 
-def call(kernel, operands, out_specs, out_shape, scratch, flops, room=24):
+def call(kernel, operands, out_specs, out_shape, scratch, flops, room=12):
     return pl.pallas_call(
         kernel,
         in_specs=[SMALL] + [FAST] * (len(operands) - 1),
@@ -225,12 +238,12 @@
 
     def split(sources, parts):
         shape = (sum(sources[part[0]].shape[0] for part in parts), cols)
-        first, mine, far = pl.pallas_call(
+        first, second, mine, far = pl.pallas_call(
             functools.partial(split_kernel, parts, cols),
-            out_shape=[sd(shape, BF16)] * 3,
+            out_shape=[sd(shape, BF16)] * 4,
             cost_estimate=pl.CostEstimate(flops=1 << 20, bytes_accessed=2 << 20, transcendentals=0),
         )(*sources)
-        return first, mine, swap(far, 0)
+        return first, second, mine, swap(far, 0)
 
     kv_split = split((w_qkv,), ((0, 2 * head_cols, cols), (0, head_cols, cols)))
     out_parts = out_cols // cols
@@ -250,8 +263,8 @@
     scale = jnp.stack([own_w, far_w]) * on[:, :, None, None]
     scale = jnp.transpose(scale, (0, 3, 2, 1)).reshape(2, toks, heads * levels)
 
-    kvp = gather_rows(*kv_split, zbits, 0)
-    qop = gather_rows(*qo_split, zbits, 1)
+    kvp = gather_rows(*kv_split, zbits, (0,))
+    qop = gather_rows(*qo_split, zbits, (0, 1))
 
     act = sd((toks, cols), BF16)
     state = sd((heads, HEAD, HEAD), BF16)
@@ -275,22 +288,33 @@
     )
 
     def attend(which, x, k, v, other):
-        shapes = [act] + [sd((head_cols, out_cols), BF16)] * which
+        shapes = [sd((toks, cols), F32), act] + [sd((head_cols, out_cols), BF16)] * which
         return call(
             functools.partial(
-                attend_kernel, which, len(qop), len(buckets), rows, out_rows, heads, levels, local_bits
+                attend_kernel, which, len(qop), len(buckets) - 1, rows, out_rows, heads, levels, local_bits
             ),
-            [starts, x, k, v, other, scale, *buckets, *(piece[0] for piece in qop)],
+            [starts, x, k, v, other, scale, *buckets[:-1], *(piece[0] for piece in qop)],
             [FAST] * len(shapes),
             shapes,
             [pltpu.VMEM((width, cols), BF16)],
             2 * toks * width * cols,
         )
 
-    far_part, w_mine = attend(1, far_tokens, kb, vb, da)
-    theirs = swap(far_part, 0)
+    def read(which, part, q):
+        return pl.pallas_call(
+            functools.partial(reads_kernel, which, heads, levels, first_bit + seq_bits - 1),
+            in_specs=[FAST] * 4,
+            out_specs=FAST,
+            out_shape=act,
+            compiler_params=pltpu.CompilerParams(vmem_limit_bytes=8 << 20),
+            cost_estimate=pl.CostEstimate(flops=1 << 28, bytes_accessed=2 << 20, transcendentals=0),
+        )(scale, part, q, buckets[-1])
+
+    far_part, far_q, w_mine = attend(1, far_tokens, kb, vb, da)
     w_theirs = swap(w_mine, 0)
-    (mine,) = attend(0, tokens, ka, va, db)
+    own_part, own_q = attend(0, tokens, ka, va, db)
+    theirs = swap(read(1, far_part, far_q), 0)
+    mine = read(0, own_part, own_q)
     n_blocks = CORES * out_parts
     return call(
         functools.partial(output_kernel, cols),

time: 120 us -> 133 us (1.11); the launches traced: 117 us -> 132 us
  waiting for transfers between devices: 50.6 us -> 68.1 us
  starting transfers between devices: 38.8 us -> 36.8 us
  other arithmetic: 1.85 us -> 0.48 us
    ppermute x6 -> x8, waiting for transfers between devices: 8.02 us -> 15.7 us  [swap_crossed(): return lax.ppermute(value, ('group', 'seq'), pairs)]
    ppermute x20, waiting for transfers between devices: 27.1 us -> 34.1 us  [swap(): lax.ppermute(value, 'seq', [(i, i ^ mask) for i in range(lax.axis_size('s...]
    ppermute x20, starting transfers between devices: 15.4 us -> 11.8 us  [swap(): lax.ppermute(value, 'seq', [(i, i ^ mask) for i in range(lax.axis_size('s...]
    ppermute x11 -> x9, waiting for transfers between devices: 15.4 us -> 18.3 us  [swap_x(): lax.ppermute(value, 'group', [(i, i ^ 1) for i in range(lax.axis_size('gr...]
    ppermute x11 -> x9, starting transfers between devices: 13 us -> 14.5 us  [swap_x(): lax.ppermute(value, 'group', [(i, i ^ 1) for i in range(lax.axis_size('gr...]
    ppermute x6 -> x8, starting transfers between devices: 10.3 us -> 10.5 us  [swap_crossed(): return lax.ppermute(value, ('group', 'seq'), pairs)]
  transfers between devices with their start and end apart: 37 -> 37, of which waited for: 19 -> 17; matrix products, arithmetic and copies ran while one was open for 3% -> 1% of each run, Pallas kernels for 13% -> 12%
where the time goes in v3:
time: 133 us; the launch traced here: 132 us
  waiting for transfers between devices  68.1 us (51%)
  starting transfers between devices  36.8 us (28%)
  Pallas kernels  23.2 us (17%)
  local copies, waits for them, and re-layouts  3.34 us (3%)
    ppermute x20, waiting for transfers between devices, swap(): lax.ppermute(value, 'seq', [(i, i ^ mask) for i in range(lax.axis_size('s...  34.1 us
    ppermute x9, waiting for transfers between devices, swap_x(): lax.ppermute(value, 'group', [(i, i ^ 1) for i in range(lax.axis_size('gr...  18.3 us
    pallas_call x4, Pallas kernels, call(): pl.pallas_call(kernel, in_specs=[SMALL] + [FAST] * (len(operands) - 1), o...  18.1 us
    ppermute x8, waiting for transfers between devices, swap_crossed(): return lax.ppermute(value, ('group', 'seq'), pairs)  15.7 us
    ppermute x9, starting transfers between devices, swap_x(): lax.ppermute(value, 'group', [(i, i ^ 1) for i in range(lax.axis_size('gr...  14.5 us
    ppermute x20, starting transfers between devices, swap(): lax.ppermute(value, 'seq', [(i, i ^ mask) for i in range(lax.axis_size('s...  11.8 us
    ppermute x8, starting transfers between devices, swap_crossed(): return lax.ppermute(value, ('group', 'seq'), pairs)  10.5 us
    pallas_call x2, Pallas kernels, split(): pl.pallas_call(functools.partial(split_kernel, parts, cols), out_shape=[s...  4.43 us
  transfers between devices with their start and end apart: 37, of which 17 were waited for; matrix products, arithmetic and copies ran while one was open for 1% of the time, Pallas kernels for 12%

profile of v3, /device:TPU:0, one launch (start us, length us, event | category | flops | bytes accessed | tf_op | source)
XLA Modules:
  0.0 132.2 jit_solution(7751685843209713120)
XLA Ops:
  0.0 0.6 collective-permute-start.1
  0.6 1.1 dynamic-slice_bitcast_fusion
  1.7 0.1 collective-permute-start
  1.9 2.2 %shard_map.127 = (bf16[256,512]{1,0:T(8,128)(2,1)}, bf16[256,512]{1,0:T(8,128)(2,1)}, bf16[256,512]{1,0:T(8,128)(2,1)}, bf16[256,512]{1,0:T(8,128)(2,1)}) custom-call(bf16[128,3072]{1,0:T(8,128)(2,1)} %refs_0_.3), custom_call_target="tpu_custom_call" | custom-call | flops 1048576 | bytes 2097152 | tf_op jit(solution)/shard_map/pallas_call | solution.py:241
  4.1 0.4 collective-permute-start.2
  4.5 2.6 %collective-permute-start.3 = (bf16[256,512]{1,0:T(8,128)(2,1)}, bf16[256,512]{1,0:T(8,128)(2,1)S(1)}, u32[]{:S(2)}, u32[]{:S(2)}) collective-permute-start(bf16[256,512]{1,0:T(8,128)(2,1)} %get-tuple-element.27), channel_id=1, source_target_pairs={{0,2},{1,3},{2,0},{3,1},{4,6},{5,7},{6,4},{7,5},{8,10},{9,11},{10,... | collective-permute-start | bytes 786440 | tf_op jit(solution)/shard_map/ppermute | solution.py:33
  7.1 2.6 %collective-permute-start.5 = (bf16[256,512]{1,0:T(8,128)(2,1)}, bf16[256,512]{1,0:T(8,128)(2,1)S(1)}, u32[]{:S(2)}, u32[]{:S(2)}) collective-permute-start(bf16[256,512]{1,0:T(8,128)(2,1)} %get-tuple-element.27), channel_id=1, source_target_pairs={{0,8},{1,9},{2,10},{3,11},{4,12},{5,13},{6,14},{7,15},{8,0},{9,1},... | collective-permute-start | bytes 786440 | tf_op jit(solution)/shard_map/ppermute | solution.py:33
  9.7 1.6 %collective-permute-start.9 = (bf16[256,512]{1,0:T(8,128)(2,1)}, bf16[256,512]{1,0:T(8,128)(2,1)}, u32[]{:S(2)}, u32[]{:S(2)}) collective-permute-start(bf16[256,512]{1,0:T(8,128)(2,1)} %get-tuple-element.27), channel_id=1, source_target_pairs={{0,4},{1,5},{2,6},{3,7},{4,0},{5,1},{6,2},{7,3},{8,12},{9,13},{10,... | collective-permute-start | bytes 786440 | tf_op jit(solution)/shard_map/ppermute | solution.py:33
  11.2 2.2 %shard_map.129 = (bf16[256,512]{1,0:T(8,128)(2,1)}, bf16[256,512]{1,0:T(8,128)(2,1)}, bf16[256,512]{1,0:T(8,128)(2,1)}, bf16[256,512]{1,0:T(8,128)(2,1)}) custom-call(bf16[128,3072]{1,0:T(8,128)(2,1)} %refs_0_.3, bf16[64,2048]{1,0:T(8,128)(2,1)} %refs_1_.1), custom_call_target="tpu_custom_call" | custom-call | flops 1048576 | bytes 2097152 | tf_op jit(solution)/shard_map/pallas_call | solution.py:241
  13.5 0.6 collective-permute-done.3.refs_2_
  14.1 2.8 %collective-permute-start.22 = (bf16[256,512]{1,0:T(8,128)(2,1)}, bf16[256,512]{1,0:T(8,128)(2,1)S(1)}, u32[]{:S(2)}, u32[]{:S(2)}) collective-permute-start(bf16[256,512]{1,0:T(8,128)(2,1)} %get-tuple-element.35), channel_id=1, source_target_pairs={{0,8},{1,9},{2,10},{3,11},{4,12},{5,13},{6,14},{7,15},{8,0},{9,1},... | collective-permute-start | bytes 786440 | tf_op jit(solution)/shard_map/ppermute | solution.py:33
  16.9 6.2 %collective-permute-done.5.refs_4_ = bf16[256,512]{1,0:T(8,128)(2,1)S(1)} collective-permute-done((bf16[256,512]{1,0:T(8,128)(2,1)}, bf16[256,512]{1,0:T(8,128)(2,1)S(1)}, u32[]{:S(2)}, u32[]{:S(2)}) %collective-permute-start.5) | collective-permute-done | bytes 262176 | tf_op jit(solution)/shard_map/ppermute | solution.py:33
  23.1 0.5 collective-permute-start.4
  23.6 5.7 %collective-permute-done.9.refs_8_ = bf16[256,512]{1,0:T(8,128)(2,1)} collective-permute-done((bf16[256,512]{1,0:T(8,128)(2,1)}, bf16[256,512]{1,0:T(8,128)(2,1)}, u32[]{:S(2)}, u32[]{:S(2)}) %collective-permute-start.9) | collective-permute-done | bytes 262176 | tf_op jit(solution)/shard_map/ppermute | solution.py:33
  29.3 3.3 %collective-permute-done.10.refs_9_ = bf16[256,512]{1,0:T(8,128)(2,1)} collective-permute-done((bf16[256,512]{1,0:T(8,128)(2,1)}, bf16[256,512]{1,0:T(8,128)(2,1)}, u32[]{:S(2)}, u32[]{:S(2)}) %collective-permute-start.10) | collective-permute-done | bytes 262176 | tf_op jit(solution)/shard_map/ppermute | solution.py:33
  32.5 3.5 %collective-permute-start.6 = (bf16[256,512]{1,0:T(8,128)(2,1)S(1)}, bf16[256,512]{1,0:T(8,128)(2,1)}, u32[]{:S(2)}, u32[]{:S(2)}) collective-permute-start(bf16[256,512]{1,0:T(8,128)(2,1)S(1)} %collective-permute-done.5.refs_4_), channel_id=1, source_target_pairs={{0,16},{16,0},{1,17},{17,1},{2,18},{18,2},{3,19},{19,3},{4,20},{20... | collective-permute-start | bytes 786440 | tf_op jit(solution)/shard_map/ppermute | solution.py:37
  36.1 0.5 collective-permute-start.7
  36.6 3.9 %collective-permute-done.13.refs_12_ = bf16[256,512]{1,0:T(8,128)(2,1)} collective-permute-done((bf16[256,512]{1,0:T(8,128)(2,1)S(1)}, bf16[256,512]{1,0:T(8,128)(2,1)}, u32[]{:S(2)}, u32[]{:S(2)}) %collective-permute-start.13) | collective-permute-done | bytes 262176 | tf_op jit(solution)/shard_map/ppermute | solution.py:23
  40.5 1.2 collective-permute-start.14
  41.7 0.1 pad_add_fusion
  41.8 0.1 convert_multiply_fusion
  41.8 1.5 %collective-permute-done.6.refs_5_ = bf16[256,512]{1,0:T(8,128)(2,1)} collective-permute-done((bf16[256,512]{1,0:T(8,128)(2,1)S(1)}, bf16[256,512]{1,0:T(8,128)(2,1)}, u32[]{:S(2)}, u32[]{:S(2)}) %collective-permute-start.6) | collective-permute-done | bytes 262176 | tf_op jit(solution)/shard_map/ppermute | solution.py:37
  43.3 0.5 collective-permute-start.12
  43.8 1.5 %collective-permute-start.15 = (bf16[256,512]{1,0:T(8,128)(2,1)}, bf16[256,512]{1,0:T(8,128)(2,1)}, u32[]{:S(2)}, u32[]{:S(2)}) collective-permute-start(bf16[256,512]{1,0:T(8,128)(2,1)} %collective-permute-done.13.refs_12_), channel_id=1, source_target_pairs={{0,2},{1,3},{2,0},{3,1},{4,6},{5,7},{6,4},{7,5},{8,10},{9,11},{10,... | collective-permute-start | bytes 786440 | tf_op jit(solution)/shard_map/ppermute | solution.py:23
  45.4 1.4 %collective-permute-start.8 = (bf16[256,512]{1,0:T(8,128)(2,1)}, bf16[256,512]{1,0:T(8,128)(2,1)}, u32[]{:S(2)}, u32[]{:S(2)}) collective-permute-start(bf16[256,512]{1,0:T(8,128)(2,1)} %collective-permute-done.7.refs_6_), channel_id=1, source_target_pairs={{0,16},{16,0},{1,17},{17,1},{2,18},{18,2},{3,19},{19,3},{4,20},{20... | collective-permute-start | bytes 786440 | tf_op jit(solution)/shard_map/ppermute | solution.py:37
  46.8 3.0 %collective-permute-done.14.refs_13_ = bf16[256,512]{1,0:T(8,128)(2,1)} collective-permute-done((bf16[256,512]{1,0:T(8,128)(2,1)}, bf16[256,512]{1,0:T(8,128)(2,1)}, u32[]{:S(2)}, u32[]{:S(2)}) %collective-permute-start.14) | collective-permute-done | bytes 262176 | tf_op jit(solution)/shard_map/ppermute | solution.py:37
  49.8 0.1 fusion
  50.0 0.2 copy.18.scale
  50.3 2.6 %collective-permute-done.12.refs_11_ = bf16[256,512]{1,0:T(8,128)(2,1)} collective-permute-done((bf16[256,512]{1,0:T(8,128)(2,1)}, bf16[256,512]{1,0:T(8,128)(2,1)}, u32[]{:S(2)}, u32[]{:S(2)}) %collective-permute-start.12) | collective-permute-done | bytes 262176 | tf_op jit(solution)/shard_map/ppermute | solution.py:23
  52.8 0.5 collective-permute-start.20
  53.3 0.9 collective-permute-done.8.refs_7_
  54.3 0.4 collective-permute-start.26
  54.7 3.7 %collective-permute-done.15.refs_14_ = bf16[256,512]{1,0:T(8,128)(2,1)} collective-permute-done((bf16[256,512]{1,0:T(8,128)(2,1)}, bf16[256,512]{1,0:T(8,128)(2,1)}, u32[]{:S(2)}, u32[]{:S(2)}) %collective-permute-start.15) | collective-permute-done | bytes 262176 | tf_op jit(solution)/shard_map/ppermute | solution.py:23
  58.4 5.6 %collective-permute-done.16.refs_15_ = bf16[256,512]{1,0:T(8,128)(2,1)} collective-permute-done((bf16[256,512]{1,0:T(8,128)(2,1)}, bf16[256,512]{1,0:T(8,128)(2,1)}, u32[]{:S(2)}, u32[]{:S(2)}) %collective-permute-start.16) | collective-permute-done | bytes 262176 | tf_op jit(solution)/shard_map/ppermute | solution.py:23
  64.1 0.9 copy-done.4
  65.1 0.9 copy-done.6
  66.0 7.6 %shard_map.128 = (bf16[512,512]{1,0:T(8,128)(2,1)S(1)}, bf16[512,512]{1,0:T(8,128)(2,1)S(1)}, bf16[512,512]{1,0:T(8,128)(2,1)S(1)}, bf16[512,512]{1,0:T(8,128)(2...) custom-call(s32[16]{0:T(128)S(1)} %get-tuple-element.45.starts, ...), custom_call_target="tpu_custom_call" | custom-call | flops 4294967296 | bytes 8388608 | tf_op jit(solution)/shard_map/pallas_call | solution.py:210
  73.6 0.6 collective-permute-start.17
  74.2 2.1 %collective-permute-start.21 = (bf16[256,512]{1,0:T(8,128)(2,1)S(1)}, bf16[256,512]{1,0:T(8,128)(2,1)S(1)}, u32[]{:S(2)}, u32[]{:S(2)}) collective-permute-start(bf16[256,512]{1,0:T(8,128)(2,1)S(1)} %collective-permute-done.20.refs_4_), channel_id=1, source_target_pairs={{0,16},{16,0},{1,17},{17,1},{2,18},{18,2},{3,19},{19,3},{4,20},{20... | collective-permute-start | bytes 786440 | tf_op jit(solution)/shard_map/ppermute | solution.py:37
  76.3 1.5 %collective-permute-start.24 = (bf16[256,512]{1,0:T(8,128)(2,1)S(1)}, bf16[256,512]{1,0:T(8,128)(2,1)S(1)}, u32[]{:S(2)}, u32[]{:S(2)}) collective-permute-start(bf16[256,512]{1,0:T(8,128)(2,1)S(1)} %collective-permute-done.22.refs_6_), channel_id=1, source_target_pairs={{0,2},{1,3},{2,0},{3,1},{4,6},{5,7},{6,4},{7,5},{8,10},{9,11},{10,... | collective-permute-start | bytes 786440 | tf_op jit(solution)/shard_map/ppermute | solution.py:23
  77.9 0.4 collective-permute-start.28
  78.3 1.5 %collective-permute-start.31 = (bf16[256,512]{1,0:T(8,128)(2,1)S(1)}, bf16[256,512]{1,0:T(8,128)(2,1)S(1)}, u32[]{:S(2)}, u32[]{:S(2)}) collective-permute-start(bf16[256,512]{1,0:T(8,128)(2,1)S(1)} %collective-permute-done.30.refs_14_), channel_id=1, source_target_pairs={{0,16},{16,0},{1,17},{17,1},{2,18},{18,2},{3,19},{19,3},{4,20},{20... | collective-permute-start | bytes 786440 | tf_op jit(solution)/shard_map/ppermute | solution.py:37
  79.8 2.2 %collective-permute-done.17.refs_0_ = bf16[2,256,256]{2,1,0:T(8,128)(2,1)S(1)} collective-permute-done((bf16[2,256,256]{2,1,0:T(8,128)(2,1)S(1)}, bf16[2,256,256]{2,1,0:T(8,128)(2,1)S(1)}, u32[]{:S(2)}, u32[]{:S(2)}) %collective-permute-start.17) | collective-permute-done | bytes 262176 | tf_op jit(solution)/shard_map/ppermute | solution.py:23
  82.0 2.2 %collective-permute-start.23 = (bf16[256,512]{1,0:T(8,128)(2,1)S(1)}, bf16[256,512]{1,0:T(8,128)(2,1)S(1)}, u32[]{:S(2)}, u32[]{:S(2)}) collective-permute-start(bf16[256,512]{1,0:T(8,128)(2,1)S(1)} %collective-permute-done.22.refs_6_), channel_id=1, source_target_pairs={{0,16},{16,0},{1,17},{17,1},{2,18},{18,2},{3,19},{19,3},{4,20},{20... | collective-permute-start | bytes 786440 | tf_op jit(solution)/shard_map/ppermute | solution.py:37
  84.3 0.1 add_convert_fusion.1
  84.3 0.2 collective-permute-start.32
  84.5 3.1 %collective-permute-done.24.refs_8_ = bf16[256,512]{1,0:T(8,128)(2,1)S(1)} collective-permute-done((bf16[256,512]{1,0:T(8,128)(2,1)S(1)}, bf16[256,512]{1,0:T(8,128)(2,1)S(1)}, u32[]{:S(2)}, u32[]{:S(2)}) %collective-permute-start.24) | collective-permute-done | bytes 262176 | tf_op jit(solution)/shard_map/ppermute | solution.py:23
  87.6 0.2 collective-permute-start.25
  87.8 1.9 %collective-permute-start.29 = (bf16[256,512]{1,0:T(8,128)(2,1)S(1)}, bf16[256,512]{1,0:T(8,128)(2,1)S(1)}, u32[]{:S(2)}, u32[]{:S(2)}) collective-permute-start(bf16[256,512]{1,0:T(8,128)(2,1)S(1)} %collective-permute-done.28.refs_12_), channel_id=1, source_target_pairs={{0,16},{16,0},{1,17},{17,1},{2,18},{18,2},{3,19},{19,3},{4,20},{20... | collective-permute-start | bytes 786440 | tf_op jit(solution)/shard_map/ppermute | solution.py:37
  89.7 0.5 collective-permute-start.33
  90.2 4.1 %collective-permute-done.23.refs_7_ = bf16[256,512]{1,0:T(8,128)(2,1)S(1)} collective-permute-done((bf16[256,512]{1,0:T(8,128)(2,1)S(1)}, bf16[256,512]{1,0:T(8,128)(2,1)S(1)}, u32[]{:S(2)}, u32[]{:S(2)}) %collective-permute-start.23) | collective-permute-done | bytes 262176 | tf_op jit(solution)/shard_map/ppermute | solution.py:37
  94.3 2.4 %collective-permute-start.18 = (bf16[2,256,256]{2,1,0:T(8,128)(2,1)S(1)}, bf16[2,256,256]{2,1,0:T(8,128)(2,1)S(1)}, u32[]{:S(2)}, u32[]{:S(2)}) collective-permute-start(bf16[2,256,256]{2,1,0:T(8,128)(2,1)S(1)} %add_convert_fusion.1), channel_id=1, source_target_pairs={{0,4},{1,5},{2,6},{3,7},{4,0},{5,1},{6,2},{7,3},{8,12},{9,13},{10,... | collective-permute-start | bytes 786440 | tf_op jit(solution)/shard_map/ppermute | solution.py:23
  96.6 0.1 pad_add_fusion.1.starts
  96.7 3.2 %collective-permute-done.25.refs_9_ = bf16[256,512]{1,0:T(8,128)(2,1)S(1)} collective-permute-done((bf16[256,512]{1,0:T(8,128)(2,1)S(1)}, bf16[256,512]{1,0:T(8,128)(2,1)S(1)}, u32[]{:S(2)}, u32[]{:S(2)}) %collective-permute-start.25) | collective-permute-done | bytes 262176 | tf_op jit(solution)/shard_map/ppermute | solution.py:37
  99.9 5.6 %collective-permute-done.29.refs_13_ = bf16[256,512]{1,0:T(8,128)(2,1)S(1)} collective-permute-done((bf16[256,512]{1,0:T(8,128)(2,1)S(1)}, bf16[256,512]{1,0:T(8,128)(2,1)S(1)}, u32[]{:S(2)}, u32[]{:S(2)}) %collective-permute-start.29) | collective-permute-done | bytes 262176 | tf_op jit(solution)/shard_map/ppermute | solution.py:37
  105.5 4.3 %shard_map.132 = (f32[512,512]{1,0:T(8,128)S(1)}, bf16[512,512]{1,0:T(8,128)(2,1)S(1)}, bf16[1024,1024]{1,0:T(8,128)(2,1)S(1)}) custom-call(s32[32]{0:T(128)S(1)} %pad_add_fusion.1.starts, bf16[512,2048]{1,0:T(8,128)(2,1)} %collective-permute-done.1.xb.x, bf16[512,512]{1,0:T(8,128)(2,1)S(1)} %get-tuple-element.39.k, ...), custom_call_target="tpu_custom_call" | custom-call | flops 1073741824 | bytes 8388608 | tf_op jit(solution)/shard_map/pallas_call | solution.py:210
  109.8 0.4 collective-permute-start.36
  110.2 2.0 %collective-permute-start.34 = (bf16[2,256,256]{2,1,0:T(8,128)(2,1)S(1)}, bf16[2,256,256]{2,1,0:T(8,128)(2,1)S(1)}, u32[]{:S(2)}, u32[]{:S(2)}) collective-permute-start(bf16[2,256,256]{2,1,0:T(8,128)(2,1)S(1)} %add_convert_fusion), channel_id=1, source_target_pairs={{0,8},{1,9},{2,10},{3,11},{4,12},{5,13},{6,14},{7,15},{8,0},{9,1},... | collective-permute-start | bytes 786440 | tf_op jit(solution)/shard_map/ppermute | solution.py:23
  112.3 12.9 %collective-permute-done.34.bucket = bf16[2,256,256]{2,1,0:T(8,128)(2,1)S(1)} collective-permute-done((bf16[2,256,256]{2,1,0:T(8,128)(2,1)S(1)}, bf16[2,256,256]{2,1,0:T(8,128)(2,1)S(1)}, u32[]{:S(2)}, u32[]{:S(2)}) %collective-permute-start.34) | collective-permute-done | bytes 262176 | tf_op jit(solution)/shard_map/ppermute | solution.py:23
  125.2 0.3 shard_map.133
  125.6 0.1 collective-permute-start.35
  125.6 3.0 %shard_map.130 = (f32[512,512]{1,0:T(8,128)S(1)}, bf16[512,512]{1,0:T(8,128)(2,1)S(1)}) custom-call(s32[32]{0:T(128)S(1)} %pad_add_fusion.1.starts, bf16[512,2048]{1,0:T(8,128)(2,1)S(1)} %copy-done, bf16[512,512]{1,0:T(8,128)(2,1)S(1)} %get-tuple-element.29.k, bf16[512,512]{1,0:T(8,128)(2,1)S(1)} %get-tuple-element.30.v, ...), custom_call_target="tpu_custom_call" | custom-call | flops 1073741824 | bytes 8388608 | tf_op jit(solution)/shard_map/pallas_call | solution.py:210
  128.7 0.3 shard_map.131.mine
  129.0 3.2 %shard_map.134 = bf16[512,2048]{1,0:T(8,128)(2,1)} custom-call(s32[1]{0:T(128)} %bitcast.core_ref, bf16[512,512]{1,0:T(8,128)(2,1)S(1)} %shard_map.131.mine, bf16[512,512]{1,0:T(8,128)(2,1)S(1)} %collective-permute-done.35.theirs, bf16[1024,1024]{1,0:T(8,128)(2,1)S(1)} %get-tuple-element.44.w_mine, bf16[1024,1024]{1,0:T(8,128)(2,1)S(1)} %collective-permute-done.36.w_theirs), custom_call_target="tpu_custom_call" | custom-call | flops 2147483648 | bytes 8388608 | tf_op jit(solution)/shard_map/pallas_call | solution.py:210
  (55 shorter events, 0.3 us)
Async XLA Ops:
  0.0 41.8 %copy-start.7 = (pred[14]{0:T(512)(128)(4,1)S(1)}, pred[14]{0:T(512)(128)(4,1)}, u32[]{:S(2)}) copy-start(pred[14]{0:T(512)(128)(4,1)} %constant.69.clone) | copy-start | bytes 46
  0.0 41.8 %copy-start.8 = (f32[14]{0:T(128)S(1)}, f32[14]{0:T(128)}, u32[]{:S(2)}) copy-start(f32[14]{0:T(128)} %constant.70.clone) | copy-start | bytes 172
  0.0 41.8 %copy-start.9 = (s32[14]{0:T(128)S(1)}, s32[14]{0:T(128)}, u32[]{:S(2)}) copy-start(s32[14]{0:T(128)} %constant.68.clone) | copy-start | bytes 172
  0.0 49.8 %copy-start.10 = (s32[16]{0:T(128)S(1)}, s32[16]{0:T(128)}, u32[]{:S(2)}) copy-start(s32[16]{0:T(128)} %constant.74) | copy-start | bytes 196
  0.0 49.8 %copy-start.11 = (pred[16]{0:T(512)(128)(4,1)S(1)}, pred[16]{0:T(512)(128)(4,1)}, u32[]{:S(2)}) copy-start(pred[16]{0:T(512)(128)(4,1)} %constant.73) | copy-start | bytes 52
  0.0 49.8 %copy-start.12 = (s32[16]{0:T(128)S(1)}, s32[16]{0:T(128)}, u32[]{:S(2)}) copy-start(s32[16]{0:T(128)} %constant.71.clone) | copy-start | bytes 196
  0.0 64.1 %copy-start = (bf16[512,2048]{1,0:T(8,128)(2,1)S(1)}, bf16[512,2048]{1,0:T(8,128)(2,1)}, u32[]{:S(2)}) copy-start(bf16[512,2048]{1,0:T(8,128)(2,1)} %x.1) | copy-start | bytes 6291460
  0.0 64.0 %collective-permute-start.1 = (bf16[512,2048]{1,0:T(8,128)(2,1)}, bf16[512,2048]{1,0:T(8,128)(2,1)}, u32[]{:S(2)}, u32[]{:S(2)}) collective-permute-start(bf16[512,2048]{1,0:T(8,128)(2,1)} %x.1), channel_id=1, source_target_pairs={{0,1},{1,0},{2,3},{3,2},{4,5},{5,4},{6,7},{7,6},{8,9},{9,8},{10,11... | collective-permute-start | bytes 6291464 | tf_op jit(solution)/shard_map/ppermute | solution.py:23
  1.7 7.9 %collective-permute-start = (f32[14,2,512]{2,1,0:T(2,128)S(1)}, f32[14,2,512]{2,1,0:T(2,128)S(1)}, u32[]{:S(2)}, u32[]{:S(2)}) collective-permute-start(f32[14,2,512]{2,1,0:T(2,128)S(1)} %get-tuple-element.48), channel_id=1, source_target_pairs={{0,1},{1,0},{2,3},{3,2},{4,5},{5,4},{6,7},{7,6},{8,9},{9,8},{10,11... | collective-permute-start | bytes 172040 | tf_op jit(solution)/shard_map/ppermute | solution.py:23
  4.1 60.0 %copy-start.2 = (bf16[256,512]{1,0:T(8,128)(2,1)S(1)}, bf16[256,512]{1,0:T(8,128)(2,1)}, u32[]{:S(2)}) copy-start(bf16[256,512]{1,0:T(8,128)(2,1)} %get-tuple-element.25.refs_0_) | copy-start | bytes 786436
  4.1 9.4 %collective-permute-start.2 = (bf16[256,512]{1,0:T(8,128)(2,1)}, bf16[256,512]{1,0:T(8,128)(2,1)S(1)}, u32[]{:S(2)}, u32[]{:S(2)}) collective-permute-start(bf16[256,512]{1,0:T(8,128)(2,1)} %get-tuple-element.26), channel_id=1, source_target_pairs={{0,1},{1,0},{2,3},{3,2},{4,5},{5,4},{6,7},{7,6},{8,9},{9,8},{10,11... | collective-permute-start | bytes 786440 | tf_op jit(solution)/shard_map/ppermute | solution.py:23
  4.5 9.6 %collective-permute-start.3 = (bf16[256,512]{1,0:T(8,128)(2,1)}, bf16[256,512]{1,0:T(8,128)(2,1)S(1)}, u32[]{:S(2)}, u32[]{:S(2)}) collective-permute-start(bf16[256,512]{1,0:T(8,128)(2,1)} %get-tuple-element.27), channel_id=1, source_target_pairs={{0,2},{1,3},{2,0},{3,1},{4,6},{5,7},{6,4},{7,5},{8,10},{9,11},{10,... | collective-permute-start | bytes 786440 | tf_op jit(solution)/shard_map/ppermute | solution.py:33
  7.1 16.0 %collective-permute-start.5 = (bf16[256,512]{1,0:T(8,128)(2,1)}, bf16[256,512]{1,0:T(8,128)(2,1)S(1)}, u32[]{:S(2)}, u32[]{:S(2)}) collective-permute-start(bf16[256,512]{1,0:T(8,128)(2,1)} %get-tuple-element.27), channel_id=1, source_target_pairs={{0,8},{1,9},{2,10},{3,11},{4,12},{5,13},{6,14},{7,15},{8,0},{9,1},... | collective-permute-start | bytes 786440 | tf_op jit(solution)/shard_map/ppermute | solution.py:33
  9.7 19.6 %collective-permute-start.9 = (bf16[256,512]{1,0:T(8,128)(2,1)}, bf16[256,512]{1,0:T(8,128)(2,1)}, u32[]{:S(2)}, u32[]{:S(2)}) collective-permute-start(bf16[256,512]{1,0:T(8,128)(2,1)} %get-tuple-element.27), channel_id=1, source_target_pairs={{0,4},{1,5},{2,6},{3,7},{4,0},{5,1},{6,2},{7,3},{8,12},{9,13},{10,... | collective-permute-start | bytes 786440 | tf_op jit(solution)/shard_map/ppermute | solution.py:33
  13.5 19.0 %collective-permute-start.10 = (bf16[256,512]{1,0:T(8,128)(2,1)}, bf16[256,512]{1,0:T(8,128)(2,1)}, u32[]{:S(2)}, u32[]{:S(2)}) collective-permute-start(bf16[256,512]{1,0:T(8,128)(2,1)} %get-tuple-element.28), channel_id=1, source_target_pairs={{0,5},{1,4},{2,7},{3,6},{4,1},{5,0},{6,3},{7,2},{8,13},{9,12},{10,... | collective-permute-start | bytes 786440 | tf_op jit(solution)/shard_map/ppermute | solution.py:33
  14.1 35.9 %copy-start.3 = (bf16[256,512]{1,0:T(8,128)(2,1)}, bf16[256,512]{1,0:T(8,128)(2,1)S(1)}, u32[]{:S(2)}) copy-start(bf16[256,512]{1,0:T(8,128)(2,1)S(1)} %collective-permute-done.3.refs_2_) | copy-start | bytes 786436
  14.1 22.0 %collective-permute-start.22 = (bf16[256,512]{1,0:T(8,128)(2,1)}, bf16[256,512]{1,0:T(8,128)(2,1)S(1)}, u32[]{:S(2)}, u32[]{:S(2)}) collective-permute-start(bf16[256,512]{1,0:T(8,128)(2,1)} %get-tuple-element.35), channel_id=1, source_target_pairs={{0,8},{1,9},{2,10},{3,11},{4,12},{5,13},{6,14},{7,15},{8,0},{9,1},... | collective-permute-start | bytes 786440 | tf_op jit(solution)/shard_map/ppermute | solution.py:33
  23.1 26.9 %copy-start.5 = (bf16[256,512]{1,0:T(8,128)(2,1)}, bf16[256,512]{1,0:T(8,128)(2,1)S(1)}, u32[]{:S(2)}) copy-start(bf16[256,512]{1,0:T(8,128)(2,1)S(1)} %collective-permute-done.5.refs_4_) | copy-start | bytes 786436
  23.1 13.5 %collective-permute-start.4 = (bf16[256,512]{1,0:T(8,128)(2,1)S(1)}, bf16[256,512]{1,0:T(8,128)(2,1)}, u32[]{:S(2)}, u32[]{:S(2)}) collective-permute-start(bf16[256,512]{1,0:T(8,128)(2,1)S(1)} %collective-permute-done.3.refs_2_), channel_id=1, source_target_pairs={{0,16},{16,0},{1,17},{17,1},{2,18},{18,2},{3,19},{19,3},{4,20},{20... | collective-permute-start | bytes 786440 | tf_op jit(solution)/shard_map/ppermute | solution.py:37
  29.3 11.2 %collective-permute-start.13 = (bf16[256,512]{1,0:T(8,128)(2,1)S(1)}, bf16[256,512]{1,0:T(8,128)(2,1)}, u32[]{:S(2)}, u32[]{:S(2)}) collective-permute-start(bf16[256,512]{1,0:T(8,128)(2,1)S(1)} %collective-permute-done.5.refs_4_), channel_id=1, source_target_pairs={{0,4},{1,5},{2,6},{3,7},{4,0},{5,1},{6,2},{7,3},{8,12},{9,13},{10,... | collective-permute-start | bytes 786440 | tf_op jit(solution)/shard_map/ppermute | solution.py:23
  32.5 10.8 %collective-permute-start.6 = (bf16[256,512]{1,0:T(8,128)(2,1)S(1)}, bf16[256,512]{1,0:T(8,128)(2,1)}, u32[]{:S(2)}, u32[]{:S(2)}) collective-permute-start(bf16[256,512]{1,0:T(8,128)(2,1)S(1)} %collective-permute-done.5.refs_4_), channel_id=1, source_target_pairs={{0,16},{16,0},{1,17},{17,1},{2,18},{18,2},{3,19},{19,3},{4,20},{20... | collective-permute-start | bytes 786440 | tf_op jit(solution)/shard_map/ppermute | solution.py:37
  36.1 7.8 %collective-permute-start.7 = (bf16[256,512]{1,0:T(8,128)(2,1)S(1)}, bf16[256,512]{1,0:T(8,128)(2,1)}, u32[]{:S(2)}, u32[]{:S(2)}) collective-permute-start(bf16[256,512]{1,0:T(8,128)(2,1)S(1)} %collective-permute-done.5.refs_4_), channel_id=1, source_target_pairs={{0,2},{1,3},{2,0},{3,1},{4,6},{5,7},{6,4},{7,5},{8,10},{9,11},{10,... | collective-permute-start | bytes 786440 | tf_op jit(solution)/shard_map/ppermute | solution.py:23
  36.6 8.8 %collective-permute-start.11 = (bf16[256,512]{1,0:T(8,128)(2,1)S(1)}, bf16[256,512]{1,0:T(8,128)(2,1)}, u32[]{:S(2)}, u32[]{:S(2)}) collective-permute-start(bf16[256,512]{1,0:T(8,128)(2,1)S(1)} %collective-permute-done.3.refs_2_), channel_id=1, source_target_pairs={{0,4},{1,5},{2,6},{3,7},{4,0},{5,1},{6,2},{7,3},{8,12},{9,13},{10,... | collective-permute-start | bytes 786440 | tf_op jit(solution)/shard_map/ppermute | solution.py:23
  40.5 9.3 %collective-permute-start.14 = (bf16[256,512]{1,0:T(8,128)(2,1)}, bf16[256,512]{1,0:T(8,128)(2,1)}, u32[]{:S(2)}, u32[]{:S(2)}) collective-permute-start(bf16[256,512]{1,0:T(8,128)(2,1)} %collective-permute-done.13.refs_12_), channel_id=1, source_target_pairs={{0,16},{16,0},{1,17},{17,1},{2,18},{18,2},{3,19},{19,3},{4,20},{20... | collective-permute-start | bytes 786440 | tf_op jit(solution)/shard_map/ppermute | solution.py:37
  43.3 9.5 %collective-permute-start.12 = (bf16[256,512]{1,0:T(8,128)(2,1)}, bf16[256,512]{1,0:T(8,128)(2,1)}, u32[]{:S(2)}, u32[]{:S(2)}) collective-permute-start(bf16[256,512]{1,0:T(8,128)(2,1)} %collective-permute-done.10.refs_9_), channel_id=1, source_target_pairs={{0,2},{1,3},{2,0},{3,1},{4,6},{5,7},{6,4},{7,5},{8,10},{9,11},{10,... | collective-permute-start | bytes 786440 | tf_op jit(solution)/shard_map/ppermute | solution.py:23
  43.8 14.6 %collective-permute-start.15 = (bf16[256,512]{1,0:T(8,128)(2,1)}, bf16[256,512]{1,0:T(8,128)(2,1)}, u32[]{:S(2)}, u32[]{:S(2)}) collective-permute-start(bf16[256,512]{1,0:T(8,128)(2,1)} %collective-permute-done.13.refs_12_), channel_id=1, source_target_pairs={{0,2},{1,3},{2,0},{3,1},{4,6},{5,7},{6,4},{7,5},{8,10},{9,11},{10,... | collective-permute-start | bytes 786440 | tf_op jit(solution)/shard_map/ppermute | solution.py:23
  45.4 8.9 %collective-permute-start.8 = (bf16[256,512]{1,0:T(8,128)(2,1)}, bf16[256,512]{1,0:T(8,128)(2,1)}, u32[]{:S(2)}, u32[]{:S(2)}) collective-permute-start(bf16[256,512]{1,0:T(8,128)(2,1)} %collective-permute-done.7.refs_6_), channel_id=1, source_target_pairs={{0,16},{16,0},{1,17},{17,1},{2,18},{18,2},{3,19},{19,3},{4,20},{20... | collective-permute-start | bytes 786440 | tf_op jit(solution)/shard_map/ppermute | solution.py:37
  49.8 14.3 %collective-permute-start.16 = (bf16[256,512]{1,0:T(8,128)(2,1)}, bf16[256,512]{1,0:T(8,128)(2,1)}, u32[]{:S(2)}, u32[]{:S(2)}) collective-permute-start(bf16[256,512]{1,0:T(8,128)(2,1)} %collective-permute-done.14.refs_13_), channel_id=1, source_target_pairs={{0,2},{1,3},{2,0},{3,1},{4,6},{5,7},{6,4},{7,5},{8,10},{9,11},{10,... | collective-permute-start | bytes 786440 | tf_op jit(solution)/shard_map/ppermute | solution.py:23
  52.8 21.4 %collective-permute-start.20 = (bf16[256,512]{1,0:T(8,128)(2,1)}, bf16[256,512]{1,0:T(8,128)(2,1)S(1)}, u32[]{:S(2)}, u32[]{:S(2)}) collective-permute-start(bf16[256,512]{1,0:T(8,128)(2,1)} %get-tuple-element.35), channel_id=1, source_target_pairs={{0,2},{1,3},{2,0},{3,1},{4,6},{5,7},{6,4},{7,5},{8,10},{9,11},{10,... | collective-permute-start | bytes 786440 | tf_op jit(solution)/shard_map/ppermute | solution.py:33
  54.3 22.1 %collective-permute-start.26 = (bf16[256,512]{1,0:T(8,128)(2,1)}, bf16[256,512]{1,0:T(8,128)(2,1)S(1)}, u32[]{:S(2)}, u32[]{:S(2)}) collective-permute-start(bf16[256,512]{1,0:T(8,128)(2,1)} %get-tuple-element.35), channel_id=1, source_target_pairs={{0,4},{1,5},{2,6},{3,7},{4,0},{5,1},{6,2},{7,3},{8,12},{9,13},{10,... | collective-permute-start | bytes 786440 | tf_op jit(solution)/shard_map/ppermute | solution.py:33
  58.4 15.2 %collective-permute-start.19 = (bf16[256,512]{1,0:T(8,128)(2,1)}, bf16[256,512]{1,0:T(8,128)(2,1)S(1)}, u32[]{:S(2)}, u32[]{:S(2)}) collective-permute-start(bf16[256,512]{1,0:T(8,128)(2,1)} %get-tuple-element.34), channel_id=1, source_target_pairs={{0,1},{1,0},{2,3},{3,2},{4,5},{5,4},{6,7},{7,6},{8,9},{9,8},{10,11... | collective-permute-start | bytes 786440 | tf_op jit(solution)/shard_map/ppermute | solution.py:23
  64.1 13.8 %collective-permute-start.27 = (bf16[256,512]{1,0:T(8,128)(2,1)}, bf16[256,512]{1,0:T(8,128)(2,1)S(1)}, u32[]{:S(2)}, u32[]{:S(2)}) collective-permute-start(bf16[256,512]{1,0:T(8,128)(2,1)} %get-tuple-element.36), channel_id=1, source_target_pairs={{0,5},{1,4},{2,7},{3,6},{4,1},{5,0},{6,3},{7,2},{8,13},{9,12},{10,... | collective-permute-start | bytes 786440 | tf_op jit(solution)/shard_map/ppermute | solution.py:33
  64.1 14.2 %collective-permute-start.30 = (bf16[256,512]{1,0:T(8,128)(2,1)S(1)}, bf16[256,512]{1,0:T(8,128)(2,1)S(1)}, u32[]{:S(2)}, u32[]{:S(2)}) collective-permute-start(bf16[256,512]{1,0:T(8,128)(2,1)S(1)} %collective-permute-done.22.refs_6_), channel_id=1, source_target_pairs={{0,4},{1,5},{2,6},{3,7},{4,0},{5,1},{6,2},{7,3},{8,12},{9,13},{10,... | collective-permute-start | bytes 786440 | tf_op jit(solution)/shard_map/ppermute | solution.py:23
  64.1 1.0 copy-start.4
  65.0 0.9 copy-start.6
  66.0 39.5 %copy-start.1 = (bf16[256,512]{1,0:T(8,128)(2,1)S(1)}, bf16[256,512]{1,0:T(8,128)(2,1)}, u32[]{:S(2)}) copy-start(bf16[256,512]{1,0:T(8,128)(2,1)} %get-tuple-element.33.refs_2_) | copy-start | bytes 786436
  73.6 8.4 %collective-permute-start.17 = (bf16[2,256,256]{2,1,0:T(8,128)(2,1)S(1)}, bf16[2,256,256]{2,1,0:T(8,128)(2,1)S(1)}, u32[]{:S(2)}, u32[]{:S(2)}) collective-permute-start(bf16[2,256,256]{2,1,0:T(8,128)(2,1)S(1)} %get-tuple-element.32), channel_id=1, source_target_pairs={{0,2},{1,3},{2,0},{3,1},{4,6},{5,7},{6,4},{7,5},{8,10},{9,11},{10,... | collective-permute-start | bytes 786440 | tf_op jit(solution)/shard_map/ppermute | solution.py:23
  74.2 10.1 %collective-permute-start.21 = (bf16[256,512]{1,0:T(8,128)(2,1)S(1)}, bf16[256,512]{1,0:T(8,128)(2,1)S(1)}, u32[]{:S(2)}, u32[]{:S(2)}) collective-permute-start(bf16[256,512]{1,0:T(8,128)(2,1)S(1)} %collective-permute-done.20.refs_4_), channel_id=1, source_target_pairs={{0,16},{16,0},{1,17},{17,1},{2,18},{18,2},{3,19},{19,3},{4,20},{20... | collective-permute-start | bytes 786440 | tf_op jit(solution)/shard_map/ppermute | solution.py:37
  76.3 11.3 %collective-permute-start.24 = (bf16[256,512]{1,0:T(8,128)(2,1)S(1)}, bf16[256,512]{1,0:T(8,128)(2,1)S(1)}, u32[]{:S(2)}, u32[]{:S(2)}) collective-permute-start(bf16[256,512]{1,0:T(8,128)(2,1)S(1)} %collective-permute-done.22.refs_6_), channel_id=1, source_target_pairs={{0,2},{1,3},{2,0},{3,1},{4,6},{5,7},{6,4},{7,5},{8,10},{9,11},{10,... | collective-permute-start | bytes 786440 | tf_op jit(solution)/shard_map/ppermute | solution.py:23
  77.9 10.0 %collective-permute-start.28 = (bf16[256,512]{1,0:T(8,128)(2,1)S(1)}, bf16[256,512]{1,0:T(8,128)(2,1)S(1)}, u32[]{:S(2)}, u32[]{:S(2)}) collective-permute-start(bf16[256,512]{1,0:T(8,128)(2,1)S(1)} %collective-permute-done.20.refs_4_), channel_id=1, source_target_pairs={{0,4},{1,5},{2,6},{3,7},{4,0},{5,1},{6,2},{7,3},{8,12},{9,13},{10,... | collective-permute-start | bytes 786440 | tf_op jit(solution)/shard_map/ppermute | solution.py:23
  78.3 11.4 %collective-permute-start.31 = (bf16[256,512]{1,0:T(8,128)(2,1)S(1)}, bf16[256,512]{1,0:T(8,128)(2,1)S(1)}, u32[]{:S(2)}, u32[]{:S(2)}) collective-permute-start(bf16[256,512]{1,0:T(8,128)(2,1)S(1)} %collective-permute-done.30.refs_14_), channel_id=1, source_target_pairs={{0,16},{16,0},{1,17},{17,1},{2,18},{18,2},{3,19},{19,3},{4,20},{20... | collective-permute-start | bytes 786440 | tf_op jit(solution)/shard_map/ppermute | solution.py:37
  82.0 12.2 %collective-permute-start.23 = (bf16[256,512]{1,0:T(8,128)(2,1)S(1)}, bf16[256,512]{1,0:T(8,128)(2,1)S(1)}, u32[]{:S(2)}, u32[]{:S(2)}) collective-permute-start(bf16[256,512]{1,0:T(8,128)(2,1)S(1)} %collective-permute-done.22.refs_6_), channel_id=1, source_target_pairs={{0,16},{16,0},{1,17},{17,1},{2,18},{18,2},{3,19},{19,3},{4,20},{20... | collective-permute-start | bytes 786440 | tf_op jit(solution)/shard_map/ppermute | solution.py:37
  84.3 21.1 %collective-permute-start.32 = (bf16[256,512]{1,0:T(8,128)(2,1)S(1)}, bf16[256,512]{1,0:T(8,128)(2,1)S(1)}, u32[]{:S(2)}, u32[]{:S(2)}) collective-permute-start(bf16[256,512]{1,0:T(8,128)(2,1)S(1)} %collective-permute-done.30.refs_14_), channel_id=1, source_target_pairs={{0,2},{1,3},{2,0},{3,1},{4,6},{5,7},{6,4},{7,5},{8,10},{9,11},{10,... | collective-permute-start | bytes 786440 | tf_op jit(solution)/shard_map/ppermute | solution.py:23
  87.6 12.2 %collective-permute-start.25 = (bf16[256,512]{1,0:T(8,128)(2,1)S(1)}, bf16[256,512]{1,0:T(8,128)(2,1)S(1)}, u32[]{:S(2)}, u32[]{:S(2)}) collective-permute-start(bf16[256,512]{1,0:T(8,128)(2,1)S(1)} %collective-permute-done.24.refs_8_), channel_id=1, source_target_pairs={{0,16},{16,0},{1,17},{17,1},{2,18},{18,2},{3,19},{19,3},{4,20},{20... | collective-permute-start | bytes 786440 | tf_op jit(solution)/shard_map/ppermute | solution.py:37
  87.8 17.7 %collective-permute-start.29 = (bf16[256,512]{1,0:T(8,128)(2,1)S(1)}, bf16[256,512]{1,0:T(8,128)(2,1)S(1)}, u32[]{:S(2)}, u32[]{:S(2)}) collective-permute-start(bf16[256,512]{1,0:T(8,128)(2,1)S(1)} %collective-permute-done.28.refs_12_), channel_id=1, source_target_pairs={{0,16},{16,0},{1,17},{17,1},{2,18},{18,2},{3,19},{19,3},{4,20},{20... | collective-permute-start | bytes 786440 | tf_op jit(solution)/shard_map/ppermute | solution.py:37
  89.7 15.8 %collective-permute-start.33 = (bf16[256,512]{1,0:T(8,128)(2,1)S(1)}, bf16[256,512]{1,0:T(8,128)(2,1)S(1)}, u32[]{:S(2)}, u32[]{:S(2)}) collective-permute-start(bf16[256,512]{1,0:T(8,128)(2,1)S(1)} %collective-permute-done.31.refs_15_), channel_id=1, source_target_pairs={{0,2},{1,3},{2,0},{3,1},{4,6},{5,7},{6,4},{7,5},{8,10},{9,11},{10,... | collective-permute-start | bytes 786440 | tf_op jit(solution)/shard_map/ppermute | solution.py:23
  94.3 11.2 %collective-permute-start.18 = (bf16[2,256,256]{2,1,0:T(8,128)(2,1)S(1)}, bf16[2,256,256]{2,1,0:T(8,128)(2,1)S(1)}, u32[]{:S(2)}, u32[]{:S(2)}) collective-permute-start(bf16[2,256,256]{2,1,0:T(8,128)(2,1)S(1)} %add_convert_fusion.1), channel_id=1, source_target_pairs={{0,4},{1,5},{2,6},{3,7},{4,0},{5,1},{6,2},{7,3},{8,12},{9,13},{10,... | collective-permute-start | bytes 786440 | tf_op jit(solution)/shard_map/ppermute | solution.py:23
  109.8 19.2 %collective-permute-start.36 = (bf16[1024,1024]{1,0:T(8,128)(2,1)S(1)}, bf16[1024,1024]{1,0:T(8,128)(2,1)S(1)}, u32[]{:S(2)}, u32[]{:S(2)}) collective-permute-start(bf16[1024,1024]{1,0:T(8,128)(2,1)S(1)} %get-tuple-element.44.w_mine), channel_id=1, source_target_pairs={{0,1},{1,0},{2,3},{3,2},{4,5},{5,4},{6,7},{7,6},{8,9},{9,8},{10,11... | collective-permute-start | bytes 6291464 | tf_op jit(solution)/shard_map/ppermute | solution.py:23
  110.2 15.0 %collective-permute-start.34 = (bf16[2,256,256]{2,1,0:T(8,128)(2,1)S(1)}, bf16[2,256,256]{2,1,0:T(8,128)(2,1)S(1)}, u32[]{:S(2)}, u32[]{:S(2)}) collective-permute-start(bf16[2,256,256]{2,1,0:T(8,128)(2,1)S(1)} %add_convert_fusion), channel_id=1, source_target_pairs={{0,8},{1,9},{2,10},{3,11},{4,12},{5,13},{6,14},{7,15},{8,0},{9,1},... | collective-permute-start | bytes 786440 | tf_op jit(solution)/shard_map/ppermute | solution.py:23
  125.6 3.5 %collective-permute-start.35 = (bf16[512,512]{1,0:T(8,128)(2,1)S(1)}, bf16[512,512]{1,0:T(8,128)(2,1)S(1)}, u32[]{:S(2)}, u32[]{:S(2)}) collective-permute-start(bf16[512,512]{1,0:T(8,128)(2,1)S(1)} %shard_map.133), channel_id=1, source_target_pairs={{0,1},{1,0},{2,3},{3,2},{4,5},{5,4},{6,7},{7,6},{8,9},{9,8},{10,11... | collective-permute-start | bytes 1572872 | tf_op jit(solution)/shard_map/ppermute | solution.py:23

commit v4 on v3

--- a/solution.py
+++ b/solution.py
@@ -108,7 +108,7 @@
 def keys_values_kernel(n, rows, heads, starts, xa, xb, scale, *refs):
     del scale
     pieces = refs[:n]
-    ka, kb, va, vb, da, db, sent, wk, wv = refs[n:]
+    ka, kb, va, vb, da, db, *sent, wk, wv = refs[n:]
     everything = slice(None)
     place_rows(wk, pieces, rows, everything, starts, 0, rows)
     place_rows(wv, pieces, 0, everything, starts, 0, rows)
@@ -124,7 +124,7 @@
             device_sum[h] = state.astype(BF16)
             sums[h] = state if i == 0 else sums[h] + state
     for h in range(heads):
-        sent[h] = sums[h].astype(BF16)
+        sent[h][...] = sums[h].astype(BF16)
 
 
 def attend_kernel(which, n, nb, rows, out_rows, heads, levels, local_bits, starts, x, k, v, other, scale, *refs):
@@ -167,17 +167,18 @@
                     base = (c >> b) << b
                     bucket = sum(states[base + 1 : base + half], states[base])
                     value = value + dot(qh, bucket.astype(BF16)) * weight(CBITS + b)
-            for at, bucket in enumerate((other, *buckets)):
-                value = value + dot(qh, bucket[h]) * weight(first + at)
+            for at, bucket in enumerate((other.at[h], *buckets[h::heads])):
+                value = value + dot(qh, bucket[...]) * weight(first + at)
             out[span, cols] = value
 
 
-def reads_kernel(which, heads, levels, level, scale, part, q, bucket, out):
+def reads_kernel(which, heads, levels, level, scale, part, q, *refs):
+    buckets, out = refs[:-1], refs[-1]
     for h in range(heads):
         cols = slice(h * HEAD, (h + 1) * HEAD)
         at = h * levels + level
         weight = scale[which, :, at : at + 1]
-        out[:, cols] = (part[:, cols] + dot(q[:, cols], bucket[h]) * weight).astype(BF16)
+        out[:, cols] = (part[:, cols] + dot(q[:, cols], buckets[h][...]) * weight).astype(BF16)
 
 
 def output_kernel(width, core_ref, mine, theirs, w_mine, w_theirs, out, block, sem):
@@ -268,20 +269,21 @@
 
     act = sd((toks, cols), BF16)
     state = sd((heads, HEAD, HEAD), BF16)
-    ka, kb, va, vb, da, db, total = call(
+    ka, kb, va, vb, da, db, *totals = call(
         functools.partial(keys_values_kernel, len(kvp), rows, heads),
         [first_rows(kvp, rows, device, sent_core), tokens, far_tokens, scale, *(piece[0] for piece in kvp)],
-        [FAST] * 7,
-        [act] * 4 + [state] * 3,
+        [FAST] * (6 + heads),
+        [act] * 4 + [state] * 2 + [sd((HEAD, HEAD), BF16)] * heads,
         [pltpu.VMEM((width, cols), BF16), pltpu.VMEM((width, cols), BF16)],
         2 * 2 * toks * width * 2 * cols,
     )
 
     buckets = []
     for bit in range(1, seq_bits):
-        arrived = swap(total, bit)
-        buckets.append(arrived)
-        total = (total.astype(F32) + arrived.astype(F32)).astype(BF16)
+        for h in range(heads):
+            arrived = swap(totals[h], bit)
+            buckets.append(arrived)
+            totals[h] = (totals[h].astype(F32) + arrived.astype(F32)).astype(BF16)
 
     starts = jnp.concatenate(
         [first_rows(qop, rows, device, sent_core), first_rows(qop, out_rows, device, sent_core)]
@@ -291,9 +293,9 @@
         shapes = [sd((toks, cols), F32), act] + [sd((head_cols, out_cols), BF16)] * which
         return call(
             functools.partial(
-                attend_kernel, which, len(qop), len(buckets) - 1, rows, out_rows, heads, levels, local_bits
+                attend_kernel, which, len(qop), len(buckets) - heads, rows, out_rows, heads, levels, local_bits
             ),
-            [starts, x, k, v, other, scale, *buckets[:-1], *(piece[0] for piece in qop)],
+            [starts, x, k, v, other, scale, *buckets[:-heads], *(piece[0] for piece in qop)],
             [FAST] * len(shapes),
             shapes,
             [pltpu.VMEM((width, cols), BF16)],
@@ -303,12 +305,12 @@
     def read(which, part, q):
         return pl.pallas_call(
             functools.partial(reads_kernel, which, heads, levels, first_bit + seq_bits - 1),
-            in_specs=[FAST] * 4,
+            in_specs=[FAST] * (3 + heads),
             out_specs=FAST,
             out_shape=act,
             compiler_params=pltpu.CompilerParams(vmem_limit_bytes=8 << 20),
             cost_estimate=pl.CostEstimate(flops=1 << 28, bytes_accessed=2 << 20, transcendentals=0),
-        )(scale, part, q, buckets[-1])
+        )(scale, part, q, *buckets[-heads:])
 
     far_part, far_q, w_mine = attend(1, far_tokens, kb, vb, da)
     w_theirs = swap(w_mine, 0)

time: 133 us -> 139 us (1.045)
  starting transfers between devices: 36.8 us -> 39.2 us
  waiting for transfers between devices: 68.1 us -> 70.2 us
  local copies, waits for them, and re-layouts: 3.34 us -> 4.93 us
    ppermute x20 -> x23, starting transfers between devices: 11.8 us -> 19.7 us  [swap(): lax.ppermute(value, 'seq', [(i, i ^ mask) for i in range(lax.axis_size('s...]
    ppermute x8, waiting for transfers between devices: 15.7 us -> 20 us  [swap_crossed(): return lax.ppermute(value, ('group', 'seq'), pairs)]
    ppermute x8, starting transfers between devices: 10.5 us -> 6.73 us  [swap_crossed(): return lax.ppermute(value, ('group', 'seq'), pairs)]
    ppermute x20 -> x23, waiting for transfers between devices: 34.1 us -> 31.7 us  [swap(): lax.ppermute(value, 'seq', [(i, i ^ mask) for i in range(lax.axis_size('s...]
    ppermute x9, starting transfers between devices: 14.5 us -> 12.8 us  [swap_x(): lax.ppermute(value, 'group', [(i, i ^ 1) for i in range(lax.axis_size('gr...]
    unnamed x26 -> x30, local copies, waits for them, and re-layouts: 1.94 us -> 3.6 us
  transfers between devices with their start and end apart: 37 -> 40, of which waited for: 17 -> 19; matrix products, arithmetic and copies ran while one was open for 1% -> 1% of each run, Pallas kernels for 12% -> 12%
where the time goes in v4:
time: 139 us
  waiting for transfers between devices  70.2 us (51%)
  starting transfers between devices  39.2 us (28%)
  Pallas kernels  23.5 us (17%)
  local copies, waits for them, and re-layouts  4.93 us (4%)
    ppermute x23, waiting for transfers between devices, swap(): lax.ppermute(value, 'seq', [(i, i ^ mask) for i in range(lax.axis_size('s...  31.7 us
    ppermute x8, waiting for transfers between devices, swap_crossed(): return lax.ppermute(value, ('group', 'seq'), pairs)  20 us
    ppermute x23, starting transfers between devices, swap(): lax.ppermute(value, 'seq', [(i, i ^ mask) for i in range(lax.axis_size('s...  19.7 us
    ppermute x9, waiting for transfers between devices, swap_x(): lax.ppermute(value, 'group', [(i, i ^ 1) for i in range(lax.axis_size('gr...  18.5 us
    pallas_call x4, Pallas kernels, call(): pl.pallas_call(kernel, in_specs=[SMALL] + [FAST] * (len(operands) - 1), o...  18.2 us
    ppermute x9, starting transfers between devices, swap_x(): lax.ppermute(value, 'group', [(i, i ^ 1) for i in range(lax.axis_size('gr...  12.8 us
    ppermute x8, starting transfers between devices, swap_crossed(): return lax.ppermute(value, ('group', 'seq'), pairs)  6.73 us
    pallas_call x2, Pallas kernels, split(): pl.pallas_call(functools.partial(split_kernel, parts, cols), out_shape=[s...  4.67 us
  transfers between devices with their start and end apart: 40, of which 19 were waited for; matrix products, arithmetic and copies ran while one was open for 1% of the time, Pallas kernels for 12%

profile of v4, /device:TPU:0, one launch (start us, length us, event | category | flops | bytes accessed | tf_op | source)
XLA Modules:
  0.0 138.8 jit_solution(3849680769560010772)
XLA Ops:
  0.0 0.6 collective-permute-start.1
  0.6 2.3 %shard_map.127 = (bf16[256,512]{1,0:T(8,128)(2,1)}, bf16[256,512]{1,0:T(8,128)(2,1)}, bf16[256,512]{1,0:T(8,128)(2,1)}, bf16[256,512]{1,0:T(8,128)(2,1)}) custom-call(bf16[128,3072]{1,0:T(8,128)(2,1)} %refs_0_.3), custom_call_target="tpu_custom_call" | custom-call | flops 1048576 | bytes 2097152 | tf_op jit(solution)/shard_map/pallas_call | solution.py:242
  3.0 1.0 dynamic-slice_bitcast_fusion
  4.0 0.5 collective-permute-start
  4.5 2.6 %collective-permute-start.3 = (bf16[256,512]{1,0:T(8,128)(2,1)}, bf16[256,512]{1,0:T(8,128)(2,1)S(1)}, u32[]{:S(2)}, u32[]{:S(2)}) collective-permute-start(bf16[256,512]{1,0:T(8,128)(2,1)} %get-tuple-element.28), channel_id=1, source_target_pairs={{0,2},{1,3},{2,0},{3,1},{4,6},{5,7},{6,4},{7,5},{8,10},{9,11},{10,... | collective-permute-start | bytes 786440 | tf_op jit(solution)/shard_map/ppermute | solution.py:33
  7.1 2.6 %collective-permute-start.5 = (bf16[256,512]{1,0:T(8,128)(2,1)}, bf16[256,512]{1,0:T(8,128)(2,1)S(1)}, u32[]{:S(2)}, u32[]{:S(2)}) collective-permute-start(bf16[256,512]{1,0:T(8,128)(2,1)} %get-tuple-element.28), channel_id=1, source_target_pairs={{0,8},{1,9},{2,10},{3,11},{4,12},{5,13},{6,14},{7,15},{8,0},{9,1},... | collective-permute-start | bytes 786440 | tf_op jit(solution)/shard_map/ppermute | solution.py:33
  9.7 1.6 %collective-permute-start.9 = (bf16[256,512]{1,0:T(8,128)(2,1)}, bf16[256,512]{1,0:T(8,128)(2,1)}, u32[]{:S(2)}, u32[]{:S(2)}) collective-permute-start(bf16[256,512]{1,0:T(8,128)(2,1)} %get-tuple-element.28), channel_id=1, source_target_pairs={{0,4},{1,5},{2,6},{3,7},{4,0},{5,1},{6,2},{7,3},{8,12},{9,13},{10,... | collective-permute-start | bytes 786440 | tf_op jit(solution)/shard_map/ppermute | solution.py:33
  11.3 2.4 %shard_map.129 = (bf16[256,512]{1,0:T(8,128)(2,1)}, bf16[256,512]{1,0:T(8,128)(2,1)}, bf16[256,512]{1,0:T(8,128)(2,1)}, bf16[256,512]{1,0:T(8,128)(2,1)}) custom-call(bf16[128,3072]{1,0:T(8,128)(2,1)} %refs_0_.3, bf16[64,2048]{1,0:T(8,128)(2,1)} %refs_1_.1), custom_call_target="tpu_custom_call" | custom-call | flops 1048576 | bytes 2097152 | tf_op jit(solution)/shard_map/pallas_call | solution.py:242
  13.6 0.5 collective-permute-done.3.refs_2_
  14.1 8.1 %collective-permute-done.5.refs_4_ = bf16[256,512]{1,0:T(8,128)(2,1)S(1)} collective-permute-done((bf16[256,512]{1,0:T(8,128)(2,1)}, bf16[256,512]{1,0:T(8,128)(2,1)S(1)}, u32[]{:S(2)}, u32[]{:S(2)}) %collective-permute-start.5) | collective-permute-done | bytes 262176 | tf_op jit(solution)/shard_map/ppermute | solution.py:33
  22.2 0.7 copy-done.7
  22.9 0.7 collective-permute-done.9.refs_8_
  23.7 0.7 collective-permute-start.4
  24.3 5.6 %collective-permute-done.10.refs_9_ = bf16[256,512]{1,0:T(8,128)(2,1)} collective-permute-done((bf16[256,512]{1,0:T(8,128)(2,1)}, bf16[256,512]{1,0:T(8,128)(2,1)}, u32[]{:S(2)}, u32[]{:S(2)}) %collective-permute-start.10) | collective-permute-done | bytes 262176 | tf_op jit(solution)/shard_map/ppermute | solution.py:33
  30.0 0.7 collective-permute-start.13
  30.7 1.4 %collective-permute-start.6 = (bf16[256,512]{1,0:T(8,128)(2,1)}, bf16[256,512]{1,0:T(8,128)(2,1)}, u32[]{:S(2)}, u32[]{:S(2)}) collective-permute-start(bf16[256,512]{1,0:T(8,128)(2,1)} %copy-done.7), channel_id=1, source_target_pairs={{0,16},{16,0},{1,17},{17,1},{2,18},{18,2},{3,19},{19,3},{4,20},{20... | collective-permute-start | bytes 786440 | tf_op jit(solution)/shard_map/ppermute | solution.py:37
  32.1 5.1 %collective-permute-done.24.refs_8_ = bf16[256,512]{1,0:T(8,128)(2,1)S(1)} collective-permute-done((bf16[256,512]{1,0:T(8,128)(2,1)}, bf16[256,512]{1,0:T(8,128)(2,1)S(1)}, u32[]{:S(2)}, u32[]{:S(2)}) %collective-permute-start.24) | collective-permute-done | bytes 262176 | tf_op jit(solution)/shard_map/ppermute | solution.py:33
  37.2 0.7 collective-permute-start.7
  37.9 1.2 collective-permute-start.11
  39.1 2.7 %collective-permute-done.13.refs_12_ = bf16[256,512]{1,0:T(8,128)(2,1)} collective-permute-done((bf16[256,512]{1,0:T(8,128)(2,1)}, bf16[256,512]{1,0:T(8,128)(2,1)}, u32[]{:S(2)}, u32[]{:S(2)}) %collective-permute-start.13) | collective-permute-done | bytes 262176 | tf_op jit(solution)/shard_map/ppermute | solution.py:23
  41.8 2.9 %collective-permute-start.14 = (bf16[256,512]{1,0:T(8,128)(2,1)}, bf16[256,512]{1,0:T(8,128)(2,1)}, u32[]{:S(2)}, u32[]{:S(2)}) collective-permute-start(bf16[256,512]{1,0:T(8,128)(2,1)} %collective-permute-done.13.refs_12_), channel_id=1, source_target_pairs={{0,16},{16,0},{1,17},{17,1},{2,18},{18,2},{3,19},{19,3},{4,20},{20... | collective-permute-start | bytes 786440 | tf_op jit(solution)/shard_map/ppermute | solution.py:37
  44.7 0.1 pad_add_fusion
  44.9 2.0 %collective-permute-start.15 = (bf16[256,512]{1,0:T(8,128)(2,1)}, bf16[256,512]{1,0:T(8,128)(2,1)}, u32[]{:S(2)}, u32[]{:S(2)}) collective-permute-start(bf16[256,512]{1,0:T(8,128)(2,1)} %collective-permute-done.13.refs_12_), channel_id=1, source_target_pairs={{0,2},{1,3},{2,0},{3,1},{4,6},{5,7},{6,4},{7,5},{8,10},{9,11},{10,... | collective-permute-start | bytes 786440 | tf_op jit(solution)/shard_map/ppermute | solution.py:23
  46.9 0.5 collective-permute-done.11.refs_10_
  47.5 2.0 %collective-permute-start.8 = (bf16[256,512]{1,0:T(8,128)(2,1)}, bf16[256,512]{1,0:T(8,128)(2,1)}, u32[]{:S(2)}, u32[]{:S(2)}) collective-permute-start(bf16[256,512]{1,0:T(8,128)(2,1)} %collective-permute-done.7.refs_6_), channel_id=1, source_target_pairs={{0,16},{16,0},{1,17},{17,1},{2,18},{18,2},{3,19},{19,3},{4,20},{20... | collective-permute-start | bytes 786440 | tf_op jit(solution)/shard_map/ppermute | solution.py:37
  49.5 1.5 %collective-permute-done.14.refs_13_ = bf16[256,512]{1,0:T(8,128)(2,1)} collective-permute-done((bf16[256,512]{1,0:T(8,128)(2,1)}, bf16[256,512]{1,0:T(8,128)(2,1)}, u32[]{:S(2)}, u32[]{:S(2)}) %collective-permute-start.14) | collective-permute-done | bytes 262176 | tf_op jit(solution)/shard_map/ppermute | solution.py:37
  51.0 0.4 collective-permute-start.16
  51.4 0.1 fusion
  51.6 0.2 copy.18.scale
  51.8 2.6 %collective-permute-done.12.refs_11_ = bf16[256,512]{1,0:T(8,128)(2,1)} collective-permute-done((bf16[256,512]{1,0:T(8,128)(2,1)}, bf16[256,512]{1,0:T(8,128)(2,1)}, u32[]{:S(2)}, u32[]{:S(2)}) %collective-permute-start.12) | collective-permute-done | bytes 262176 | tf_op jit(solution)/shard_map/ppermute | solution.py:23
  54.4 2.0 %collective-permute-done.8.refs_7_ = bf16[256,512]{1,0:T(8,128)(2,1)} collective-permute-done((bf16[256,512]{1,0:T(8,128)(2,1)}, bf16[256,512]{1,0:T(8,128)(2,1)}, u32[]{:S(2)}, u32[]{:S(2)}) %collective-permute-start.8) | collective-permute-done | bytes 262176 | tf_op jit(solution)/shard_map/ppermute | solution.py:37
  56.4 3.6 %collective-permute-done.15.refs_14_ = bf16[256,512]{1,0:T(8,128)(2,1)} collective-permute-done((bf16[256,512]{1,0:T(8,128)(2,1)}, bf16[256,512]{1,0:T(8,128)(2,1)}, u32[]{:S(2)}, u32[]{:S(2)}) %collective-permute-start.15) | collective-permute-done | bytes 262176 | tf_op jit(solution)/shard_map/ppermute | solution.py:23
  60.0 5.6 %collective-permute-done.16.refs_15_ = bf16[256,512]{1,0:T(8,128)(2,1)} collective-permute-done((bf16[256,512]{1,0:T(8,128)(2,1)}, bf16[256,512]{1,0:T(8,128)(2,1)}, u32[]{:S(2)}, u32[]{:S(2)}) %collective-permute-start.16) | collective-permute-done | bytes 262176 | tf_op jit(solution)/shard_map/ppermute | solution.py:23
  65.7 0.9 copy-done.4
  66.6 0.9 copy-done.6
  67.6 0.9 copy-done.8
  68.5 7.6 %shard_map.128 = (bf16[512,512]{1,0:T(8,128)(2,1)S(1)}, bf16[512,512]{1,0:T(8,128)(2,1)S(1)}, bf16[512,512]{1,0:T(8,128)(2,1)S(1)}, bf16[512,512]{1,0:T(8,128)(2...) custom-call(s32[16]{0:T(128)S(1)} %get-tuple-element.47.starts, ...), custom_call_target="tpu_custom_call" | custom-call | flops 4294967296 | bytes 8388608 | tf_op jit(solution)/shard_map/pallas_call | solution.py:211
  76.2 2.1 %collective-permute-start.17 = (bf16[256,256]{1,0:T(8,128)(2,1)S(1)}, bf16[256,256]{1,0:T(8,128)(2,1)S(1)}, u32[]{:S(2)}, u32[]{:S(2)}) collective-permute-start(bf16[256,256]{1,0:T(8,128)(2,1)S(1)} %get-tuple-element.33), channel_id=1, source_target_pairs={{0,2},{1,3},{2,0},{3,1},{4,6},{5,7},{6,4},{7,5},{8,10},{9,11},{10,... | collective-permute-start | bytes 393224 | tf_op jit(solution)/shard_map/ppermute | solution.py:23
  78.2 0.1 collective-permute-start.18
  78.3 1.9 %collective-permute-start.25 = (bf16[256,512]{1,0:T(8,128)(2,1)S(1)}, bf16[256,512]{1,0:T(8,128)(2,1)S(1)}, u32[]{:S(2)}, u32[]{:S(2)}) collective-permute-start(bf16[256,512]{1,0:T(8,128)(2,1)S(1)} %collective-permute-done.24.refs_8_), channel_id=1, source_target_pairs={{0,16},{16,0},{1,17},{17,1},{2,18},{18,2},{3,19},{19,3},{4,20},{20... | collective-permute-start | bytes 786440 | tf_op jit(solution)/shard_map/ppermute | solution.py:37
  80.3 0.1 collective-permute-start.23
  80.4 2.0 %collective-permute-start.30 = (bf16[256,512]{1,0:T(8,128)(2,1)S(1)}, bf16[256,512]{1,0:T(8,128)(2,1)S(1)}, u32[]{:S(2)}, u32[]{:S(2)}) collective-permute-start(bf16[256,512]{1,0:T(8,128)(2,1)S(1)} %collective-permute-done.22.refs_6_), channel_id=1, source_target_pairs={{0,4},{1,5},{2,6},{3,7},{4,0},{5,1},{6,2},{7,3},{8,12},{9,13},{10,... | collective-permute-start | bytes 786440 | tf_op jit(solution)/shard_map/ppermute | solution.py:23
  82.4 0.8 collective-permute-start.27
  83.2 1.5 %collective-permute-start.33 = (bf16[256,512]{1,0:T(8,128)(2,1)S(1)}, bf16[256,512]{1,0:T(8,128)(2,1)S(1)}, u32[]{:S(2)}, u32[]{:S(2)}) collective-permute-start(bf16[256,512]{1,0:T(8,128)(2,1)S(1)} %collective-permute-done.32.refs_16_), channel_id=1, source_target_pairs={{0,16},{16,0},{1,17},{17,1},{2,18},{18,2},{3,19},{19,3},{4,20},{20... | collective-permute-start | bytes 786440 | tf_op jit(solution)/shard_map/ppermute | solution.py:37
  84.8 8.3 %collective-permute-done.23.refs_7_ = bf16[256,512]{1,0:T(8,128)(2,1)S(1)} collective-permute-done((bf16[256,512]{1,0:T(8,128)(2,1)S(1)}, bf16[256,512]{1,0:T(8,128)(2,1)S(1)}, u32[]{:S(2)}, u32[]{:S(2)}) %collective-permute-start.23) | collective-permute-done | bytes 262176 | tf_op jit(solution)/shard_map/ppermute | solution.py:37
  93.1 1.9 %collective-permute-start.34 = (bf16[256,512]{1,0:T(8,128)(2,1)S(1)}, bf16[256,512]{1,0:T(8,128)(2,1)S(1)}, u32[]{:S(2)}, u32[]{:S(2)}) collective-permute-start(bf16[256,512]{1,0:T(8,128)(2,1)S(1)} %collective-permute-done.32.refs_16_), channel_id=1, source_target_pairs={{0,2},{1,3},{2,0},{3,1},{4,6},{5,7},{6,4},{7,5},{8,10},{9,11},{10,... | collective-permute-start | bytes 786440 | tf_op jit(solution)/shard_map/ppermute | solution.py:23
  95.1 1.5 %collective-permute-start.31 = (bf16[256,512]{1,0:T(8,128)(2,1)S(1)}, bf16[256,512]{1,0:T(8,128)(2,1)S(1)}, u32[]{:S(2)}, u32[]{:S(2)}) collective-permute-start(bf16[256,512]{1,0:T(8,128)(2,1)S(1)} %collective-permute-done.30.refs_14_), channel_id=1, source_target_pairs={{0,16},{16,0},{1,17},{17,1},{2,18},{18,2},{3,19},{19,3},{4,20},{20... | collective-permute-start | bytes 786440 | tf_op jit(solution)/shard_map/ppermute | solution.py:37
  96.6 6.6 %collective-permute-done.33.refs_17_ = bf16[256,512]{1,0:T(8,128)(2,1)S(1)} collective-permute-done((bf16[256,512]{1,0:T(8,128)(2,1)S(1)}, bf16[256,512]{1,0:T(8,128)(2,1)S(1)}, u32[]{:S(2)}, u32[]{:S(2)}) %collective-permute-start.33) | collective-permute-done | bytes 262176 | tf_op jit(solution)/shard_map/ppermute | solution.py:37
  103.2 1.5 %collective-permute-start.35 = (bf16[256,512]{1,0:T(8,128)(2,1)S(1)}, bf16[256,512]{1,0:T(8,128)(2,1)S(1)}, u32[]{:S(2)}, u32[]{:S(2)}) collective-permute-start(bf16[256,512]{1,0:T(8,128)(2,1)S(1)} %collective-permute-done.33.refs_17_), channel_id=1, source_target_pairs={{0,2},{1,3},{2,0},{3,1},{4,6},{5,7},{6,4},{7,5},{8,10},{9,11},{10,... | collective-permute-start | bytes 786440 | tf_op jit(solution)/shard_map/ppermute | solution.py:23
  104.7 1.3 collective-permute-start.19
  106.0 0.7 collective-permute-start.20
  106.7 0.1 pad_add_fusion.1.starts
  106.8 2.7 %collective-permute-done.35.refs_19_ = bf16[256,512]{1,0:T(8,128)(2,1)S(1)} collective-permute-done((bf16[256,512]{1,0:T(8,128)(2,1)S(1)}, bf16[256,512]{1,0:T(8,128)(2,1)S(1)}, u32[]{:S(2)}, u32[]{:S(2)}) %collective-permute-start.35) | collective-permute-done | bytes 262176 | tf_op jit(solution)/shard_map/ppermute | solution.py:23
  109.6 0.1 collective-permute-done.19.refs_2_
  109.7 1.4 %collective-permute-done.20.refs_3_ = bf16[256,256]{1,0:T(8,128)(2,1)S(1)} collective-permute-done((bf16[256,256]{1,0:T(8,128)(2,1)S(1)}, bf16[256,256]{1,0:T(8,128)(2,1)S(1)}, u32[]{:S(2)}, u32[]{:S(2)}) %collective-permute-start.20) | collective-permute-done | bytes 131104 | tf_op jit(solution)/shard_map/ppermute | solution.py:23
  111.1 4.2 %shard_map.132 = (f32[512,512]{1,0:T(8,128)S(1)}, bf16[512,512]{1,0:T(8,128)(2,1)S(1)}, bf16[1024,1024]{1,0:T(8,128)(2,1)S(1)}) custom-call(s32[32]{0:T(128)S(1)} %pad_add_fusion.1.starts, bf16[512,2048]{1,0:T(8,128)(2,1)} %collective-permute-done.1.xb.x, bf16[512,512]{1,0:T(8,128)(2,1)S(1)} %get-tuple-element.41.k, ...), custom_call_target="tpu_custom_call" | custom-call | flops 1073741824 | bytes 8388608 | tf_op jit(solution)/shard_map/pallas_call | solution.py:211
  115.4 3.5 %collective-permute-start.36 = (bf16[256,256]{1,0:T(8,128)(2,1)S(1)}, bf16[256,256]{1,0:T(8,128)(2,1)S(1)}, u32[]{:S(2)}, u32[]{:S(2)}) collective-permute-start(bf16[256,256]{1,0:T(8,128)(2,1)S(1)} %add_convert_fusion.1), channel_id=1, source_target_pairs={{0,8},{1,9},{2,10},{3,11},{4,12},{5,13},{6,14},{7,15},{8,0},{9,1},... | collective-permute-start | bytes 393224 | tf_op jit(solution)/shard_map/ppermute | solution.py:23
  119.0 0.1 collective-permute-start.37
  119.0 9.8 %collective-permute-done.36.refs_0_ = bf16[256,256]{1,0:T(8,128)(2,1)S(1)} collective-permute-done((bf16[256,256]{1,0:T(8,128)(2,1)S(1)}, bf16[256,256]{1,0:T(8,128)(2,1)S(1)}, u32[]{:S(2)}, u32[]{:S(2)}) %collective-permute-start.36) | collective-permute-done | bytes 131104 | tf_op jit(solution)/shard_map/ppermute | solution.py:23
  128.9 2.6 %collective-permute-done.37.refs_1_ = bf16[256,256]{1,0:T(8,128)(2,1)S(1)} collective-permute-done((bf16[256,256]{1,0:T(8,128)(2,1)S(1)}, bf16[256,256]{1,0:T(8,128)(2,1)S(1)}, u32[]{:S(2)}, u32[]{:S(2)}) %collective-permute-start.37) | collective-permute-done | bytes 131104 | tf_op jit(solution)/shard_map/ppermute | solution.py:23
  131.5 0.3 shard_map.133
  131.9 3.2 %shard_map.130 = (f32[512,512]{1,0:T(8,128)S(1)}, bf16[512,512]{1,0:T(8,128)(2,1)S(1)}) custom-call(s32[32]{0:T(128)S(1)} %pad_add_fusion.1.starts, bf16[512,2048]{1,0:T(8,128)(2,1)S(1)} %copy-done, bf16[512,512]{1,0:T(8,128)(2,1)S(1)} %get-tuple-element.30.k, bf16[512,512]{1,0:T(8,128)(2,1)S(1)} %get-tuple-element.31.v, ...), custom_call_target="tpu_custom_call" | custom-call | flops 1073741824 | bytes 8388608 | tf_op jit(solution)/shard_map/pallas_call | solution.py:211
  135.1 0.3 shard_map.131.mine
  135.4 3.2 %shard_map.134 = bf16[512,2048]{1,0:T(8,128)(2,1)} custom-call(s32[1]{0:T(128)} %bitcast.core_ref, bf16[512,512]{1,0:T(8,128)(2,1)S(1)} %shard_map.131.mine, bf16[512,512]{1,0:T(8,128)(2,1)S(1)} %collective-permute-done.38.theirs, bf16[1024,1024]{1,0:T(8,128)(2,1)S(1)} %get-tuple-element.46.w_mine, bf16[1024,1024]{1,0:T(8,128)(2,1)S(1)} %collective-permute-done.39.w_theirs), custom_call_target="tpu_custom_call" | custom-call | flops 2147483648 | bytes 8388608 | tf_op jit(solution)/shard_map/pallas_call | solution.py:211
  (67 shorter events, 0.7 us)
Async XLA Ops:
  0.0 44.8 %copy-start.9 = (pred[14]{0:T(512)(128)(4,1)S(1)}, pred[14]{0:T(512)(128)(4,1)}, u32[]{:S(2)}) copy-start(pred[14]{0:T(512)(128)(4,1)} %constant.69.clone) | copy-start | bytes 46
  0.0 44.8 %copy-start.10 = (f32[14]{0:T(128)S(1)}, f32[14]{0:T(128)}, u32[]{:S(2)}) copy-start(f32[14]{0:T(128)} %constant.70.clone) | copy-start | bytes 172
  0.0 44.8 %copy-start.11 = (s32[14]{0:T(128)S(1)}, s32[14]{0:T(128)}, u32[]{:S(2)}) copy-start(s32[14]{0:T(128)} %constant.68.clone) | copy-start | bytes 172
  0.0 51.4 %copy-start.12 = (s32[16]{0:T(128)S(1)}, s32[16]{0:T(128)}, u32[]{:S(2)}) copy-start(s32[16]{0:T(128)} %constant.74) | copy-start | bytes 196
  0.0 51.4 %copy-start.13 = (pred[16]{0:T(512)(128)(4,1)S(1)}, pred[16]{0:T(512)(128)(4,1)}, u32[]{:S(2)}) copy-start(pred[16]{0:T(512)(128)(4,1)} %constant.73) | copy-start | bytes 52
  0.0 51.4 %copy-start.14 = (s32[16]{0:T(128)S(1)}, s32[16]{0:T(128)}, u32[]{:S(2)}) copy-start(s32[16]{0:T(128)} %constant.71.clone) | copy-start | bytes 196
  0.0 65.6 %copy-start = (bf16[512,2048]{1,0:T(8,128)(2,1)S(1)}, bf16[512,2048]{1,0:T(8,128)(2,1)}, u32[]{:S(2)}) copy-start(bf16[512,2048]{1,0:T(8,128)(2,1)} %x.1) | copy-start | bytes 6291460
  0.0 65.6 %collective-permute-start.1 = (bf16[512,2048]{1,0:T(8,128)(2,1)}, bf16[512,2048]{1,0:T(8,128)(2,1)}, u32[]{:S(2)}, u32[]{:S(2)}) collective-permute-start(bf16[512,2048]{1,0:T(8,128)(2,1)} %x.1), channel_id=1, source_target_pairs={{0,1},{1,0},{2,3},{3,2},{4,5},{5,4},{6,7},{7,6},{8,9},{9,8},{10,11... | collective-permute-start | bytes 6291464 | tf_op jit(solution)/shard_map/ppermute | solution.py:23
  2.9 62.8 %copy-start.2 = (bf16[256,512]{1,0:T(8,128)(2,1)S(1)}, bf16[256,512]{1,0:T(8,128)(2,1)}, u32[]{:S(2)}) copy-start(bf16[256,512]{1,0:T(8,128)(2,1)} %get-tuple-element.26.refs_0_) | copy-start | bytes 786436
  2.9 8.3 %collective-permute-start.2 = (bf16[256,512]{1,0:T(8,128)(2,1)}, bf16[256,512]{1,0:T(8,128)(2,1)S(1)}, u32[]{:S(2)}, u32[]{:S(2)}) collective-permute-start(bf16[256,512]{1,0:T(8,128)(2,1)} %get-tuple-element.27), channel_id=1, source_target_pairs={{0,1},{1,0},{2,3},{3,2},{4,5},{5,4},{6,7},{7,6},{8,9},{9,8},{10,11... | collective-permute-start | bytes 786440 | tf_op jit(solution)/shard_map/ppermute | solution.py:23
  4.0 5.7 %collective-permute-start = (f32[14,2,512]{2,1,0:T(2,128)S(1)}, f32[14,2,512]{2,1,0:T(2,128)S(1)}, u32[]{:S(2)}, u32[]{:S(2)}) collective-permute-start(f32[14,2,512]{2,1,0:T(2,128)S(1)} %get-tuple-element.50), channel_id=1, source_target_pairs={{0,1},{1,0},{2,3},{3,2},{4,5},{5,4},{6,7},{7,6},{8,9},{9,8},{10,11... | collective-permute-start | bytes 172040 | tf_op jit(solution)/shard_map/ppermute | solution.py:23
  4.5 9.6 %collective-permute-start.3 = (bf16[256,512]{1,0:T(8,128)(2,1)}, bf16[256,512]{1,0:T(8,128)(2,1)S(1)}, u32[]{:S(2)}, u32[]{:S(2)}) collective-permute-start(bf16[256,512]{1,0:T(8,128)(2,1)} %get-tuple-element.28), channel_id=1, source_target_pairs={{0,2},{1,3},{2,0},{3,1},{4,6},{5,7},{6,4},{7,5},{8,10},{9,11},{10,... | collective-permute-start | bytes 786440 | tf_op jit(solution)/shard_map/ppermute | solution.py:33
  7.1 15.1 %collective-permute-start.5 = (bf16[256,512]{1,0:T(8,128)(2,1)}, bf16[256,512]{1,0:T(8,128)(2,1)S(1)}, u32[]{:S(2)}, u32[]{:S(2)}) collective-permute-start(bf16[256,512]{1,0:T(8,128)(2,1)} %get-tuple-element.28), channel_id=1, source_target_pairs={{0,8},{1,9},{2,10},{3,11},{4,12},{5,13},{6,14},{7,15},{8,0},{9,1},... | collective-permute-start | bytes 786440 | tf_op jit(solution)/shard_map/ppermute | solution.py:33
  9.7 14.0 %collective-permute-start.9 = (bf16[256,512]{1,0:T(8,128)(2,1)}, bf16[256,512]{1,0:T(8,128)(2,1)}, u32[]{:S(2)}, u32[]{:S(2)}) collective-permute-start(bf16[256,512]{1,0:T(8,128)(2,1)} %get-tuple-element.28), channel_id=1, source_target_pairs={{0,4},{1,5},{2,6},{3,7},{4,0},{5,1},{6,2},{7,3},{8,12},{9,13},{10,... | collective-permute-start | bytes 786440 | tf_op jit(solution)/shard_map/ppermute | solution.py:33
  11.2 40.4 %copy-start.3 = (bf16[256,512]{1,0:T(8,128)(2,1)}, bf16[256,512]{1,0:T(8,128)(2,1)S(1)}, u32[]{:S(2)}) copy-start(bf16[256,512]{1,0:T(8,128)(2,1)S(1)} %collective-permute-done.2.refs_1_) | copy-start | bytes 786436
  11.2 18.7 %collective-permute-start.10 = (bf16[256,512]{1,0:T(8,128)(2,1)}, bf16[256,512]{1,0:T(8,128)(2,1)}, u32[]{:S(2)}, u32[]{:S(2)}) collective-permute-start(bf16[256,512]{1,0:T(8,128)(2,1)} %get-tuple-element.29), channel_id=1, source_target_pairs={{0,5},{1,4},{2,7},{3,6},{4,1},{5,0},{6,3},{7,2},{8,13},{9,12},{10,... | collective-permute-start | bytes 786440 | tf_op jit(solution)/shard_map/ppermute | solution.py:33
  14.1 37.5 %copy-start.5 = (bf16[256,512]{1,0:T(8,128)(2,1)}, bf16[256,512]{1,0:T(8,128)(2,1)S(1)}, u32[]{:S(2)}) copy-start(bf16[256,512]{1,0:T(8,128)(2,1)S(1)} %collective-permute-done.3.refs_2_) | copy-start | bytes 786436
  14.1 16.6 %collective-permute-start.21 = (bf16[256,512]{1,0:T(8,128)(2,1)}, bf16[256,512]{1,0:T(8,128)(2,1)S(1)}, u32[]{:S(2)}, u32[]{:S(2)}) collective-permute-start(bf16[256,512]{1,0:T(8,128)(2,1)} %get-tuple-element.36), channel_id=1, source_target_pairs={{0,1},{1,0},{2,3},{3,2},{4,5},{5,4},{6,7},{7,6},{8,9},{9,8},{10,11... | collective-permute-start | bytes 786440 | tf_op jit(solution)/shard_map/ppermute | solution.py:23
  22.2 0.7 copy-start.7
  22.9 14.3 %collective-permute-start.24 = (bf16[256,512]{1,0:T(8,128)(2,1)}, bf16[256,512]{1,0:T(8,128)(2,1)S(1)}, u32[]{:S(2)}, u32[]{:S(2)}) collective-permute-start(bf16[256,512]{1,0:T(8,128)(2,1)} %get-tuple-element.37), channel_id=1, source_target_pairs={{0,8},{1,9},{2,10},{3,11},{4,12},{5,13},{6,14},{7,15},{8,0},{9,1},... | collective-permute-start | bytes 786440 | tf_op jit(solution)/shard_map/ppermute | solution.py:33
  23.7 14.2 %collective-permute-start.4 = (bf16[256,512]{1,0:T(8,128)(2,1)S(1)}, bf16[256,512]{1,0:T(8,128)(2,1)}, u32[]{:S(2)}, u32[]{:S(2)}) collective-permute-start(bf16[256,512]{1,0:T(8,128)(2,1)S(1)} %collective-permute-done.3.refs_2_), channel_id=1, source_target_pairs={{0,16},{16,0},{1,17},{17,1},{2,18},{18,2},{3,19},{19,3},{4,20},{20... | collective-permute-start | bytes 786440 | tf_op jit(solution)/shard_map/ppermute | solution.py:37
  30.0 11.9 %collective-permute-start.13 = (bf16[256,512]{1,0:T(8,128)(2,1)}, bf16[256,512]{1,0:T(8,128)(2,1)}, u32[]{:S(2)}, u32[]{:S(2)}) collective-permute-start(bf16[256,512]{1,0:T(8,128)(2,1)} %copy-done.7), channel_id=1, source_target_pairs={{0,4},{1,5},{2,6},{3,7},{4,0},{5,1},{6,2},{7,3},{8,12},{9,13},{10,... | collective-permute-start | bytes 786440 | tf_op jit(solution)/shard_map/ppermute | solution.py:23
  30.7 14.2 %collective-permute-start.6 = (bf16[256,512]{1,0:T(8,128)(2,1)}, bf16[256,512]{1,0:T(8,128)(2,1)}, u32[]{:S(2)}, u32[]{:S(2)}) collective-permute-start(bf16[256,512]{1,0:T(8,128)(2,1)} %copy-done.7), channel_id=1, source_target_pairs={{0,16},{16,0},{1,17},{17,1},{2,18},{18,2},{3,19},{19,3},{4,20},{20... | collective-permute-start | bytes 786440 | tf_op jit(solution)/shard_map/ppermute | solution.py:37
  37.2 7.8 %collective-permute-start.7 = (bf16[256,512]{1,0:T(8,128)(2,1)}, bf16[256,512]{1,0:T(8,128)(2,1)}, u32[]{:S(2)}, u32[]{:S(2)}) collective-permute-start(bf16[256,512]{1,0:T(8,128)(2,1)} %copy-done.7), channel_id=1, source_target_pairs={{0,2},{1,3},{2,0},{3,1},{4,6},{5,7},{6,4},{7,5},{8,10},{9,11},{10,... | collective-permute-start | bytes 786440 | tf_op jit(solution)/shard_map/ppermute | solution.py:23
  37.9 9.6 %collective-permute-start.11 = (bf16[256,512]{1,0:T(8,128)(2,1)S(1)}, bf16[256,512]{1,0:T(8,128)(2,1)}, u32[]{:S(2)}, u32[]{:S(2)}) collective-permute-start(bf16[256,512]{1,0:T(8,128)(2,1)S(1)} %collective-permute-done.3.refs_2_), channel_id=1, source_target_pairs={{0,4},{1,5},{2,6},{3,7},{4,0},{5,1},{6,2},{7,3},{8,12},{9,13},{10,... | collective-permute-start | bytes 786440 | tf_op jit(solution)/shard_map/ppermute | solution.py:23
  41.8 9.1 %collective-permute-start.14 = (bf16[256,512]{1,0:T(8,128)(2,1)}, bf16[256,512]{1,0:T(8,128)(2,1)}, u32[]{:S(2)}, u32[]{:S(2)}) collective-permute-start(bf16[256,512]{1,0:T(8,128)(2,1)} %collective-permute-done.13.refs_12_), channel_id=1, source_target_pairs={{0,16},{16,0},{1,17},{17,1},{2,18},{18,2},{3,19},{19,3},{4,20},{20... | collective-permute-start | bytes 786440 | tf_op jit(solution)/shard_map/ppermute | solution.py:37
  44.9 9.5 %collective-permute-start.12 = (bf16[256,512]{1,0:T(8,128)(2,1)}, bf16[256,512]{1,0:T(8,128)(2,1)}, u32[]{:S(2)}, u32[]{:S(2)}) collective-permute-start(bf16[256,512]{1,0:T(8,128)(2,1)} %collective-permute-done.10.refs_9_), channel_id=1, source_target_pairs={{0,2},{1,3},{2,0},{3,1},{4,6},{5,7},{6,4},{7,5},{8,10},{9,11},{10,... | collective-permute-start | bytes 786440 | tf_op jit(solution)/shard_map/ppermute | solution.py:23
  44.9 15.1 %collective-permute-start.15 = (bf16[256,512]{1,0:T(8,128)(2,1)}, bf16[256,512]{1,0:T(8,128)(2,1)}, u32[]{:S(2)}, u32[]{:S(2)}) collective-permute-start(bf16[256,512]{1,0:T(8,128)(2,1)} %collective-permute-done.13.refs_12_), channel_id=1, source_target_pairs={{0,2},{1,3},{2,0},{3,1},{4,6},{5,7},{6,4},{7,5},{8,10},{9,11},{10,... | collective-permute-start | bytes 786440 | tf_op jit(solution)/shard_map/ppermute | solution.py:23
  47.5 9.0 %collective-permute-start.8 = (bf16[256,512]{1,0:T(8,128)(2,1)}, bf16[256,512]{1,0:T(8,128)(2,1)}, u32[]{:S(2)}, u32[]{:S(2)}) collective-permute-start(bf16[256,512]{1,0:T(8,128)(2,1)} %collective-permute-done.7.refs_6_), channel_id=1, source_target_pairs={{0,16},{16,0},{1,17},{17,1},{2,18},{18,2},{3,19},{19,3},{4,20},{20... | collective-permute-start | bytes 786440 | tf_op jit(solution)/shard_map/ppermute | solution.py:37
  51.0 14.7 %collective-permute-start.16 = (bf16[256,512]{1,0:T(8,128)(2,1)}, bf16[256,512]{1,0:T(8,128)(2,1)}, u32[]{:S(2)}, u32[]{:S(2)}) collective-permute-start(bf16[256,512]{1,0:T(8,128)(2,1)} %collective-permute-done.14.refs_13_), channel_id=1, source_target_pairs={{0,2},{1,3},{2,0},{3,1},{4,6},{5,7},{6,4},{7,5},{8,10},{9,11},{10,... | collective-permute-start | bytes 786440 | tf_op jit(solution)/shard_map/ppermute | solution.py:23
  54.4 21.8 %collective-permute-start.22 = (bf16[256,512]{1,0:T(8,128)(2,1)}, bf16[256,512]{1,0:T(8,128)(2,1)S(1)}, u32[]{:S(2)}, u32[]{:S(2)}) collective-permute-start(bf16[256,512]{1,0:T(8,128)(2,1)} %get-tuple-element.37), channel_id=1, source_target_pairs={{0,2},{1,3},{2,0},{3,1},{4,6},{5,7},{6,4},{7,5},{8,10},{9,11},{10,... | collective-permute-start | bytes 786440 | tf_op jit(solution)/shard_map/ppermute | solution.py:33
  56.4 21.8 %collective-permute-start.28 = (bf16[256,512]{1,0:T(8,128)(2,1)}, bf16[256,512]{1,0:T(8,128)(2,1)S(1)}, u32[]{:S(2)}, u32[]{:S(2)}) collective-permute-start(bf16[256,512]{1,0:T(8,128)(2,1)} %get-tuple-element.37), channel_id=1, source_target_pairs={{0,4},{1,5},{2,6},{3,7},{4,0},{5,1},{6,2},{7,3},{8,12},{9,13},{10,... | collective-permute-start | bytes 786440 | tf_op jit(solution)/shard_map/ppermute | solution.py:33
  60.0 18.3 %collective-permute-start.29 = (bf16[256,512]{1,0:T(8,128)(2,1)}, bf16[256,512]{1,0:T(8,128)(2,1)S(1)}, u32[]{:S(2)}, u32[]{:S(2)}) collective-permute-start(bf16[256,512]{1,0:T(8,128)(2,1)} %get-tuple-element.38), channel_id=1, source_target_pairs={{0,5},{1,4},{2,7},{3,6},{4,1},{5,0},{6,3},{7,2},{8,13},{9,12},{10,... | collective-permute-start | bytes 786440 | tf_op jit(solution)/shard_map/ppermute | solution.py:33
  65.6 14.6 %collective-permute-start.26 = (bf16[256,512]{1,0:T(8,128)(2,1)S(1)}, bf16[256,512]{1,0:T(8,128)(2,1)S(1)}, u32[]{:S(2)}, u32[]{:S(2)}) collective-permute-start(bf16[256,512]{1,0:T(8,128)(2,1)S(1)} %collective-permute-done.24.refs_8_), channel_id=1, source_target_pairs={{0,2},{1,3},{2,0},{3,1},{4,6},{5,7},{6,4},{7,5},{8,10},{9,11},{10,... | collective-permute-start | bytes 786440 | tf_op jit(solution)/shard_map/ppermute | solution.py:23
  65.6 14.7 %collective-permute-start.32 = (bf16[256,512]{1,0:T(8,128)(2,1)S(1)}, bf16[256,512]{1,0:T(8,128)(2,1)S(1)}, u32[]{:S(2)}, u32[]{:S(2)}) collective-permute-start(bf16[256,512]{1,0:T(8,128)(2,1)S(1)} %collective-permute-done.24.refs_8_), channel_id=1, source_target_pairs={{0,4},{1,5},{2,6},{3,7},{4,0},{5,1},{6,2},{7,3},{8,12},{9,13},{10,... | collective-permute-start | bytes 786440 | tf_op jit(solution)/shard_map/ppermute | solution.py:23
  65.7 1.0 copy-start.4
  66.6 0.9 copy-start.6
  67.6 0.9 copy-start.8
  68.5 42.6 %copy-start.1 = (bf16[256,512]{1,0:T(8,128)(2,1)S(1)}, bf16[256,512]{1,0:T(8,128)(2,1)}, u32[]{:S(2)}) copy-start(bf16[256,512]{1,0:T(8,128)(2,1)} %get-tuple-element.35.refs_4_) | copy-start | bytes 786436
  76.2 6.2 %collective-permute-start.17 = (bf16[256,256]{1,0:T(8,128)(2,1)S(1)}, bf16[256,256]{1,0:T(8,128)(2,1)S(1)}, u32[]{:S(2)}, u32[]{:S(2)}) collective-permute-start(bf16[256,256]{1,0:T(8,128)(2,1)S(1)} %get-tuple-element.33), channel_id=1, source_target_pairs={{0,2},{1,3},{2,0},{3,1},{4,6},{5,7},{6,4},{7,5},{8,10},{9,11},{10,... | collective-permute-start | bytes 393224 | tf_op jit(solution)/shard_map/ppermute | solution.py:23
  78.2 5.0 %collective-permute-start.18 = (bf16[256,256]{1,0:T(8,128)(2,1)S(1)}, bf16[256,256]{1,0:T(8,128)(2,1)S(1)}, u32[]{:S(2)}, u32[]{:S(2)}) collective-permute-start(bf16[256,256]{1,0:T(8,128)(2,1)S(1)} %get-tuple-element.34), channel_id=1, source_target_pairs={{0,2},{1,3},{2,0},{3,1},{4,6},{5,7},{6,4},{7,5},{8,10},{9,11},{10,... | collective-permute-start | bytes 393224 | tf_op jit(solution)/shard_map/ppermute | solution.py:23
  78.3 26.4 %collective-permute-start.25 = (bf16[256,512]{1,0:T(8,128)(2,1)S(1)}, bf16[256,512]{1,0:T(8,128)(2,1)S(1)}, u32[]{:S(2)}, u32[]{:S(2)}) collective-permute-start(bf16[256,512]{1,0:T(8,128)(2,1)S(1)} %collective-permute-done.24.refs_8_), channel_id=1, source_target_pairs={{0,16},{16,0},{1,17},{17,1},{2,18},{18,2},{3,19},{19,3},{4,20},{20... | collective-permute-start | bytes 786440 | tf_op jit(solution)/shard_map/ppermute | solution.py:37
  80.3 12.9 %collective-permute-start.23 = (bf16[256,512]{1,0:T(8,128)(2,1)S(1)}, bf16[256,512]{1,0:T(8,128)(2,1)S(1)}, u32[]{:S(2)}, u32[]{:S(2)}) collective-permute-start(bf16[256,512]{1,0:T(8,128)(2,1)S(1)} %collective-permute-done.22.refs_6_), channel_id=1, source_target_pairs={{0,16},{16,0},{1,17},{17,1},{2,18},{18,2},{3,19},{19,3},{4,20},{20... | collective-permute-start | bytes 786440 | tf_op jit(solution)/shard_map/ppermute | solution.py:37
  80.4 14.7 %collective-permute-start.30 = (bf16[256,512]{1,0:T(8,128)(2,1)S(1)}, bf16[256,512]{1,0:T(8,128)(2,1)S(1)}, u32[]{:S(2)}, u32[]{:S(2)}) collective-permute-start(bf16[256,512]{1,0:T(8,128)(2,1)S(1)} %collective-permute-done.22.refs_6_), channel_id=1, source_target_pairs={{0,4},{1,5},{2,6},{3,7},{4,0},{5,1},{6,2},{7,3},{8,12},{9,13},{10,... | collective-permute-start | bytes 786440 | tf_op jit(solution)/shard_map/ppermute | solution.py:23
  82.4 23.6 %collective-permute-start.27 = (bf16[256,512]{1,0:T(8,128)(2,1)S(1)}, bf16[256,512]{1,0:T(8,128)(2,1)S(1)}, u32[]{:S(2)}, u32[]{:S(2)}) collective-permute-start(bf16[256,512]{1,0:T(8,128)(2,1)S(1)} %collective-permute-done.26.refs_10_), channel_id=1, source_target_pairs={{0,16},{16,0},{1,17},{17,1},{2,18},{18,2},{3,19},{19,3},{4,20},{20... | collective-permute-start | bytes 786440 | tf_op jit(solution)/shard_map/ppermute | solution.py:37
  83.2 20.0 %collective-permute-start.33 = (bf16[256,512]{1,0:T(8,128)(2,1)S(1)}, bf16[256,512]{1,0:T(8,128)(2,1)S(1)}, u32[]{:S(2)}, u32[]{:S(2)}) collective-permute-start(bf16[256,512]{1,0:T(8,128)(2,1)S(1)} %collective-permute-done.32.refs_16_), channel_id=1, source_target_pairs={{0,16},{16,0},{1,17},{17,1},{2,18},{18,2},{3,19},{19,3},{4,20},{20... | collective-permute-start | bytes 786440 | tf_op jit(solution)/shard_map/ppermute | solution.py:37
  93.1 13.7 %collective-permute-start.34 = (bf16[256,512]{1,0:T(8,128)(2,1)S(1)}, bf16[256,512]{1,0:T(8,128)(2,1)S(1)}, u32[]{:S(2)}, u32[]{:S(2)}) collective-permute-start(bf16[256,512]{1,0:T(8,128)(2,1)S(1)} %collective-permute-done.32.refs_16_), channel_id=1, source_target_pairs={{0,2},{1,3},{2,0},{3,1},{4,6},{5,7},{6,4},{7,5},{8,10},{9,11},{10,... | collective-permute-start | bytes 786440 | tf_op jit(solution)/shard_map/ppermute | solution.py:23
  95.1 11.7 %collective-permute-start.31 = (bf16[256,512]{1,0:T(8,128)(2,1)S(1)}, bf16[256,512]{1,0:T(8,128)(2,1)S(1)}, u32[]{:S(2)}, u32[]{:S(2)}) collective-permute-start(bf16[256,512]{1,0:T(8,128)(2,1)S(1)} %collective-permute-done.30.refs_14_), channel_id=1, source_target_pairs={{0,16},{16,0},{1,17},{17,1},{2,18},{18,2},{3,19},{19,3},{4,20},{20... | collective-permute-start | bytes 786440 | tf_op jit(solution)/shard_map/ppermute | solution.py:37
  103.2 6.4 %collective-permute-start.35 = (bf16[256,512]{1,0:T(8,128)(2,1)S(1)}, bf16[256,512]{1,0:T(8,128)(2,1)S(1)}, u32[]{:S(2)}, u32[]{:S(2)}) collective-permute-start(bf16[256,512]{1,0:T(8,128)(2,1)S(1)} %collective-permute-done.33.refs_17_), channel_id=1, source_target_pairs={{0,2},{1,3},{2,0},{3,1},{4,6},{5,7},{6,4},{7,5},{8,10},{9,11},{10,... | collective-permute-start | bytes 786440 | tf_op jit(solution)/shard_map/ppermute | solution.py:23
  104.7 5.0 %collective-permute-start.19 = (bf16[256,256]{1,0:T(8,128)(2,1)S(1)}, bf16[256,256]{1,0:T(8,128)(2,1)S(1)}, u32[]{:S(2)}, u32[]{:S(2)}) collective-permute-start(bf16[256,256]{1,0:T(8,128)(2,1)S(1)} %add_convert_fusion.3), channel_id=1, source_target_pairs={{0,4},{1,5},{2,6},{3,7},{4,0},{5,1},{6,2},{7,3},{8,12},{9,13},{10,... | collective-permute-start | bytes 393224 | tf_op jit(solution)/shard_map/ppermute | solution.py:23
  106.0 5.1 %collective-permute-start.20 = (bf16[256,256]{1,0:T(8,128)(2,1)S(1)}, bf16[256,256]{1,0:T(8,128)(2,1)S(1)}, u32[]{:S(2)}, u32[]{:S(2)}) collective-permute-start(bf16[256,256]{1,0:T(8,128)(2,1)S(1)} %add_convert_fusion.2), channel_id=1, source_target_pairs={{0,4},{1,5},{2,6},{3,7},{4,0},{5,1},{6,2},{7,3},{8,12},{9,13},{10,... | collective-permute-start | bytes 393224 | tf_op jit(solution)/shard_map/ppermute | solution.py:23
  115.3 20.1 %collective-permute-start.39 = (bf16[1024,1024]{1,0:T(8,128)(2,1)S(1)}, bf16[1024,1024]{1,0:T(8,128)(2,1)S(1)}, u32[]{:S(2)}, u32[]{:S(2)}) collective-permute-start(bf16[1024,1024]{1,0:T(8,128)(2,1)S(1)} %get-tuple-element.46.w_mine), channel_id=1, source_target_pairs={{0,1},{1,0},{2,3},{3,2},{4,5},{5,4},{6,7},{7,6},{8,9},{9,8},{10,11... | collective-permute-start | bytes 6291464 | tf_op jit(solution)/shard_map/ppermute | solution.py:23
  115.4 13.5 %collective-permute-start.36 = (bf16[256,256]{1,0:T(8,128)(2,1)S(1)}, bf16[256,256]{1,0:T(8,128)(2,1)S(1)}, u32[]{:S(2)}, u32[]{:S(2)}) collective-permute-start(bf16[256,256]{1,0:T(8,128)(2,1)S(1)} %add_convert_fusion.1), channel_id=1, source_target_pairs={{0,8},{1,9},{2,10},{3,11},{4,12},{5,13},{6,14},{7,15},{8,0},{9,1},... | collective-permute-start | bytes 393224 | tf_op jit(solution)/shard_map/ppermute | solution.py:23
  119.0 12.5 %collective-permute-start.37 = (bf16[256,256]{1,0:T(8,128)(2,1)S(1)}, bf16[256,256]{1,0:T(8,128)(2,1)S(1)}, u32[]{:S(2)}, u32[]{:S(2)}) collective-permute-start(bf16[256,256]{1,0:T(8,128)(2,1)S(1)} %add_convert_fusion), channel_id=1, source_target_pairs={{0,8},{1,9},{2,10},{3,11},{4,12},{5,13},{6,14},{7,15},{8,0},{9,1},... | collective-permute-start | bytes 393224 | tf_op jit(solution)/shard_map/ppermute | solution.py:23
  131.8 3.6 %collective-permute-start.38 = (bf16[512,512]{1,0:T(8,128)(2,1)S(1)}, bf16[512,512]{1,0:T(8,128)(2,1)S(1)}, u32[]{:S(2)}, u32[]{:S(2)}) collective-permute-start(bf16[512,512]{1,0:T(8,128)(2,1)S(1)} %shard_map.133), channel_id=1, source_target_pairs={{0,1},{1,0},{2,3},{3,2},{4,5},{5,4},{6,7},{7,6},{8,9},{9,8},{10,11... | collective-permute-start | bytes 1572872 | tf_op jit(solution)/shard_map/ppermute | solution.py:23

commit v5 on v4

--- a/solution.py
+++ b/solution.py
@@ -40,30 +40,24 @@
 OWN, OTHER, MINE, FAR = range(4)
 
 
-def gather_rows(first, second, mine, arrived, zbits, turn):
+def gather_rows(first, second, mine, arrived, chips, routes):
+    made = {}
+
+    def piece(flip, half):
+        if (flip, half) not in made:
+            digit = routes.get((flip, half), 0 if half else flip & -flip)
+            if digit == 0:
+                value = swap_x(piece(flip, 0))
+            elif digit == flip:
+                value = swap_crossed((first, second)[half], digit.bit_length(), half)
+            else:
+                value = swap(piece(flip ^ digit, half), digit.bit_length())
+            made[flip, half] = value
+        return made[flip, half]
+
     pieces = [(mine, 0, MINE), (arrived, 0, FAR)]
-    beside = swap_crossed(first, 1)
-    pieces.append((beside, 1, OWN))
-    pieces.append((swap_x(beside), 1, OTHER))
-    held = []
-    for bit in reversed(zbits):
-        flip = 1 << (bit - 1)
-        got = [(swap_crossed(first, bit), flip)]
-        for piece, before in held:
-            got.append((swap(piece, bit), before ^ flip))
-        held += got
-    for at, (piece, flip) in enumerate(held):
-        if flip == 1 << (zbits[0] - 1):
-            side = swap_crossed(second, zbits[0], 1)
-            across = swap(beside, zbits[0])
-        else:
-            side = swap_x(piece)
-            across = swap(piece, 1)
-        if at in turn:
-            corner = swap_x(across)
-        else:
-            corner = swap(side, 1)
-        pieces += [(piece, flip, OWN), (side, flip, OTHER), (across, flip ^ 1, OWN), (corner, flip ^ 1, OTHER)]
+    for flip in range(1, chips):
+        pieces += [(piece(flip, 0), flip, OWN), (piece(flip, 1), flip, OTHER)]
     return pieces
 
 
@@ -225,7 +219,6 @@
     core = device % CORES
     odd_group = lax.axis_index("group") % 2
     sent_core = core ^ odd_group
-    zbits = list(range(2, seq_bits))
     toks, width = tokens.shape
     levels = level_weight.shape[0]
     heads = HEADS // CORES
@@ -264,8 +257,9 @@
     scale = jnp.stack([own_w, far_w]) * on[:, :, None, None]
     scale = jnp.transpose(scale, (0, 3, 2, 1)).reshape(2, toks, heads * levels)
 
-    kvp = gather_rows(*kv_split, zbits, (0,))
-    qop = gather_rows(*qo_split, zbits, (0, 1))
+    chips = lax.axis_size("seq") // CORES
+    kvp = gather_rows(*kv_split, chips, KV_ROUTES)
+    qop = gather_rows(*qo_split, chips, QO_ROUTES)
 
     act = sd((toks, cols), BF16)
     state = sd((heads, HEAD, HEAD), BF16)
@@ -328,6 +322,10 @@
     )
 
 
+KV_ROUTES = {(1, 1): 1, (3, 0): 2, (3, 1): 1, (5, 1): 1}
+QO_ROUTES = {(2, 1): 2, (3, 0): 2, (5, 1): 1}
+
+
 def solution(mesh):
     return jax.shard_map(
         on_device,

time: 139 us -> 135 us (0.971)
  waiting for transfers between devices: 70.2 us -> 59.2 us
  starting transfers between devices: 39.2 us -> 46.2 us
    ppermute x9, waiting for transfers between devices: 18.5 us -> 11.8 us  [swap_x(): lax.ppermute(value, 'group', [(i, i ^ 1) for i in range(lax.axis_size('gr...]
    ppermute x8, starting transfers between devices: 6.73 us -> 13.2 us  [swap_crossed(): return lax.ppermute(value, ('group', 'seq'), pairs)]
    ppermute x8, waiting for transfers between devices: 20 us -> 13.8 us  [swap_crossed(): return lax.ppermute(value, ('group', 'seq'), pairs)]
    ppermute x23, waiting for transfers between devices: 31.7 us -> 33.7 us  [swap(): lax.ppermute(value, 'seq', [(i, i ^ mask) for i in range(lax.axis_size('s...]
  transfers between devices with their start and end apart: 40 -> 40, of which waited for: 19 -> 16; matrix products, arithmetic and copies ran while one was open for 1% -> 1% of each run, Pallas kernels for 12% -> 12%
where the time goes in v5:
time: 135 us
  waiting for transfers between devices  59.2 us (44%)
  starting transfers between devices  46.2 us (34%)
  Pallas kernels  23.6 us (17%)
  local copies, waits for them, and re-layouts  4.93 us (4%)
    ppermute x23, waiting for transfers between devices, swap(): lax.ppermute(value, 'seq', [(i, i ^ mask) for i in range(lax.axis_size('s...  33.7 us
    ppermute x23, starting transfers between devices, swap(): lax.ppermute(value, 'seq', [(i, i ^ mask) for i in range(lax.axis_size('s...  20.3 us
    pallas_call x4, Pallas kernels, call(): pl.pallas_call(kernel, in_specs=[SMALL] + [FAST] * (len(operands) - 1), o...  18.4 us
    ppermute x8, waiting for transfers between devices, swap_crossed(): return lax.ppermute(value, ('group', 'seq'), pairs)  13.8 us
    ppermute x8, starting transfers between devices, swap_crossed(): return lax.ppermute(value, ('group', 'seq'), pairs)  13.2 us
    ppermute x9, starting transfers between devices, swap_x(): lax.ppermute(value, 'group', [(i, i ^ 1) for i in range(lax.axis_size('gr...  12.6 us
    ppermute x9, waiting for transfers between devices, swap_x(): lax.ppermute(value, 'group', [(i, i ^ 1) for i in range(lax.axis_size('gr...  11.8 us
    pallas_call x2, Pallas kernels, split(): pl.pallas_call(functools.partial(split_kernel, parts, cols), out_shape=[s...  4.53 us
  transfers between devices with their start and end apart: 40, of which 16 were waited for; matrix products, arithmetic and copies ran while one was open for 1% of the time, Pallas kernels for 12%

profile of v5, /device:TPU:0, one launch (start us, length us, event | category | flops | bytes accessed | tf_op | source)
XLA Modules:
  0.0 134.8 jit_solution(5238688075422502534)
XLA Ops:
  0.0 0.6 collective-permute-start.1
  0.6 2.3 %shard_map.127 = (bf16[256,512]{1,0:T(8,128)(2,1)}, bf16[256,512]{1,0:T(8,128)(2,1)}, bf16[256,512]{1,0:T(8,128)(2,1)}, bf16[256,512]{1,0:T(8,128)(2,1)}) custom-call(bf16[128,3072]{1,0:T(8,128)(2,1)} %refs_0_.3), custom_call_target="tpu_custom_call" | custom-call | flops 1048576 | bytes 2097152 | tf_op jit(solution)/shard_map/pallas_call | solution.py:235
  2.9 1.0 dynamic-slice_bitcast_fusion
  4.0 0.5 collective-permute-start
  4.5 2.6 %collective-permute-start.3 = (bf16[256,512]{1,0:T(8,128)(2,1)}, bf16[256,512]{1,0:T(8,128)(2,1)S(1)}, u32[]{:S(2)}, u32[]{:S(2)}) collective-permute-start(bf16[256,512]{1,0:T(8,128)(2,1)} %get-tuple-element.28), channel_id=1, source_target_pairs={{0,2},{1,3},{2,0},{3,1},{4,6},{5,7},{6,4},{7,5},{8,10},{9,11},{10,... | collective-permute-start | bytes 786440 | tf_op jit(solution)/shard_map/ppermute | solution.py:33
  7.1 1.8 %collective-permute-start.5 = (bf16[256,512]{1,0:T(8,128)(2,1)}, bf16[256,512]{1,0:T(8,128)(2,1)}, u32[]{:S(2)}, u32[]{:S(2)}) collective-permute-start(bf16[256,512]{1,0:T(8,128)(2,1)} %get-tuple-element.28), channel_id=1, source_target_pairs={{0,4},{1,5},{2,6},{3,7},{4,0},{5,1},{6,2},{7,3},{8,12},{9,13},{10,... | collective-permute-start | bytes 786440 | tf_op jit(solution)/shard_map/ppermute | solution.py:33
  8.8 2.6 %collective-permute-start.9 = (bf16[256,512]{1,0:T(8,128)(2,1)}, bf16[256,512]{1,0:T(8,128)(2,1)}, u32[]{:S(2)}, u32[]{:S(2)}) collective-permute-start(bf16[256,512]{1,0:T(8,128)(2,1)} %get-tuple-element.28), channel_id=1, source_target_pairs={{0,8},{1,9},{2,10},{3,11},{4,12},{5,13},{6,14},{7,15},{8,0},{9,1},... | collective-permute-start | bytes 786440 | tf_op jit(solution)/shard_map/ppermute | solution.py:33
  11.4 2.3 %shard_map.129 = (bf16[256,512]{1,0:T(8,128)(2,1)}, bf16[256,512]{1,0:T(8,128)(2,1)}, bf16[256,512]{1,0:T(8,128)(2,1)}, bf16[256,512]{1,0:T(8,128)(2,1)}) custom-call(bf16[128,3072]{1,0:T(8,128)(2,1)} %refs_0_.3, bf16[64,2048]{1,0:T(8,128)(2,1)} %refs_1_.1), custom_call_target="tpu_custom_call" | custom-call | flops 1048576 | bytes 2097152 | tf_op jit(solution)/shard_map/pallas_call | solution.py:235
  13.7 0.7 collective-permute-done.3.refs_2_
  14.4 2.0 %collective-permute-start.22 = (bf16[256,512]{1,0:T(8,128)(2,1)}, bf16[256,512]{1,0:T(8,128)(2,1)S(1)}, u32[]{:S(2)}, u32[]{:S(2)}) collective-permute-start(bf16[256,512]{1,0:T(8,128)(2,1)} %get-tuple-element.37), channel_id=1, source_target_pairs={{0,2},{1,3},{2,0},{3,1},{4,6},{5,7},{6,4},{7,5},{8,10},{9,11},{10,... | collective-permute-start | bytes 786440 | tf_op jit(solution)/shard_map/ppermute | solution.py:33
  16.4 3.2 %collective-permute-done.4.refs_3_ = bf16[256,512]{1,0:T(8,128)(2,1)S(1)} collective-permute-done((bf16[256,512]{1,0:T(8,128)(2,1)}, bf16[256,512]{1,0:T(8,128)(2,1)S(1)}, u32[]{:S(2)}, u32[]{:S(2)}) %collective-permute-start.4) | collective-permute-done | bytes 262176 | tf_op jit(solution)/shard_map/ppermute | solution.py:33
  19.7 0.7 copy-done.7
  20.4 2.6 %collective-permute-start.28 = (bf16[256,512]{1,0:T(8,128)(2,1)}, bf16[256,512]{1,0:T(8,128)(2,1)S(1)}, u32[]{:S(2)}, u32[]{:S(2)}) collective-permute-start(bf16[256,512]{1,0:T(8,128)(2,1)} %get-tuple-element.37), channel_id=1, source_target_pairs={{0,8},{1,9},{2,10},{3,11},{4,12},{5,13},{6,14},{7,15},{8,0},{9,1},... | collective-permute-start | bytes 786440 | tf_op jit(solution)/shard_map/ppermute | solution.py:33
  23.0 1.1 collective-permute-start.6
  24.1 1.6 %collective-permute-start.13 = (bf16[256,512]{1,0:T(8,128)(2,1)}, bf16[256,512]{1,0:T(8,128)(2,1)}, u32[]{:S(2)}, u32[]{:S(2)}) collective-permute-start(bf16[256,512]{1,0:T(8,128)(2,1)} %collective-permute-done.9.refs_8_), channel_id=1, source_target_pairs={{0,4},{1,5},{2,6},{3,7},{4,0},{5,1},{6,2},{7,3},{8,12},{9,13},{10,... | collective-permute-start | bytes 786440 | tf_op jit(solution)/shard_map/ppermute | solution.py:23
  25.6 1.0 collective-permute-start.10
  26.6 9.7 %collective-permute-done.28.refs_12_ = bf16[256,512]{1,0:T(8,128)(2,1)S(1)} collective-permute-done((bf16[256,512]{1,0:T(8,128)(2,1)}, bf16[256,512]{1,0:T(8,128)(2,1)S(1)}, u32[]{:S(2)}, u32[]{:S(2)}) %collective-permute-start.28) | collective-permute-done | bytes 262176 | tf_op jit(solution)/shard_map/ppermute | solution.py:33
  36.3 0.7 collective-permute-start.11
  37.1 1.2 collective-permute-start.7
  38.2 1.3 collective-permute-start.15
  39.7 5.7 %collective-permute-done.7.refs_6_ = bf16[256,512]{1,0:T(8,128)(2,1)} collective-permute-done((bf16[256,512]{1,0:T(8,128)(2,1)S(1)}, bf16[256,512]{1,0:T(8,128)(2,1)}, u32[]{:S(2)}, u32[]{:S(2)}) %collective-permute-start.7) | collective-permute-done | bytes 262176 | tf_op jit(solution)/shard_map/ppermute | solution.py:23
  45.4 2.1 %collective-permute-start.14 = (bf16[256,512]{1,0:T(8,128)(2,1)}, bf16[256,512]{1,0:T(8,128)(2,1)}, u32[]{:S(2)}, u32[]{:S(2)}) collective-permute-start(bf16[256,512]{1,0:T(8,128)(2,1)} %collective-permute-done.13.refs_12_), channel_id=1, source_target_pairs={{0,16},{16,0},{1,17},{17,1},{2,18},{18,2},{3,19},{19,3},{4,20},{20... | collective-permute-start | bytes 786440 | tf_op jit(solution)/shard_map/ppermute | solution.py:37
  47.5 0.5 collective-permute-start.8
  48.0 1.5 %collective-permute-start.12 = (bf16[256,512]{1,0:T(8,128)(2,1)}, bf16[256,512]{1,0:T(8,128)(2,1)}, u32[]{:S(2)}, u32[]{:S(2)}) collective-permute-start(bf16[256,512]{1,0:T(8,128)(2,1)} %collective-permute-done.10.refs_9_), channel_id=1, source_target_pairs={{0,2},{1,3},{2,0},{3,1},{4,6},{5,7},{6,4},{7,5},{8,10},{9,11},{10,... | collective-permute-start | bytes 786440 | tf_op jit(solution)/shard_map/ppermute | solution.py:23
  49.5 1.9 %collective-permute-done.15.refs_14_ = bf16[256,512]{1,0:T(8,128)(2,1)} collective-permute-done((bf16[256,512]{1,0:T(8,128)(2,1)}, bf16[256,512]{1,0:T(8,128)(2,1)}, u32[]{:S(2)}, u32[]{:S(2)}) %collective-permute-start.15) | collective-permute-done | bytes 262176 | tf_op jit(solution)/shard_map/ppermute | solution.py:23
  51.5 1.5 %collective-permute-start.16 = (bf16[256,512]{1,0:T(8,128)(2,1)}, bf16[256,512]{1,0:T(8,128)(2,1)}, u32[]{:S(2)}, u32[]{:S(2)}) collective-permute-start(bf16[256,512]{1,0:T(8,128)(2,1)} %collective-permute-done.15.refs_14_), channel_id=1, source_target_pairs={{0,16},{16,0},{1,17},{17,1},{2,18},{18,2},{3,19},{19,3},{4,20},{20... | collective-permute-start | bytes 786440 | tf_op jit(solution)/shard_map/ppermute | solution.py:37
  53.2 0.2 copy.18.scale
  53.4 3.6 %collective-permute-done.8.refs_7_ = bf16[256,512]{1,0:T(8,128)(2,1)} collective-permute-done((bf16[256,512]{1,0:T(8,128)(2,1)}, bf16[256,512]{1,0:T(8,128)(2,1)}, u32[]{:S(2)}, u32[]{:S(2)}) %collective-permute-start.8) | collective-permute-done | bytes 262176 | tf_op jit(solution)/shard_map/ppermute | solution.py:23
  57.1 0.8 collective-permute-start.24
  57.8 3.9 %collective-permute-done.12.refs_11_ = bf16[256,512]{1,0:T(8,128)(2,1)} collective-permute-done((bf16[256,512]{1,0:T(8,128)(2,1)}, bf16[256,512]{1,0:T(8,128)(2,1)}, u32[]{:S(2)}, u32[]{:S(2)}) %collective-permute-start.12) | collective-permute-done | bytes 262176 | tf_op jit(solution)/shard_map/ppermute | solution.py:23
  61.8 0.9 collective-permute-start.25
  62.7 1.2 collective-permute-start.26
  63.9 0.8 collective-permute-start.32
  64.8 0.9 copy-done.4
  65.7 0.9 copy-done.6
  66.7 0.9 copy-done.8
  67.6 7.6 %shard_map.128 = (bf16[512,512]{1,0:T(8,128)(2,1)S(1)}, bf16[512,512]{1,0:T(8,128)(2,1)S(1)}, bf16[512,512]{1,0:T(8,128)(2,1)S(1)}, bf16[512,512]{1,0:T(8,128)(2...) custom-call(s32[16]{0:T(128)S(1)} %get-tuple-element.47.starts, ...), custom_call_target="tpu_custom_call" | custom-call | flops 4294967296 | bytes 8388608 | tf_op jit(solution)/shard_map/pallas_call | solution.py:205
  75.3 1.2 collective-permute-start.17
  76.5 0.9 collective-permute-start.18
  77.4 1.0 collective-permute-start.23
  78.4 1.0 collective-permute-start.29
  79.4 2.4 %collective-permute-done.32.refs_16_ = bf16[256,512]{1,0:T(8,128)(2,1)S(1)} collective-permute-done((bf16[256,512]{1,0:T(8,128)(2,1)S(1)}, bf16[256,512]{1,0:T(8,128)(2,1)S(1)}, u32[]{:S(2)}, u32[]{:S(2)}) %collective-permute-start.32) | collective-permute-done | bytes 262176 | tf_op jit(solution)/shard_map/ppermute | solution.py:23
  81.8 1.0 collective-permute-start.30
  82.8 2.2 %collective-permute-start.27 = (bf16[256,512]{1,0:T(8,128)(2,1)S(1)}, bf16[256,512]{1,0:T(8,128)(2,1)S(1)}, u32[]{:S(2)}, u32[]{:S(2)}) collective-permute-start(bf16[256,512]{1,0:T(8,128)(2,1)S(1)} %collective-permute-done.26.refs_10_), channel_id=1, source_target_pairs={{0,16},{16,0},{1,17},{17,1},{2,18},{18,2},{3,19},{19,3},{4,20},{20... | collective-permute-start | bytes 786440 | tf_op jit(solution)/shard_map/ppermute | solution.py:37
  85.0 0.5 collective-permute-start.34
  85.6 0.9 collective-permute-done.23.refs_7_
  86.6 1.0 collective-permute-start.33
  87.6 4.6 %collective-permute-done.29.refs_13_ = bf16[256,512]{1,0:T(8,128)(2,1)S(1)} collective-permute-done((bf16[256,512]{1,0:T(8,128)(2,1)S(1)}, bf16[256,512]{1,0:T(8,128)(2,1)S(1)}, u32[]{:S(2)}, u32[]{:S(2)}) %collective-permute-start.29) | collective-permute-done | bytes 262176 | tf_op jit(solution)/shard_map/ppermute | solution.py:37
  92.2 1.2 collective-permute-start.31
  93.3 3.3 %collective-permute-done.34.refs_18_ = bf16[256,512]{1,0:T(8,128)(2,1)S(1)} collective-permute-done((bf16[256,512]{1,0:T(8,128)(2,1)S(1)}, bf16[256,512]{1,0:T(8,128)(2,1)S(1)}, u32[]{:S(2)}, u32[]{:S(2)}) %collective-permute-start.34) | collective-permute-done | bytes 262176 | tf_op jit(solution)/shard_map/ppermute | solution.py:23
  96.6 1.7 %collective-permute-start.35 = (bf16[256,512]{1,0:T(8,128)(2,1)S(1)}, bf16[256,512]{1,0:T(8,128)(2,1)S(1)}, u32[]{:S(2)}, u32[]{:S(2)}) collective-permute-start(bf16[256,512]{1,0:T(8,128)(2,1)S(1)} %collective-permute-done.34.refs_18_), channel_id=1, source_target_pairs={{0,16},{16,0},{1,17},{17,1},{2,18},{18,2},{3,19},{19,3},{4,20},{20... | collective-permute-start | bytes 786440 | tf_op jit(solution)/shard_map/ppermute | solution.py:37
  98.3 1.0 collective-permute-start.19
  99.3 1.0 collective-permute-start.20
  100.4 0.3 collective-permute-done.31.refs_15_
  100.7 2.7 %collective-permute-done.33.refs_17_ = bf16[256,512]{1,0:T(8,128)(2,1)S(1)} collective-permute-done((bf16[256,512]{1,0:T(8,128)(2,1)S(1)}, bf16[256,512]{1,0:T(8,128)(2,1)S(1)}, u32[]{:S(2)}, u32[]{:S(2)}) %collective-permute-start.33) | collective-permute-done | bytes 262176 | tf_op jit(solution)/shard_map/ppermute | solution.py:37
  103.4 3.5 %collective-permute-done.35.refs_19_ = bf16[256,512]{1,0:T(8,128)(2,1)S(1)} collective-permute-done((bf16[256,512]{1,0:T(8,128)(2,1)S(1)}, bf16[256,512]{1,0:T(8,128)(2,1)S(1)}, u32[]{:S(2)}, u32[]{:S(2)}) %collective-permute-start.35) | collective-permute-done | bytes 262176 | tf_op jit(solution)/shard_map/ppermute | solution.py:37
  106.9 4.3 %shard_map.132 = (f32[512,512]{1,0:T(8,128)S(1)}, bf16[512,512]{1,0:T(8,128)(2,1)S(1)}, bf16[1024,1024]{1,0:T(8,128)(2,1)S(1)}) custom-call(s32[32]{0:T(128)S(1)} %pad_add_fusion.1.starts, bf16[512,2048]{1,0:T(8,128)(2,1)} %collective-permute-done.1.xb.x, bf16[512,512]{1,0:T(8,128)(2,1)S(1)} %get-tuple-element.41.k, ...), custom_call_target="tpu_custom_call" | custom-call | flops 1073741824 | bytes 8388608 | tf_op jit(solution)/shard_map/pallas_call | solution.py:205
  111.4 3.3 %collective-permute-start.36 = (bf16[256,256]{1,0:T(8,128)(2,1)S(1)}, bf16[256,256]{1,0:T(8,128)(2,1)S(1)}, u32[]{:S(2)}, u32[]{:S(2)}) collective-permute-start(bf16[256,256]{1,0:T(8,128)(2,1)S(1)} %add_convert_fusion.1), channel_id=1, source_target_pairs={{0,8},{1,9},{2,10},{3,11},{4,12},{5,13},{6,14},{7,15},{8,0},{9,1},... | collective-permute-start | bytes 393224 | tf_op jit(solution)/shard_map/ppermute | solution.py:23
  114.9 9.6 %collective-permute-done.36.refs_0_ = bf16[256,256]{1,0:T(8,128)(2,1)S(1)} collective-permute-done((bf16[256,256]{1,0:T(8,128)(2,1)S(1)}, bf16[256,256]{1,0:T(8,128)(2,1)S(1)}, u32[]{:S(2)}, u32[]{:S(2)}) %collective-permute-start.36) | collective-permute-done | bytes 131104 | tf_op jit(solution)/shard_map/ppermute | solution.py:23
  124.5 2.8 %collective-permute-done.37.refs_1_ = bf16[256,256]{1,0:T(8,128)(2,1)S(1)} collective-permute-done((bf16[256,256]{1,0:T(8,128)(2,1)S(1)}, bf16[256,256]{1,0:T(8,128)(2,1)S(1)}, u32[]{:S(2)}, u32[]{:S(2)}) %collective-permute-start.37) | collective-permute-done | bytes 131104 | tf_op jit(solution)/shard_map/ppermute | solution.py:23
  127.3 0.3 shard_map.133
  127.8 3.3 %shard_map.130 = (f32[512,512]{1,0:T(8,128)S(1)}, bf16[512,512]{1,0:T(8,128)(2,1)S(1)}) custom-call(s32[32]{0:T(128)S(1)} %pad_add_fusion.1.starts, bf16[512,2048]{1,0:T(8,128)(2,1)S(1)} %copy-done, bf16[512,512]{1,0:T(8,128)(2,1)S(1)} %get-tuple-element.30.k, bf16[512,512]{1,0:T(8,128)(2,1)S(1)} %get-tuple-element.31.v, ...), custom_call_target="tpu_custom_call" | custom-call | flops 1073741824 | bytes 8388608 | tf_op jit(solution)/shard_map/pallas_call | solution.py:205
  131.1 0.3 shard_map.131.mine
  131.4 3.2 %shard_map.134 = bf16[512,2048]{1,0:T(8,128)(2,1)} custom-call(s32[1]{0:T(128)} %bitcast.core_ref, bf16[512,512]{1,0:T(8,128)(2,1)S(1)} %shard_map.131.mine, bf16[512,512]{1,0:T(8,128)(2,1)S(1)} %collective-permute-done.38.theirs, bf16[1024,1024]{1,0:T(8,128)(2,1)S(1)} %get-tuple-element.46.w_mine, bf16[1024,1024]{1,0:T(8,128)(2,1)S(1)} %collective-permute-done.39.w_theirs), custom_call_target="tpu_custom_call" | custom-call | flops 2147483648 | bytes 8388608 | tf_op jit(solution)/shard_map/pallas_call | solution.py:205
  (67 shorter events, 1.0 us)
Async XLA Ops:
  0.0 39.6 %copy-start.9 = (pred[14]{0:T(512)(128)(4,1)S(1)}, pred[14]{0:T(512)(128)(4,1)}, u32[]{:S(2)}) copy-start(pred[14]{0:T(512)(128)(4,1)} %constant.69.clone) | copy-start | bytes 46
  0.0 39.6 %copy-start.10 = (f32[14]{0:T(128)S(1)}, f32[14]{0:T(128)}, u32[]{:S(2)}) copy-start(f32[14]{0:T(128)} %constant.70.clone) | copy-start | bytes 172
  0.0 39.6 %copy-start.11 = (s32[14]{0:T(128)S(1)}, s32[14]{0:T(128)}, u32[]{:S(2)}) copy-start(s32[14]{0:T(128)} %constant.68.clone) | copy-start | bytes 172
  0.0 53.0 %copy-start.12 = (s32[16]{0:T(128)S(1)}, s32[16]{0:T(128)}, u32[]{:S(2)}) copy-start(s32[16]{0:T(128)} %constant.74) | copy-start | bytes 196
  0.0 53.0 %copy-start.13 = (pred[16]{0:T(512)(128)(4,1)S(1)}, pred[16]{0:T(512)(128)(4,1)}, u32[]{:S(2)}) copy-start(pred[16]{0:T(512)(128)(4,1)} %constant.73) | copy-start | bytes 52
  0.0 53.0 %copy-start.14 = (s32[16]{0:T(128)S(1)}, s32[16]{0:T(128)}, u32[]{:S(2)}) copy-start(s32[16]{0:T(128)} %constant.71.clone) | copy-start | bytes 196
  0.0 64.7 %copy-start = (bf16[512,2048]{1,0:T(8,128)(2,1)S(1)}, bf16[512,2048]{1,0:T(8,128)(2,1)}, u32[]{:S(2)}) copy-start(bf16[512,2048]{1,0:T(8,128)(2,1)} %x.1) | copy-start | bytes 6291460
  0.0 63.9 %collective-permute-start.1 = (bf16[512,2048]{1,0:T(8,128)(2,1)}, bf16[512,2048]{1,0:T(8,128)(2,1)}, u32[]{:S(2)}, u32[]{:S(2)}) collective-permute-start(bf16[512,2048]{1,0:T(8,128)(2,1)} %x.1), channel_id=1, source_target_pairs={{0,1},{1,0},{2,3},{3,2},{4,5},{5,4},{6,7},{7,6},{8,9},{9,8},{10,11... | collective-permute-start | bytes 6291464 | tf_op jit(solution)/shard_map/ppermute | solution.py:23
  2.9 61.9 %copy-start.2 = (bf16[256,512]{1,0:T(8,128)(2,1)S(1)}, bf16[256,512]{1,0:T(8,128)(2,1)}, u32[]{:S(2)}) copy-start(bf16[256,512]{1,0:T(8,128)(2,1)} %get-tuple-element.26.refs_0_) | copy-start | bytes 786436
  2.9 5.9 %collective-permute-start.2 = (bf16[256,512]{1,0:T(8,128)(2,1)}, bf16[256,512]{1,0:T(8,128)(2,1)S(1)}, u32[]{:S(2)}, u32[]{:S(2)}) collective-permute-start(bf16[256,512]{1,0:T(8,128)(2,1)} %get-tuple-element.27), channel_id=1, source_target_pairs={{0,1},{1,0},{2,3},{3,2},{4,5},{5,4},{6,7},{7,6},{8,9},{9,8},{10,11... | collective-permute-start | bytes 786440 | tf_op jit(solution)/shard_map/ppermute | solution.py:23
  4.0 3.1 %collective-permute-start = (f32[14,2,512]{2,1,0:T(2,128)S(1)}, f32[14,2,512]{2,1,0:T(2,128)S(1)}, u32[]{:S(2)}, u32[]{:S(2)}) collective-permute-start(f32[14,2,512]{2,1,0:T(2,128)S(1)} %get-tuple-element.50), channel_id=1, source_target_pairs={{0,1},{1,0},{2,3},{3,2},{4,5},{5,4},{6,7},{7,6},{8,9},{9,8},{10,11... | collective-permute-start | bytes 172040 | tf_op jit(solution)/shard_map/ppermute | solution.py:23
  4.5 9.9 %collective-permute-start.3 = (bf16[256,512]{1,0:T(8,128)(2,1)}, bf16[256,512]{1,0:T(8,128)(2,1)S(1)}, u32[]{:S(2)}, u32[]{:S(2)}) collective-permute-start(bf16[256,512]{1,0:T(8,128)(2,1)} %get-tuple-element.28), channel_id=1, source_target_pairs={{0,2},{1,3},{2,0},{3,1},{4,6},{5,7},{6,4},{7,5},{8,10},{9,11},{10,... | collective-permute-start | bytes 786440 | tf_op jit(solution)/shard_map/ppermute | solution.py:33
  7.0 12.6 %collective-permute-start.4 = (bf16[256,512]{1,0:T(8,128)(2,1)}, bf16[256,512]{1,0:T(8,128)(2,1)S(1)}, u32[]{:S(2)}, u32[]{:S(2)}) collective-permute-start(bf16[256,512]{1,0:T(8,128)(2,1)} %get-tuple-element.29), channel_id=1, source_target_pairs={{0,3},{1,2},{2,1},{3,0},{4,7},{5,6},{6,5},{7,4},{8,11},{9,10},{10,... | collective-permute-start | bytes 786440 | tf_op jit(solution)/shard_map/ppermute | solution.py:33
  7.1 15.9 %collective-permute-start.5 = (bf16[256,512]{1,0:T(8,128)(2,1)}, bf16[256,512]{1,0:T(8,128)(2,1)}, u32[]{:S(2)}, u32[]{:S(2)}) collective-permute-start(bf16[256,512]{1,0:T(8,128)(2,1)} %get-tuple-element.28), channel_id=1, source_target_pairs={{0,4},{1,5},{2,6},{3,7},{4,0},{5,1},{6,2},{7,3},{8,12},{9,13},{10,... | collective-permute-start | bytes 786440 | tf_op jit(solution)/shard_map/ppermute | solution.py:33
  8.8 44.4 %copy-start.3 = (bf16[256,512]{1,0:T(8,128)(2,1)}, bf16[256,512]{1,0:T(8,128)(2,1)S(1)}, u32[]{:S(2)}) copy-start(bf16[256,512]{1,0:T(8,128)(2,1)S(1)} %collective-permute-done.2.refs_1_) | copy-start | bytes 786436
  8.8 15.3 %collective-permute-start.9 = (bf16[256,512]{1,0:T(8,128)(2,1)}, bf16[256,512]{1,0:T(8,128)(2,1)}, u32[]{:S(2)}, u32[]{:S(2)}) collective-permute-start(bf16[256,512]{1,0:T(8,128)(2,1)} %get-tuple-element.28), channel_id=1, source_target_pairs={{0,8},{1,9},{2,10},{3,11},{4,12},{5,13},{6,14},{7,15},{8,0},{9,1},... | collective-permute-start | bytes 786440 | tf_op jit(solution)/shard_map/ppermute | solution.py:33
  14.4 38.8 %copy-start.5 = (bf16[256,512]{1,0:T(8,128)(2,1)}, bf16[256,512]{1,0:T(8,128)(2,1)S(1)}, u32[]{:S(2)}) copy-start(bf16[256,512]{1,0:T(8,128)(2,1)S(1)} %collective-permute-done.3.refs_2_) | copy-start | bytes 786436
  14.4 11.2 %collective-permute-start.22 = (bf16[256,512]{1,0:T(8,128)(2,1)}, bf16[256,512]{1,0:T(8,128)(2,1)S(1)}, u32[]{:S(2)}, u32[]{:S(2)}) collective-permute-start(bf16[256,512]{1,0:T(8,128)(2,1)} %get-tuple-element.37), channel_id=1, source_target_pairs={{0,2},{1,3},{2,0},{3,1},{4,6},{5,7},{6,4},{7,5},{8,10},{9,11},{10,... | collective-permute-start | bytes 786440 | tf_op jit(solution)/shard_map/ppermute | solution.py:33
  19.7 0.7 copy-start.7
  20.4 16.0 %collective-permute-start.28 = (bf16[256,512]{1,0:T(8,128)(2,1)}, bf16[256,512]{1,0:T(8,128)(2,1)S(1)}, u32[]{:S(2)}, u32[]{:S(2)}) collective-permute-start(bf16[256,512]{1,0:T(8,128)(2,1)} %get-tuple-element.37), channel_id=1, source_target_pairs={{0,8},{1,9},{2,10},{3,11},{4,12},{5,13},{6,14},{7,15},{8,0},{9,1},... | collective-permute-start | bytes 786440 | tf_op jit(solution)/shard_map/ppermute | solution.py:33
  23.0 14.1 %collective-permute-start.6 = (bf16[256,512]{1,0:T(8,128)(2,1)}, bf16[256,512]{1,0:T(8,128)(2,1)}, u32[]{:S(2)}, u32[]{:S(2)}) collective-permute-start(bf16[256,512]{1,0:T(8,128)(2,1)} %collective-permute-done.5.refs_4_), channel_id=1, source_target_pairs={{0,16},{16,0},{1,17},{17,1},{2,18},{18,2},{3,19},{19,3},{4,20},{20... | collective-permute-start | bytes 786440 | tf_op jit(solution)/shard_map/ppermute | solution.py:37
  24.1 14.1 %collective-permute-start.13 = (bf16[256,512]{1,0:T(8,128)(2,1)}, bf16[256,512]{1,0:T(8,128)(2,1)}, u32[]{:S(2)}, u32[]{:S(2)}) collective-permute-start(bf16[256,512]{1,0:T(8,128)(2,1)} %collective-permute-done.9.refs_8_), channel_id=1, source_target_pairs={{0,4},{1,5},{2,6},{3,7},{4,0},{5,1},{6,2},{7,3},{8,12},{9,13},{10,... | collective-permute-start | bytes 786440 | tf_op jit(solution)/shard_map/ppermute | solution.py:23
  25.6 21.9 %collective-permute-start.10 = (bf16[256,512]{1,0:T(8,128)(2,1)}, bf16[256,512]{1,0:T(8,128)(2,1)}, u32[]{:S(2)}, u32[]{:S(2)}) collective-permute-start(bf16[256,512]{1,0:T(8,128)(2,1)} %collective-permute-done.9.refs_8_), channel_id=1, source_target_pairs={{0,16},{16,0},{1,17},{17,1},{2,18},{18,2},{3,19},{19,3},{4,20},{20... | collective-permute-start | bytes 786440 | tf_op jit(solution)/shard_map/ppermute | solution.py:37
  36.3 11.7 %collective-permute-start.11 = (bf16[256,512]{1,0:T(8,128)(2,1)}, bf16[256,512]{1,0:T(8,128)(2,1)}, u32[]{:S(2)}, u32[]{:S(2)}) collective-permute-start(bf16[256,512]{1,0:T(8,128)(2,1)} %collective-permute-done.9.refs_8_), channel_id=1, source_target_pairs={{0,2},{1,3},{2,0},{3,1},{4,6},{5,7},{6,4},{7,5},{8,10},{9,11},{10,... | collective-permute-start | bytes 786440 | tf_op jit(solution)/shard_map/ppermute | solution.py:23
  37.1 8.3 %collective-permute-start.7 = (bf16[256,512]{1,0:T(8,128)(2,1)S(1)}, bf16[256,512]{1,0:T(8,128)(2,1)}, u32[]{:S(2)}, u32[]{:S(2)}) collective-permute-start(bf16[256,512]{1,0:T(8,128)(2,1)S(1)} %collective-permute-done.3.refs_2_), channel_id=1, source_target_pairs={{0,4},{1,5},{2,6},{3,7},{4,0},{5,1},{6,2},{7,3},{8,12},{9,13},{10,... | collective-permute-start | bytes 786440 | tf_op jit(solution)/shard_map/ppermute | solution.py:23
  38.2 13.2 %collective-permute-start.15 = (bf16[256,512]{1,0:T(8,128)(2,1)}, bf16[256,512]{1,0:T(8,128)(2,1)}, u32[]{:S(2)}, u32[]{:S(2)}) collective-permute-start(bf16[256,512]{1,0:T(8,128)(2,1)} %collective-permute-done.13.refs_12_), channel_id=1, source_target_pairs={{0,2},{1,3},{2,0},{3,1},{4,6},{5,7},{6,4},{7,5},{8,10},{9,11},{10,... | collective-permute-start | bytes 786440 | tf_op jit(solution)/shard_map/ppermute | solution.py:23
  45.4 16.4 %collective-permute-start.14 = (bf16[256,512]{1,0:T(8,128)(2,1)}, bf16[256,512]{1,0:T(8,128)(2,1)}, u32[]{:S(2)}, u32[]{:S(2)}) collective-permute-start(bf16[256,512]{1,0:T(8,128)(2,1)} %collective-permute-done.13.refs_12_), channel_id=1, source_target_pairs={{0,16},{16,0},{1,17},{17,1},{2,18},{18,2},{3,19},{19,3},{4,20},{20... | collective-permute-start | bytes 786440 | tf_op jit(solution)/shard_map/ppermute | solution.py:37
  47.5 9.6 %collective-permute-start.8 = (bf16[256,512]{1,0:T(8,128)(2,1)}, bf16[256,512]{1,0:T(8,128)(2,1)}, u32[]{:S(2)}, u32[]{:S(2)}) collective-permute-start(bf16[256,512]{1,0:T(8,128)(2,1)} %collective-permute-done.6.refs_5_), channel_id=1, source_target_pairs={{0,2},{1,3},{2,0},{3,1},{4,6},{5,7},{6,4},{7,5},{8,10},{9,11},{10,... | collective-permute-start | bytes 786440 | tf_op jit(solution)/shard_map/ppermute | solution.py:23
  48.0 13.8 %collective-permute-start.12 = (bf16[256,512]{1,0:T(8,128)(2,1)}, bf16[256,512]{1,0:T(8,128)(2,1)}, u32[]{:S(2)}, u32[]{:S(2)}) collective-permute-start(bf16[256,512]{1,0:T(8,128)(2,1)} %collective-permute-done.10.refs_9_), channel_id=1, source_target_pairs={{0,2},{1,3},{2,0},{3,1},{4,6},{5,7},{6,4},{7,5},{8,10},{9,11},{10,... | collective-permute-start | bytes 786440 | tf_op jit(solution)/shard_map/ppermute | solution.py:23
  51.5 11.3 %collective-permute-start.16 = (bf16[256,512]{1,0:T(8,128)(2,1)}, bf16[256,512]{1,0:T(8,128)(2,1)}, u32[]{:S(2)}, u32[]{:S(2)}) collective-permute-start(bf16[256,512]{1,0:T(8,128)(2,1)} %collective-permute-done.15.refs_14_), channel_id=1, source_target_pairs={{0,16},{16,0},{1,17},{17,1},{2,18},{18,2},{3,19},{19,3},{4,20},{20... | collective-permute-start | bytes 786440 | tf_op jit(solution)/shard_map/ppermute | solution.py:37
  57.1 19.5 %collective-permute-start.24 = (bf16[256,512]{1,0:T(8,128)(2,1)}, bf16[256,512]{1,0:T(8,128)(2,1)S(1)}, u32[]{:S(2)}, u32[]{:S(2)}) collective-permute-start(bf16[256,512]{1,0:T(8,128)(2,1)} %get-tuple-element.37), channel_id=1, source_target_pairs={{0,4},{1,5},{2,6},{3,7},{4,0},{5,1},{6,2},{7,3},{8,12},{9,13},{10,... | collective-permute-start | bytes 786440 | tf_op jit(solution)/shard_map/ppermute | solution.py:33
  61.8 13.5 %collective-permute-start.21 = (bf16[256,512]{1,0:T(8,128)(2,1)}, bf16[256,512]{1,0:T(8,128)(2,1)S(1)}, u32[]{:S(2)}, u32[]{:S(2)}) collective-permute-start(bf16[256,512]{1,0:T(8,128)(2,1)} %get-tuple-element.36), channel_id=1, source_target_pairs={{0,1},{1,0},{2,3},{3,2},{4,5},{5,4},{6,7},{7,6},{8,9},{9,8},{10,11... | collective-permute-start | bytes 786440 | tf_op jit(solution)/shard_map/ppermute | solution.py:23
  61.8 15.6 %collective-permute-start.25 = (bf16[256,512]{1,0:T(8,128)(2,1)}, bf16[256,512]{1,0:T(8,128)(2,1)S(1)}, u32[]{:S(2)}, u32[]{:S(2)}) collective-permute-start(bf16[256,512]{1,0:T(8,128)(2,1)} %get-tuple-element.38), channel_id=1, source_target_pairs={{0,5},{1,4},{2,7},{3,6},{4,1},{5,0},{6,3},{7,2},{8,13},{9,12},{10,... | collective-permute-start | bytes 786440 | tf_op jit(solution)/shard_map/ppermute | solution.py:33
  62.7 15.6 %collective-permute-start.26 = (bf16[256,512]{1,0:T(8,128)(2,1)S(1)}, bf16[256,512]{1,0:T(8,128)(2,1)S(1)}, u32[]{:S(2)}, u32[]{:S(2)}) collective-permute-start(bf16[256,512]{1,0:T(8,128)(2,1)S(1)} %collective-permute-done.22.refs_6_), channel_id=1, source_target_pairs={{0,4},{1,5},{2,6},{3,7},{4,0},{5,1},{6,2},{7,3},{8,12},{9,13},{10,... | collective-permute-start | bytes 786440 | tf_op jit(solution)/shard_map/ppermute | solution.py:23
  63.9 17.9 %collective-permute-start.32 = (bf16[256,512]{1,0:T(8,128)(2,1)S(1)}, bf16[256,512]{1,0:T(8,128)(2,1)S(1)}, u32[]{:S(2)}, u32[]{:S(2)}) collective-permute-start(bf16[256,512]{1,0:T(8,128)(2,1)S(1)} %collective-permute-done.28.refs_12_), channel_id=1, source_target_pairs={{0,4},{1,5},{2,6},{3,7},{4,0},{5,1},{6,2},{7,3},{8,12},{9,13},{10,... | collective-permute-start | bytes 786440 | tf_op jit(solution)/shard_map/ppermute | solution.py:23
  64.8 1.0 copy-start.4
  65.7 0.9 copy-start.6
  66.7 0.9 copy-start.8
  67.6 39.3 %copy-start.1 = (bf16[256,512]{1,0:T(8,128)(2,1)S(1)}, bf16[256,512]{1,0:T(8,128)(2,1)}, u32[]{:S(2)}) copy-start(bf16[256,512]{1,0:T(8,128)(2,1)} %get-tuple-element.35.refs_4_) | copy-start | bytes 786436
  75.3 7.5 %collective-permute-start.17 = (bf16[256,256]{1,0:T(8,128)(2,1)S(1)}, bf16[256,256]{1,0:T(8,128)(2,1)S(1)}, u32[]{:S(2)}, u32[]{:S(2)}) collective-permute-start(bf16[256,256]{1,0:T(8,128)(2,1)S(1)} %get-tuple-element.33), channel_id=1, source_target_pairs={{0,2},{1,3},{2,0},{3,1},{4,6},{5,7},{6,4},{7,5},{8,10},{9,11},{10,... | collective-permute-start | bytes 393224 | tf_op jit(solution)/shard_map/ppermute | solution.py:23
  76.5 8.5 %collective-permute-start.18 = (bf16[256,256]{1,0:T(8,128)(2,1)S(1)}, bf16[256,256]{1,0:T(8,128)(2,1)S(1)}, u32[]{:S(2)}, u32[]{:S(2)}) collective-permute-start(bf16[256,256]{1,0:T(8,128)(2,1)S(1)} %get-tuple-element.34), channel_id=1, source_target_pairs={{0,2},{1,3},{2,0},{3,1},{4,6},{5,7},{6,4},{7,5},{8,10},{9,11},{10,... | collective-permute-start | bytes 393224 | tf_op jit(solution)/shard_map/ppermute | solution.py:23
  77.4 9.2 %collective-permute-start.23 = (bf16[256,512]{1,0:T(8,128)(2,1)S(1)}, bf16[256,512]{1,0:T(8,128)(2,1)S(1)}, u32[]{:S(2)}, u32[]{:S(2)}) collective-permute-start(bf16[256,512]{1,0:T(8,128)(2,1)S(1)} %collective-permute-done.22.refs_6_), channel_id=1, source_target_pairs={{0,16},{16,0},{1,17},{17,1},{2,18},{18,2},{3,19},{19,3},{4,20},{20... | collective-permute-start | bytes 786440 | tf_op jit(solution)/shard_map/ppermute | solution.py:37
  78.4 13.8 %collective-permute-start.29 = (bf16[256,512]{1,0:T(8,128)(2,1)S(1)}, bf16[256,512]{1,0:T(8,128)(2,1)S(1)}, u32[]{:S(2)}, u32[]{:S(2)}) collective-permute-start(bf16[256,512]{1,0:T(8,128)(2,1)S(1)} %collective-permute-done.28.refs_12_), channel_id=1, source_target_pairs={{0,16},{16,0},{1,17},{17,1},{2,18},{18,2},{3,19},{19,3},{4,20},{20... | collective-permute-start | bytes 786440 | tf_op jit(solution)/shard_map/ppermute | solution.py:37
  81.8 16.5 %collective-permute-start.30 = (bf16[256,512]{1,0:T(8,128)(2,1)S(1)}, bf16[256,512]{1,0:T(8,128)(2,1)S(1)}, u32[]{:S(2)}, u32[]{:S(2)}) collective-permute-start(bf16[256,512]{1,0:T(8,128)(2,1)S(1)} %collective-permute-done.28.refs_12_), channel_id=1, source_target_pairs={{0,2},{1,3},{2,0},{3,1},{4,6},{5,7},{6,4},{7,5},{8,10},{9,11},{10,... | collective-permute-start | bytes 786440 | tf_op jit(solution)/shard_map/ppermute | solution.py:23
  82.8 16.5 %collective-permute-start.27 = (bf16[256,512]{1,0:T(8,128)(2,1)S(1)}, bf16[256,512]{1,0:T(8,128)(2,1)S(1)}, u32[]{:S(2)}, u32[]{:S(2)}) collective-permute-start(bf16[256,512]{1,0:T(8,128)(2,1)S(1)} %collective-permute-done.26.refs_10_), channel_id=1, source_target_pairs={{0,16},{16,0},{1,17},{17,1},{2,18},{18,2},{3,19},{19,3},{4,20},{20... | collective-permute-start | bytes 786440 | tf_op jit(solution)/shard_map/ppermute | solution.py:37
  85.0 11.6 %collective-permute-start.34 = (bf16[256,512]{1,0:T(8,128)(2,1)S(1)}, bf16[256,512]{1,0:T(8,128)(2,1)S(1)}, u32[]{:S(2)}, u32[]{:S(2)}) collective-permute-start(bf16[256,512]{1,0:T(8,128)(2,1)S(1)} %collective-permute-done.32.refs_16_), channel_id=1, source_target_pairs={{0,2},{1,3},{2,0},{3,1},{4,6},{5,7},{6,4},{7,5},{8,10},{9,11},{10,... | collective-permute-start | bytes 786440 | tf_op jit(solution)/shard_map/ppermute | solution.py:23
  86.6 16.9 %collective-permute-start.33 = (bf16[256,512]{1,0:T(8,128)(2,1)S(1)}, bf16[256,512]{1,0:T(8,128)(2,1)S(1)}, u32[]{:S(2)}, u32[]{:S(2)}) collective-permute-start(bf16[256,512]{1,0:T(8,128)(2,1)S(1)} %collective-permute-done.32.refs_16_), channel_id=1, source_target_pairs={{0,16},{16,0},{1,17},{17,1},{2,18},{18,2},{3,19},{19,3},{4,20},{20... | collective-permute-start | bytes 786440 | tf_op jit(solution)/shard_map/ppermute | solution.py:37
  92.2 8.5 %collective-permute-start.31 = (bf16[256,512]{1,0:T(8,128)(2,1)S(1)}, bf16[256,512]{1,0:T(8,128)(2,1)S(1)}, u32[]{:S(2)}, u32[]{:S(2)}) collective-permute-start(bf16[256,512]{1,0:T(8,128)(2,1)S(1)} %collective-permute-done.29.refs_13_), channel_id=1, source_target_pairs={{0,2},{1,3},{2,0},{3,1},{4,6},{5,7},{6,4},{7,5},{8,10},{9,11},{10,... | collective-permute-start | bytes 786440 | tf_op jit(solution)/shard_map/ppermute | solution.py:23
  96.6 10.3 %collective-permute-start.35 = (bf16[256,512]{1,0:T(8,128)(2,1)S(1)}, bf16[256,512]{1,0:T(8,128)(2,1)S(1)}, u32[]{:S(2)}, u32[]{:S(2)}) collective-permute-start(bf16[256,512]{1,0:T(8,128)(2,1)S(1)} %collective-permute-done.34.refs_18_), channel_id=1, source_target_pairs={{0,16},{16,0},{1,17},{17,1},{2,18},{18,2},{3,19},{19,3},{4,20},{20... | collective-permute-start | bytes 786440 | tf_op jit(solution)/shard_map/ppermute | solution.py:37
  98.3 8.6 %collective-permute-start.19 = (bf16[256,256]{1,0:T(8,128)(2,1)S(1)}, bf16[256,256]{1,0:T(8,128)(2,1)S(1)}, u32[]{:S(2)}, u32[]{:S(2)}) collective-permute-start(bf16[256,256]{1,0:T(8,128)(2,1)S(1)} %add_convert_fusion.3), channel_id=1, source_target_pairs={{0,4},{1,5},{2,6},{3,7},{4,0},{5,1},{6,2},{7,3},{8,12},{9,13},{10,... | collective-permute-start | bytes 393224 | tf_op jit(solution)/shard_map/ppermute | solution.py:23
  99.3 7.6 %collective-permute-start.20 = (bf16[256,256]{1,0:T(8,128)(2,1)S(1)}, bf16[256,256]{1,0:T(8,128)(2,1)S(1)}, u32[]{:S(2)}, u32[]{:S(2)}) collective-permute-start(bf16[256,256]{1,0:T(8,128)(2,1)S(1)} %add_convert_fusion.2), channel_id=1, source_target_pairs={{0,4},{1,5},{2,6},{3,7},{4,0},{5,1},{6,2},{7,3},{8,12},{9,13},{10,... | collective-permute-start | bytes 393224 | tf_op jit(solution)/shard_map/ppermute | solution.py:23
  111.3 20.1 %collective-permute-start.39 = (bf16[1024,1024]{1,0:T(8,128)(2,1)S(1)}, bf16[1024,1024]{1,0:T(8,128)(2,1)S(1)}, u32[]{:S(2)}, u32[]{:S(2)}) collective-permute-start(bf16[1024,1024]{1,0:T(8,128)(2,1)S(1)} %get-tuple-element.46.w_mine), channel_id=1, source_target_pairs={{0,1},{1,0},{2,3},{3,2},{4,5},{5,4},{6,7},{7,6},{8,9},{9,8},{10,11... | collective-permute-start | bytes 6291464 | tf_op jit(solution)/shard_map/ppermute | solution.py:23
  111.4 13.1 %collective-permute-start.36 = (bf16[256,256]{1,0:T(8,128)(2,1)S(1)}, bf16[256,256]{1,0:T(8,128)(2,1)S(1)}, u32[]{:S(2)}, u32[]{:S(2)}) collective-permute-start(bf16[256,256]{1,0:T(8,128)(2,1)S(1)} %add_convert_fusion.1), channel_id=1, source_target_pairs={{0,8},{1,9},{2,10},{3,11},{4,12},{5,13},{6,14},{7,15},{8,0},{9,1},... | collective-permute-start | bytes 393224 | tf_op jit(solution)/shard_map/ppermute | solution.py:23
  114.8 12.5 %collective-permute-start.37 = (bf16[256,256]{1,0:T(8,128)(2,1)S(1)}, bf16[256,256]{1,0:T(8,128)(2,1)S(1)}, u32[]{:S(2)}, u32[]{:S(2)}) collective-permute-start(bf16[256,256]{1,0:T(8,128)(2,1)S(1)} %add_convert_fusion), channel_id=1, source_target_pairs={{0,8},{1,9},{2,10},{3,11},{4,12},{5,13},{6,14},{7,15},{8,0},{9,1},... | collective-permute-start | bytes 393224 | tf_op jit(solution)/shard_map/ppermute | solution.py:23
  127.6 3.8 %collective-permute-start.38 = (bf16[512,512]{1,0:T(8,128)(2,1)S(1)}, bf16[512,512]{1,0:T(8,128)(2,1)S(1)}, u32[]{:S(2)}, u32[]{:S(2)}) collective-permute-start(bf16[512,512]{1,0:T(8,128)(2,1)S(1)} %shard_map.133), channel_id=1, source_target_pairs={{0,1},{1,0},{2,3},{3,2},{4,5},{5,4},{6,7},{7,6},{8,9},{9,8},{10,11... | collective-permute-start | bytes 1572872 | tf_op jit(solution)/shard_map/ppermute | solution.py:23
